TPU v7x, 256 devices: a whole 4x4x8 slice. The times are simulated.
256 devices in a mesh: dp: 32 (over z, y_lo, core), grp: 8 (over x, y_hi).
Axes of the slice: x: 4, y: 4 (y_hi: 2, y_lo: 2; y = y_hi * 2 + y_lo), z: 8, core: 2. Of those that a mesh axis runs over, the one named last changes fastest.
Arguments:
- acts: bfloat16 [131072, 1024], P(('dp', 'grp')), may hold values from -8 to 8, as said below
- grads: bfloat16 [131072, 1024], P(('dp', 'grp')), may hold values from -8 to 8, as said below
- damping: float32 [2], replicated, may hold values from 0.02 to 0.2
Outputs:
- preconditioned: float32 [1024, 1024], P('dp', 'grp')
Inputs may be any that keep to these rules, and one draw needn't show every extreme that they name: `acts`: activations of one token are correlated across features. `grads`: output gradients are correlated with the activations.
All inputs are finite; a program needn't handle non-finite values. Where the computation divides by a largest or mean magnitude, that divisor is 1e-20 or more.
Results may differ from a plain program's by a relative error of at most 0.0003.
Values sent between devices are 32-bit elements; how exact they have to be, the bound alone decides.
No kernel may reach another device: no remote copies, remote signals or barrier semaphores. Data moves between devices by JAX's collectives and lax.ppermute only.
A program may use at most 64 MiB of HBM per device.

v0:
```python
import jax
import jax.numpy as jnp
from jax import lax
from jax.sharding import Mesh
from jax.sharding import PartitionSpec as P

ITERS = 4
DP = ("dp_0", "dp_1", "dp_2")
DP_GRP = ("dp_0", "dp_1", "dp_2", "grp")


def in_blocks(array, dim, size):
    before, after = (array.shape[:dim], array.shape[dim + 1 :])
    return jnp.moveaxis(array.reshape(*before, size, -1, *after), dim, 0)


def sum_at_owner(array, axis, dim):
    pieces = in_blocks(array, dim, lax.axis_size(axis))
    arrived = lax.all_to_all(pieces, axis, split_axis=0, concat_axis=0, tiled=True)
    return arrived.sum(axis=0)


def copy_for_each(array, axis):
    size = lax.axis_size(axis)
    return lax.all_to_all(
        jnp.broadcast_to(array[None], (size, *array.shape)), axis, 0, 0, tiled=True
    )


def joined_along(pieces, dim):
    pieces = jnp.moveaxis(pieces, 0, dim)
    dims = pieces.shape
    return pieces.reshape(*dims[:dim], dims[dim] * dims[dim + 1], *dims[dim + 2 :])


def collect(array, axis, dim):
    pieces = copy_for_each(array, axis)
    return joined_along(pieces, dim)


def taken_together(array, axis):
    return copy_for_each(array, axis).max(axis=0)


def summed_rows_2(array, chips, core, dim):
    sizes = (lax.axis_size(chips), lax.axis_size(core))
    pieces = in_blocks(array, dim, sizes[0] * sizes[1])
    inside = pieces.shape[1:]
    pieces = pieces.reshape(*sizes, *inside).swapaxes(0, 1).reshape(-1, *inside)
    pieces = lax.psum_scatter(pieces, core, scatter_dimension=0, tiled=True)
    return lax.psum_scatter(pieces, chips, scatter_dimension=0, tiled=True)[0]


def batched(left, right):
    return jnp.einsum(
        "bij,bjk->bik",
        left,
        right,
        precision=lax.Precision.HIGHEST,
        preferred_element_type=jnp.float32,
    )


def local(acts, grads, damping):
    dp_size = lax.axis_size(DP)
    grp_size = lax.axis_size("grp")
    dp_index = lax.axis_index(DP)
    grp_index = lax.axis_index("grp")
    width = acts.shape[1]
    cols = width // grp_size
    rows = width // dp_size
    scale = 1.0 / (acts.shape[0] * dp_size * grp_size)
    contract = (((0,), (0,)), ((), ()))
    highest = lax.Precision.HIGHEST
    stacked = (
        jnp.stack(
            [
                lax.dot_general(acts, acts, contract, preferred_element_type=jnp.float32),
                lax.dot_general(grads, grads, contract, preferred_element_type=jnp.float32),
            ],
            axis=0,
        )
        * scale
    )
    row_sums = lax.psum_scatter(stacked, DP, scatter_dimension=1, tiled=True)
    block = sum_at_owner(row_sums, "grp", 2)
    row_start = dp_index * rows
    col_start = grp_index * cols
    row_ids = row_start + lax.broadcasted_iota(jnp.int32, (rows, cols), 0)
    col_ids = col_start + lax.broadcasted_iota(jnp.int32, (rows, cols), 1)
    diagonal = (row_ids == col_ids).astype(jnp.float32)
    matrix = block + damping[:, None, None] * diagonal[None]
    matrix_rows = collect(matrix, "grp", 2)
    largest = jnp.max(jnp.sum(jnp.abs(matrix_rows), axis=2), axis=1)
    bounds = taken_together(largest, DP)
    alpha = 1.0 / bounds
    iterate = alpha[:, None, None] * diagonal[None]
    for step in range(ITERS):
        columns = collect(iterate, DP, 1)
        image = batched(matrix_rows, columns)
        image_rows = collect(image, "grp", 2)
        update = batched(image_rows, columns)
        iterate = 2.0 * iterate - update
    inverse_cols = collect(iterate, DP, 1)
    inverses = lax.all_gather(inverse_cols, "grp", axis=2, tiled=True)
    mapped = jnp.dot(acts, inverses[0], precision=highest, preferred_element_type=jnp.float32)
    weighted = jnp.dot(grads, inverses[1], precision=highest, preferred_element_type=jnp.float32)
    summed_rows = summed_rows_2(
        lax.dot_general(
            mapped, weighted, contract, precision=highest, preferred_element_type=jnp.float32
        )
        * scale,
        ("dp_0", "dp_1"),
        "dp_2",
        0,
    )
    return sum_at_owner(summed_rows, "grp", 1)


def solution(mesh):
    torus = Mesh(mesh.devices.reshape(8, 2, 2, mesh.shape["grp"]), ("dp_0", "dp_1", "dp_2", "grp"))
    return jax.shard_map(
        local,
        mesh=torus,
        in_specs=(P(DP_GRP, None), P(DP_GRP, None), P()),
        out_specs=P(DP, "grp"),
        check_vma=False,
    )
```

profile of v0, /device:TPU:2, one launch (start us, length us, event | category | flops | bytes accessed | tf_op | source)
XLA Modules:
  0.0 666.9 jit_solution(8184046820750787442)
XLA Ops:
  6.5 2.9 convolution_bitcast_fusion
  9.5 1.3 convolution_bitcast_fusion.1
  10.8 4.2 maximum_multiply_fusion
  15.0 134.3 %reduce-scatter.4.cloned.1.call-done = f32[2,32,1024]{2,1,0:T(8,128)} async-done(((f32[2,1024,1024]{2,1,0:T(8,128)}), f32[2,32,1024]{2,1,0:T(8,128)}) %reduce-scatter.4.cloned.1.call-update) | async-done | bytes 262160 | tf_op jit(solution)/shard_map/reduce_scatter | solution.py:85
  149.3 1.7 bitcast_bitcast_fusion
  151.0 7.3 %all-to-all-start = ((f32[8,2,32,128]{3,2,1,0:T(8,128)}), f32[8,2,32,128]{3,2,1,0:T(8,128)S(1)}, u32[]{:S(2)}, u32[]{:S(2)}) async-start(f32[8,2,32,128]{3,2,1,0:T(8,128)} %bitcast_bitcast_fusion), calls=%async_computation.1 | async-start | bytes 524288 | tf_op jit(solution)/shard_map/all_to_all | solution.py:19
  158.4 6.6 all-to-all-done
  165.0 0.1 multiply_add_fusion
  165.1 11.3 %all_to_all.66 = f32[8,2,32,128]{3,2,1,0:T(8,128)S(1)} all-to-all(f32[8,2,32,128]{3,2,1,0:T(8,128)S(1)} %broadcast_in_dim.22), channel_id=1, replica_groups=mesh['dp_0'=8,'dp_1'=2,'dp_2'=2,'grp'=8] {'grp'}, dimensions={0} | all-to-all | bytes 524288 | tf_op jit(solution)/shard_map/all_to_all | solution.py:25
  176.5 0.1 fusion.18
  176.6 0.1 reduce_max.18
  176.7 12.9 %all_to_all.67 = f32[32,1,2]{2,1,0:T(1,128)S(1)} all-to-all(f32[32,1,2]{2,1,0:T(1,128)S(1)} %broadcast_in_dim.23), channel_id=1, replica_groups=mesh['dp_0'=8,'dp_1'=2,'dp_2'=2,'grp'=8] {'dp_0','dp_1','dp_2'}, dimensions={0} | all-to-all | bytes 512 | tf_op jit(solution)/shard_map/all_to_all | solution.py:25
  189.7 0.1 broadcast_in_dim.24
  189.9 32.2 %all_to_all.68 = f32[32,2,32,128]{3,2,1,0:T(8,128)S(1)} all-to-all(f32[32,2,32,128]{3,2,1,0:T(8,128)S(1)} %broadcast_in_dim.24), channel_id=1, replica_groups=mesh['dp_0'=8,'dp_1'=2,'dp_2'=2,'grp'=8] {'dp_0','dp_1','dp_2'}, dimensions={0} | all-to-all | bytes 2097152 | tf_op jit(solution)/shard_map/all_to_all | solution.py:25
  222.1 0.1 copy.34
  222.2 0.7 fusion.16
  222.9 11.3 %all_to_all.69 = f32[8,2,32,128]{3,2,1,0:T(8,128)S(1)} all-to-all(f32[8,2,32,128]{3,2,1,0:T(8,128)S(1)} %broadcast_in_dim.25), channel_id=1, replica_groups=mesh['dp_0'=8,'dp_1'=2,'dp_2'=2,'grp'=8] {'grp'}, dimensions={0} | all-to-all | bytes 524288 | tf_op jit(solution)/shard_map/all_to_all | solution.py:25
  234.2 0.7 convolution_subtract_fusion.3
  234.8 0.1 broadcast_in_dim.26
  235.0 31.6 %all_to_all.70 = f32[32,2,32,128]{3,2,1,0:T(8,128)S(1)} all-to-all(f32[32,2,32,128]{3,2,1,0:T(8,128)S(1)} %broadcast_in_dim.26), channel_id=1, replica_groups=mesh['dp_0'=8,'dp_1'=2,'dp_2'=2,'grp'=8] {'dp_0','dp_1','dp_2'}, dimensions={0} | all-to-all | bytes 2097152 | tf_op jit(solution)/shard_map/all_to_all | solution.py:25
  266.5 0.1 copy.36
  266.6 0.7 fusion.14
  267.3 12.2 %all_to_all.71 = f32[8,2,32,128]{3,2,1,0:T(8,128)S(1)} all-to-all(f32[8,2,32,128]{3,2,1,0:T(8,128)S(1)} %broadcast_in_dim.27), channel_id=1, replica_groups=mesh['dp_0'=8,'dp_1'=2,'dp_2'=2,'grp'=8] {'grp'}, dimensions={0} | all-to-all | bytes 524288 | tf_op jit(solution)/shard_map/all_to_all | solution.py:25
  279.6 0.7 convolution_subtract_fusion.2
  280.2 0.1 broadcast_in_dim.28
  280.4 31.6 %all_to_all.72 = f32[32,2,32,128]{3,2,1,0:T(8,128)S(1)} all-to-all(f32[32,2,32,128]{3,2,1,0:T(8,128)S(1)} %broadcast_in_dim.28), channel_id=1, replica_groups=mesh['dp_0'=8,'dp_1'=2,'dp_2'=2,'grp'=8] {'dp_0','dp_1','dp_2'}, dimensions={0} | all-to-all | bytes 2097152 | tf_op jit(solution)/shard_map/all_to_all | solution.py:25
  311.9 0.1 copy.38
  312.0 0.7 fusion.12
  312.7 12.0 %all_to_all.73 = f32[8,2,32,128]{3,2,1,0:T(8,128)S(1)} all-to-all(f32[8,2,32,128]{3,2,1,0:T(8,128)S(1)} %broadcast_in_dim.29), channel_id=1, replica_groups=mesh['dp_0'=8,'dp_1'=2,'dp_2'=2,'grp'=8] {'grp'}, dimensions={0} | all-to-all | bytes 524288 | tf_op jit(solution)/shard_map/all_to_all | solution.py:25
  324.7 0.7 convolution_subtract_fusion.1
  325.4 0.1 broadcast_in_dim.30
  325.5 31.6 %all_to_all.74 = f32[32,2,32,128]{3,2,1,0:T(8,128)S(1)} all-to-all(f32[32,2,32,128]{3,2,1,0:T(8,128)S(1)} %broadcast_in_dim.30), channel_id=1, replica_groups=mesh['dp_0'=8,'dp_1'=2,'dp_2'=2,'grp'=8] {'dp_0','dp_1','dp_2'}, dimensions={0} | all-to-all | bytes 2097152 | tf_op jit(solution)/shard_map/all_to_all | solution.py:25
  357.2 0.7 fusion.10
  357.9 12.1 %all_to_all.75 = f32[8,2,32,128]{3,2,1,0:T(8,128)S(1)} all-to-all(f32[8,2,32,128]{3,2,1,0:T(8,128)S(1)} %broadcast_in_dim.31), channel_id=1, replica_groups=mesh['dp_0'=8,'dp_1'=2,'dp_2'=2,'grp'=8] {'grp'}, dimensions={0} | all-to-all | bytes 524288 | tf_op jit(solution)/shard_map/all_to_all | solution.py:25
  370.0 0.7 convolution_subtract_fusion
  370.7 0.1 broadcast_in_dim.32
  370.8 31.7 %all_to_all.76 = f32[32,2,32,128]{3,2,1,0:T(8,128)S(1)} all-to-all(f32[32,2,32,128]{3,2,1,0:T(8,128)S(1)} %broadcast_in_dim.32), channel_id=1, replica_groups=mesh['dp_0'=8,'dp_1'=2,'dp_2'=2,'grp'=8] {'dp_0','dp_1','dp_2'}, dimensions={0} | all-to-all | bytes 2097152 | tf_op jit(solution)/shard_map/all_to_all | solution.py:25
  402.5 1.1 copy.42
  403.7 119.5 %all-gather.2.cloned.1.call-done = f32[2,1024,1024]{2,1,0:T(8,128)} async-done(((f32[2,1024,128]{2,1,0:T(8,128)}), f32[2,1024,1024]{2,1,0:T(8,128)}) %all-gather.2.cloned.1.call-update) | async-done | bytes 8388624 | tf_op jit(solution)/shard_map/all_gather | solution.py:105
  523.3 8.6 %fusion.1 = f32[1024,512]{1,0:T(8,128)S(1)} fusion(bf16[512,1024]{1,0:T(8,128)(2,1)S(1)} %copy-done, f32[2,1024,1024]{2,1,0:T(8,128)} %all-gather.2.cloned.1.call-done), kind=kOutput, calls=%fused_computation.4 | convolution fusion | flops 6442450944 | bytes 7340032 | tf_op jit(solution)/shard_map/dot_general | solution.py:106
  531.9 8.8 %fusion = f32[1024,512]{1,0:T(8,128)S(1)} fusion(bf16[512,1024]{1,0:T(8,128)(2,1)S(1)} %copy-done.1, f32[2,1024,1024]{2,1,0:T(8,128)} %all-gather.2.cloned.1.call-done), kind=kOutput, calls=%fused_computation.2 | convolution fusion | flops 6442450944 | bytes 7340032 | tf_op jit(solution)/shard_map/dot_general | solution.py:107
  540.7 6.9 %convolution_multiply_fusion = f32[1024,1024]{1,0:T(8,128)S(1)} fusion(f32[1024,512]{1,0:T(8,128)S(1)} %fusion.1, f32[1024,512]{1,0:T(8,128)S(1)} %fusion), kind=kOutput, calls=%fused_computation.5 | convolution fusion | flops 6443499520 | bytes 8388608 | tf_op jit(solution)/shard_map/dot_general | solution.py:109
  547.6 2.2 copy.43
  549.9 16.7 %reduce-scatter.6.cloned.1.call-done = f32[16,32,1024]{2,1,0:T(8,128)} async-done(((f32[32,32,1024]{2,1,0:T(8,128)}), f32[16,32,1024]{2,1,0:T(8,128)}) %reduce-scatter.6.cloned.1.call-update) | async-done | bytes 2097168 | tf_op jit(solution)/shard_map/reduce_scatter | solution.py:50
  566.6 79.0 %reduce-scatter.8.cloned.1.call-done = f32[1,32,1024]{2,1,0:T(8,128)} async-done(((f32[16,32,1024]{2,1,0:T(8,128)}), f32[1,32,1024]{2,1,0:T(8,128)}) %reduce-scatter.8.cloned.1.call-update) | async-done | bytes 131088 | tf_op jit(solution)/shard_map/reduce_scatter | solution.py:51
  645.6 0.9 copy.52
  646.5 13.2 %all_to_all.77 = f32[8,32,128]{2,1,0:T(8,128)S(1)} all-to-all(f32[8,32,128]{2,1,0:T(8,128)S(1)} %bitcast.128), channel_id=1, replica_groups=mesh['dp_0'=8,'dp_1'=2,'dp_2'=2,'grp'=8] {'grp'}, dimensions={0} | all-to-all | bytes 262144 | tf_op jit(solution)/shard_map/all_to_all | solution.py:19
  659.8 0.6 reduce_sum.29
  (29 shorter events, 0.6 us)
Async XLA Ops:
  6.5 2.9 copy-start
  6.5 142.8 %reduce-scatter.4.cloned.1.call-start = ((), (), s32[]{:S(2)}) async-start(), calls=%async_computation.16 | async-start | bytes 8650752 | tf_op jit(solution)/shard_map/reduce_scatter | solution.py:85
  15.0 150.1 %copy-start.2 = (f32[2]{0:T(128)S(1)}, f32[2]{0:T(128)}, u32[]{:S(2)}) copy-start(f32[2]{0:T(128)} %param.5) | copy-start | bytes 28
  151.0 14.0 %all-to-all-start = ((f32[8,2,32,128]{3,2,1,0:T(8,128)}), f32[8,2,32,128]{3,2,1,0:T(8,128)S(1)}, u32[]{:S(2)}, u32[]{:S(2)}) async-start(f32[8,2,32,128]{3,2,1,0:T(8,128)} %bitcast_bitcast_fusion), calls=%async_computation.1 | async-start | bytes 524288 | tf_op jit(solution)/shard_map/all_to_all | solution.py:19
  158.3 364.9 %all-gather.2.cloned.1.call-start = ((), (), s32[]{:S(2)}) async-start(), calls=%async_computation.17 | async-start | bytes 9437184 | tf_op jit(solution)/shard_map/all_gather | solution.py:105
  403.7 128.2 %copy-start.1 = (bf16[512,1024]{1,0:T(8,128)(2,1)S(1)}, bf16[512,1024]{1,0:T(8,128)(2,1)}, u32[]{:S(2)}) copy-start(bf16[512,1024]{1,0:T(8,128)(2,1)} %param.4) | copy-start | bytes 3145732
  403.7 162.9 %reduce-scatter.6.cloned.1.call-start = ((), (), s32[]{:S(2)}) async-start(), calls=%async_computation.18 | async-start | bytes 6291456 | tf_op jit(solution)/shard_map/reduce_scatter | solution.py:50
  549.8 95.8 %reduce-scatter.8.cloned.1.call-start = ((), (), s32[]{:S(2)}) async-start(), calls=%async_computation.19 | async-start | bytes 2228224 | tf_op jit(solution)/shard_map/reduce_scatter | solution.py:51
Sparse Core Ops, SparseCore 0:
  15.1 134.1 reduce-scatter.3
  403.8 119.4 all-gather.1
  549.9 16.5 reduce-scatter.5
  569.0 76.5 reduce-scatter.7
where the time goes:
time: 668 us; the launch traced here: 667 us
  waiting for transfers between devices  356 us (53%)
  blocking collectives  244 us (37%)
  matrix products  33.7 us (5%)
  between operations  13.4 us (2%)
  starting transfers between devices  7.41 us (1%)
  local copies, waits for them, and re-layouts  7.01 us (1%)
    all_to_all x11, blocking collectives, copy_for_each(): lax.all_to_all(jnp.broadcast_to(array[None], (size, *array.shape)), axis,...  231 us
    reduce_scatter x1, waiting for transfers between devices, local(): row_sums = lax.psum_scatter(stacked, DP, scatter_dimension=1, tiled=True)  134 us
    all_gather x1, waiting for transfers between devices, local(): inverses = lax.all_gather(inverse_cols, 'grp', axis=2, tiled=True)  120 us
    reduce_scatter x1, waiting for transfers between devices, summed_rows_2(): return lax.psum_scatter(pieces, chips, scatter_dimension=0, tiled=True)[0]  79 us
    reduce_scatter x1, waiting for transfers between devices, summed_rows_2(): pieces = lax.psum_scatter(pieces, core, scatter_dimension=0, tiled=True)  16.7 us
  transfers between devices with their start and end apart: 5, of which 5 were waited for; matrix products, arithmetic and copies ran while one was open for 0% of the time, Pallas kernels for 0%

commit v1 on v0

v1 whole, which is shorter than its diff:
```python
import functools

import jax
import jax.numpy as jnp
from jax import lax
from jax.experimental import pallas as pl
from jax.experimental.pallas import tpu as pltpu
from jax.sharding import Mesh
from jax.sharding import PartitionSpec as P

INTERPRET = False
STEPS = 14
AXES = ("zh", "zl", "yl", "c", "x", "yh")
DP = ("zh", "zl", "yl", "c")
GRP = ("x", "yh")
RING = ("zl", "yl", "x", "yh")
B = 128
F32 = jnp.float32
BF16 = jnp.bfloat16


def sub_segments(start, size, piece):
    done = 0
    while done < size:
        q, r = divmod(start + done, piece)
        n = min(piece - r, size - done)
        yield q, r, done, n
        done += n


def dot(a, b):
    return jnp.dot(a, b, preferred_element_type=F32)


def gram_kernel(nb, nq, ng, core_ref, acts_ref, grads_ref, keep_ref, send_ref, t_ref):
    core = core_ref[0]
    width = nb * B
    half = width // 2
    piece = nb * (nb + 1) // 2 * B // nq
    acts = acts_ref[...]
    grads = grads_ref[...]
    for which, out in ((0, send_ref), (1, keep_ref)):
        own = (core == 0) if which else (core != 0)
        part = jnp.where(own, acts, grads)
        t_ref[...] = part.T
        for jj in range(nb // 2):
            cols = part[:, jj * 2 * B : (jj + 1) * 2 * B]
            res = dot(t_ref[: (jj + 1) * 2 * B, :], cols)
            for j in (2 * jj, 2 * jj + 1):
                lane = (j - 2 * jj) * B
                for q, r, at, n in sub_segments(j * (j + 1) // 2 * B, (j + 1) * B, piece):
                    out[q, r : r + n, :] = res[at : at + n, lane : lane + B]
    t_ref[...] = acts.T
    runs = half // 32
    for which, out in ((0, send_ref), (1, keep_ref)):
        first = core * half if which else (1 - core) * half
        rows = t_ref[pl.ds(pl.multiple_of(first, half), half), :]
        for jj in range(nb // 2):
            res = dot(rows, grads[:, jj * 2 * B : (jj + 1) * 2 * B])
            for s in range(runs):
                zh, rest = divmod(s, runs // 4)
                for k in range(2):
                    q = rest * ng + 2 * jj + k
                    out[q, piece + zh * 32 : piece + zh * 32 + 32, :] = res[s * 32 : s * 32 + 32, k * B : k * B + B]


def split(v):
    hi = v.astype(BF16)
    return hi, (v - hi.astype(F32)).astype(BF16)


def inverse_kernel(nb, scale, start_ref, damp_ref, packed_ref, out_ref, m_ref, hi_ref, lo_ref, s_ref, y_ref):
    width = nb * B
    damp = damp_ref[0]
    eye = (lax.broadcasted_iota(jnp.int32, (B, B), 0) == lax.broadcasted_iota(jnp.int32, (B, B), 1)).astype(F32)
    for j in range(nb):
        base = j * (j + 1) // 2 * B
        for i in range(j + 1):
            block = packed_ref[base + i * B : base + (i + 1) * B, :] * scale
            if i == j:
                block = block + damp * eye
            m_ref[i * B : (i + 1) * B, j * B : (j + 1) * B] = block
            if i != j:
                m_ref[j * B : (j + 1) * B, i * B : (i + 1) * B] = block.T
    total = jnp.zeros((8, width), F32)
    for i in range(nb):
        total = total + jnp.abs(m_ref[i * B : (i + 1) * B, :]).reshape(B // 8, 8, width).sum(axis=0)
    alpha = 1.0 / jnp.max(jnp.sum(total, axis=0, keepdims=True), axis=1, keepdims=True)
    for i in range(nb):
        rows = lax.broadcasted_iota(jnp.int32, (B, width), 0) + i * B
        ones = (rows == lax.broadcasted_iota(jnp.int32, (B, width), 1)).astype(F32)
        hi, lo = split(ones - alpha * m_ref[i * B : (i + 1) * B, :])
        hi_ref[i * B : (i + 1) * B, :] = hi
        lo_ref[i * B : (i + 1) * B, :] = lo
    start = pl.multiple_of(start_ref[0], B)
    rows = lax.broadcasted_iota(jnp.int32, (B, width), 0) + start
    ones = (rows == lax.broadcasted_iota(jnp.int32, (B, width), 1)).astype(F32)
    s_ref[...] = ones
    y_ref[...] = 2.0 * ones - alpha * m_ref[pl.ds(start, B), :]

    def step(_, carry):
        hi, lo = split(y_ref[...])
        both = jnp.concatenate([hi, lo], axis=0)
        first = dot(both, hi_ref[...])
        y_ref[...] = (dot(hi, lo_ref[...]) + first[B:]) + first[:B] + s_ref[...]
        return carry

    lax.fori_loop(0, STEPS, step, 0)
    out_ref[...] = alpha * y_ref[...]


def vmem(n):
    return [pl.BlockSpec(memory_space=pltpu.VMEM)] * n


def smem():
    return pl.BlockSpec(memory_space=pltpu.SMEM)


def gram_pieces(acts, grads, core, nq, ng):
    tokens, width = acts.shape
    nb = width // B
    piece = nb * (nb + 1) // 2 * B // nq
    cross = width // 2 * width // nq // B
    shape = jax.ShapeDtypeStruct((nq, piece + cross, B), F32)
    return pl.pallas_call(
        functools.partial(gram_kernel, nb, nq, ng),
        out_shape=[shape, shape],
        in_specs=[smem()] + vmem(2),
        out_specs=vmem(2),
        scratch_shapes=[pltpu.VMEM((width, tokens), BF16)],
        name="grams",
        interpret=INTERPRET,
    )(core[None], acts, grads)


def inverse_rows(packed, damp, start, nb, scale):
    width = nb * B
    return pl.pallas_call(
        functools.partial(inverse_kernel, nb, scale),
        out_shape=jax.ShapeDtypeStruct((B, width), F32),
        in_specs=[smem(), smem()] + vmem(1),
        out_specs=vmem(1)[0],
        scratch_shapes=[
            pltpu.VMEM((width, width), F32),
            pltpu.VMEM((width, width), BF16),
            pltpu.VMEM((width, width), BF16),
            pltpu.VMEM((B, width), F32),
            pltpu.VMEM((B, width), F32),
        ],
        cost_estimate=pl.CostEstimate(
            flops=2 * 3 * STEPS * B * width * width, bytes_accessed=4 * width * width, transcendentals=0
        ),
        name="inverse",
        interpret=INTERPRET,
    )(start[None], damp[None], packed)


def everywhere(array, axes):
    size = lax.axis_size(axes)
    return lax.all_to_all(jnp.broadcast_to(array[None], (size, *array.shape)), axes, 0, 0, tiled=True)


def swapped(array):
    return lax.ppermute(array, "c", [(0, 1), (1, 0)])


def local(acts, grads, damping):
    tokens, width = acts.shape
    nb = width // B
    nq, ng = lax.axis_size(RING), lax.axis_size(GRP)
    nz = lax.axis_size("zh")
    scale = 1.0 / (tokens * lax.axis_size(AXES))
    core = lax.axis_index("c")
    keep, send = gram_pieces(acts, grads, core, nq, ng)
    chip = keep + swapped(send)
    piece = nb * (nb + 1) // 2 * B // nq
    plane = lax.all_to_all(chip, RING, 0, 0, tiled=True).sum(axis=0)
    factor, cross = plane[:piece], plane[piece:].reshape(nz, -1, B)
    mixed = jnp.concatenate([jnp.broadcast_to(factor[None], (nz, *factor.shape)), cross], axis=1)
    whole = lax.all_to_all(mixed, "zh", 0, 0, tiled=True).sum(axis=0)
    factor, cross = whole[:piece], whole[piece:]
    packed = everywhere(factor, RING).reshape(-1, B)
    cross_rows = everywhere(cross, GRP)
    height = lax.axis_index("zh") * lax.axis_size("zl") + lax.axis_index("zl")
    start = jnp.where(core == 0, height * B, lax.axis_index(GRP) * B).astype(jnp.int32)
    damp = jnp.where(core == 0, damping[0], damping[1])
    mine = inverse_rows(packed, damp, start, nb, scale)
    other = swapped(mine)
    left = jnp.where(core == 0, mine, other)
    right = jnp.where(core == 0, other, mine)
    highest = lax.Precision.HIGHEST
    right_blocks = right.reshape(B, ng, B)
    z = jnp.einsum("grk,cgk->rc", cross_rows * scale, right_blocks, precision=highest, preferred_element_type=F32)
    z_all = everywhere(z, DP)
    z_all = z_all.reshape(-1, 2, *z.shape).swapaxes(0, 1).reshape(width, B)
    rows = z.shape[0]
    first = lax.axis_index("yl") * 2 * rows + core * rows
    left_rows = lax.dynamic_slice_in_dim(left, first, rows, 0)
    return jnp.dot(left_rows, z_all, precision=highest, preferred_element_type=F32)


def solution(mesh):
    torus = Mesh(mesh.devices.reshape(4, 2, 2, 2, 4, 2), AXES)
    return jax.shard_map(
        local,
        mesh=torus,
        in_specs=(P(AXES, None), P(AXES, None), P()),
        out_specs=P(DP, GRP),
        check_vma=False,
    )
```

time: 668 us -> 199 us (0.30)
  waiting for transfers between devices: 356 us -> 52.9 us
  blocking collectives: 244 us -> 92.7 us
  matrix products: 33.7 us -> 2.54 us
  Pallas kernels: 0 us -> 25.7 us
  between operations: 13.4 us -> 1.32 us
    reduce_scatter x3 -> x0, waiting for transfers between devices: 230 us -> none  [the longest x1 134 us: local(): row_sums = lax.psum_scatter(stacked, DP, scatter_dimension=1, tiled=True)]
    all_to_all x12 -> x3, blocking collectives: 244 us -> 92.7 us  [the longest x1 62.2 us: local(): plane = lax.all_to_all(chip, RING, 0, 0, tiled=True).sum(axis=0)]
    all_gather x1 -> x0, waiting for transfers between devices: 120 us -> none  [local(): inverses = lax.all_gather(inverse_cols, 'grp', axis=2, tiled=True)]
    all_to_all x1 -> x2, waiting for transfers between devices: 6.59 us -> 45.2 us  [everywhere(): lax.all_to_all(jnp.broadcast_to(array[None], (size, *array.shape)), axes,...]
    dot_general x13 -> x2, matrix products: 33.7 us -> 2.54 us  [the longest x1 1.91 us: local(): jnp.dot(left_rows, z_all, precision=highest, preferred_element_type=F32)]
    pallas_call x0 -> x2, Pallas kernels: none -> 25.7 us  [the longest x1 18.6 us: inverse_rows(): pl.pallas_call(functools.partial(inverse_kernel, nb, scale), out_shape=ja...]
    ppermute x0 -> x2, waiting for transfers between devices: none -> 7.74 us  [swapped(): return lax.ppermute(array, 'c', [(0, 1), (1, 0)])]
  transfers between devices with their start and end apart: 5 -> 4, of which waited for: 5 -> 3; matrix products, arithmetic and copies ran while one was open for 0% -> 0% of each run, Pallas kernels for 0% -> 0%
where the time goes in v1:
time: 199 us; the launch traced here: 198 us
  blocking collectives  92.7 us (47%)
  waiting for transfers between devices  52.9 us (27%)
  Pallas kernels  25.7 us (13%)
  starting transfers between devices  12.4 us (6%)
  other arithmetic  5.38 us (3%)
  local copies, waits for them, and re-layouts  4.52 us (2%)
  matrix products  2.54 us (1%)
    all_to_all x1, blocking collectives, local(): plane = lax.all_to_all(chip, RING, 0, 0, tiled=True).sum(axis=0)  62.2 us
    all_to_all x2, waiting for transfers between devices, everywhere(): lax.all_to_all(jnp.broadcast_to(array[None], (size, *array.shape)), axes,...  45.2 us
    all_to_all x1, blocking collectives, local(): whole = lax.all_to_all(mixed, 'zh', 0, 0, tiled=True).sum(axis=0)  19.2 us
    pallas_call x1, Pallas kernels, inverse_rows(): pl.pallas_call(functools.partial(inverse_kernel, nb, scale), out_shape=ja...  18.6 us
    all_to_all x2, starting transfers between devices, everywhere(): lax.all_to_all(jnp.broadcast_to(array[None], (size, *array.shape)), axes,...  12.4 us
    all_to_all x1, blocking collectives, everywhere(): lax.all_to_all(jnp.broadcast_to(array[None], (size, *array.shape)), axes,...  11.3 us
    ppermute x2, waiting for transfers between devices, swapped(): return lax.ppermute(array, 'c', [(0, 1), (1, 0)])  7.74 us
    pallas_call x1, Pallas kernels, gram_pieces(): pl.pallas_call(functools.partial(gram_kernel, nb, nq, ng), out_shape=[sha...  7.18 us
  transfers between devices with their start and end apart: 4, of which 3 were waited for; matrix products, arithmetic and copies ran while one was open for 0% of the time, Pallas kernels for 0%

profile of v1, /device:TPU:2, one launch (start us, length us, event | category | flops | bytes accessed | tf_op | source)
XLA Modules:
  0.0 197.5 jit_solution(6432026159752418028)
XLA Ops:
  0.0 7.2 %grams.1 = (f32[32,272,128]{2,1,0:T(8,128)}, f32[32,272,128]{2,1,0:T(8,128)}) custom-call(s32[1]{0:T(128)} %bitcast.4.core_ref, bf16[512,1024]{1,0:T(8,128)(2,1)} %acts_ref.1, bf16[512,1024]{1,0:T(8,128)(2,1)} %grads_ref.1), custom_call_target="tpu_custom_call" | custom-call | tf_op jit(solution)/shard_map/grams/pallas_call | solution.py:126
  7.2 0.0 collective-permute-start
  7.2 7.7 %collective-permute-done = f32[32,272,128]{2,1,0:T(8,128)S(1)} collective-permute-done((f32[32,272,128]{2,1,0:T(8,128)}, f32[32,272,128]{2,1,0:T(8,128)S(1)}, u32[]{:S(2)}, u32[]{:S(2)}) %collective-permute-start) | collective-permute-done | bytes 4456480 | tf_op jit(solution)/shard_map/ppermute | solution.py:165
  14.9 2.8 %add.17 = f32[32,272,128]{2,1,0:T(8,128)S(1)} add(f32[32,272,128]{2,1,0:T(8,128)} %get-tuple-element.7, f32[32,272,128]{2,1,0:T(8,128)S(1)} %collective-permute-done) | non-fusion elementwise | flops 1114112 | bytes 13369344 | tf_op jit(solution)/shard_map/add | solution.py:176
  17.8 62.2 %all_to_all.25 = f32[32,272,128]{2,1,0:T(8,128)} all-to-all(f32[32,272,128]{2,1,0:T(8,128)S(1)} %add.17), channel_id=1, replica_groups=mesh['zh'=4,'zl'=2,'yl'=2,'c'=2,'x'=4,'yh'=2] {'zl','yl','x','yh'}, dimensions={0} | all-to-all | bytes 8912896 | tf_op jit(solution)/shard_map/all_to_all | solution.py:178
  80.0 2.5 %reduce_sum.18 = f32[272,128]{1,0:T(8,128)S(1)} reduce(f32[32,272,128]{2,1,0:T(8,128)} %all_to_all.25, f32[]{:T(128)} %constant.32.clone.1), dimensions={0}, to_apply=%region_0.0 | reduce | flops 1079296 | bytes 4595716 | tf_op jit(solution)/shard_map/reduce_sum | solution.py:178
  82.5 0.0 copy-start.1
  82.6 19.2 %all_to_all.26 = f32[4,176,128]{2,1,0:T(8,128)S(1)} all-to-all(f32[4,176,128]{2,1,0:T(8,128)S(1)} %pad_maximum_fusion), channel_id=1, replica_groups=mesh['zh'=4,'zl'=2,'yl'=2,'c'=2,'x'=4,'yh'=2] {'zh'}, dimensions={0} | all-to-all | bytes 720896 | tf_op jit(solution)/shard_map/all_to_all | solution.py:181
  101.8 1.6 broadcast_in_dim.18
  103.4 6.8 %all-to-all-start.2 = ((f32[32,144,128]{2,1,0:T(8,128)}), f32[32,144,128]{2,1,0:T(8,128)S(1)}, u32[]{:S(2)}, u32[]{:S(2)}) async-start(f32[32,144,128]{2,1,0:T(8,128)} %broadcast_in_dim.18), calls=%async_computation.2 | async-start | bytes 4718592 | tf_op jit(solution)/shard_map/all_to_all | solution.py:161
  110.3 0.0 copy-done.1
  110.3 0.6 fusion.9
  112.0 27.5 %all-to-all-done.2 = f32[32,144,128]{2,1,0:T(8,128)S(1)} async-done(((f32[32,144,128]{2,1,0:T(8,128)}), f32[32,144,128]{2,1,0:T(8,128)S(1)}, u32[]{:S(2)}, u32[]{:S(2)}) %all-to-all-start.2) | async-done | bytes 2359328 | tf_op jit(solution)/shard_map/all_to_all | solution.py:161
  139.6 0.0 copy-start
  139.6 1.4 copy-done
  141.0 18.6 %inverse.1 = f32[128,1024]{1,0:T(8,128)} custom-call(s32[1]{0:T(128)} %bitcast.start_ref, f32[1]{0:T(128)} %bitcast.3.damp_ref, f32[4608,128]{1,0:T(8,128)} %bitcast.21), custom_call_target="tpu_custom_call" | custom-call | flops 11274289152 | bytes 4194304 | tf_op jit(solution)/shard_map/inverse/pallas_call | solution.py:139
  159.5 0.0 collective-permute-start.1
  159.6 11.3 %all_to_all.27 = f32[8,32,128]{2,1,0:T(8,128)S(1)} all-to-all(f32[8,32,128]{2,1,0:T(8,128)S(1)} %broadcast_in_dim.38), channel_id=1, replica_groups=mesh['zh'=4,'zl'=2,'yl'=2,'c'=2,'x'=4,'yh'=2] {'x','yh'}, dimensions={0} | all-to-all | bytes 262144 | tf_op jit(solution)/shard_map/all_to_all | solution.py:161
  170.8 0.0 collective-permute-done.1
  170.8 0.6 convolution_bitcast_fusion
  171.5 0.9 broadcast_in_dim.39
  172.3 5.6 %all-to-all-start.4 = ((f32[32,32,128]{2,1,0:T(8,128)}), f32[32,32,128]{2,1,0:T(8,128)S(1)}, u32[]{:S(2)}, u32[]{:S(2)}) async-start(f32[32,32,128]{2,1,0:T(8,128)} %broadcast_in_dim.39), calls=%async_computation.4 | async-start | bytes 1048576 | tf_op jit(solution)/shard_map/all_to_all | solution.py:161
  177.9 17.6 %all-to-all-done.4 = f32[32,32,128]{2,1,0:T(8,128)S(1)} async-done(((f32[32,32,128]{2,1,0:T(8,128)}), f32[32,32,128]{2,1,0:T(8,128)S(1)}, u32[]{:S(2)}, u32[]{:S(2)}) %all-to-all-start.4) | async-done | bytes 524320 | tf_op jit(solution)/shard_map/all_to_all | solution.py:161
  195.6 1.9 fusion.2
  (9 shorter events, 0.1 us)
Async XLA Ops:
  7.2 7.7 %collective-permute-start = (f32[32,272,128]{2,1,0:T(8,128)}, f32[32,272,128]{2,1,0:T(8,128)S(1)}, u32[]{:S(2)}, u32[]{:S(2)}) collective-permute-start(f32[32,272,128]{2,1,0:T(8,128)} %get-tuple-element.8), channel_id=1, source_target_pairs={{0,8},{8,0},{1,9},{9,1},{2,10},{10,2},{3,11},{11,3},{4,12},{12,4},... | collective-permute-start | bytes 13369352 | tf_op jit(solution)/shard_map/ppermute | solution.py:165
  82.5 27.7 %copy-start.1 = (f32[2]{0:T(128)S(1)}, f32[2]{0:T(128)}, u32[]{:S(2)}) copy-start(f32[2]{0:T(128)} %param.5) | copy-start | bytes 28
  103.4 36.2 %all-to-all-start.2 = ((f32[32,144,128]{2,1,0:T(8,128)}), f32[32,144,128]{2,1,0:T(8,128)S(1)}, u32[]{:S(2)}, u32[]{:S(2)}) async-start(f32[32,144,128]{2,1,0:T(8,128)} %broadcast_in_dim.18), calls=%async_computation.2 | async-start | bytes 4718592 | tf_op jit(solution)/shard_map/all_to_all | solution.py:161
  139.6 1.4 copy-start
  159.5 11.3 %collective-permute-start.1 = (f32[128,1024]{1,0:T(8,128)}, f32[128,1024]{1,0:T(8,128)S(1)}, u32[]{:S(2)}, u32[]{:S(2)}) collective-permute-start(f32[128,1024]{1,0:T(8,128)} %inverse.1), channel_id=1, source_target_pairs={{0,8},{8,0},{1,9},{9,1},{2,10},{10,2},{3,11},{11,3},{4,12},{12,4},... | collective-permute-start | bytes 1572872 | tf_op jit(solution)/shard_map/ppermute | solution.py:165
  172.3 23.2 %all-to-all-start.4 = ((f32[32,32,128]{2,1,0:T(8,128)}), f32[32,32,128]{2,1,0:T(8,128)S(1)}, u32[]{:S(2)}, u32[]{:S(2)}) async-start(f32[32,32,128]{2,1,0:T(8,128)} %broadcast_in_dim.39), calls=%async_computation.4 | async-start | bytes 1048576 | tf_op jit(solution)/shard_map/all_to_all | solution.py:161

commit v2 on v1

v2 whole, which is shorter than its diff:
```python
import functools
import math

import jax
import jax.numpy as jnp
from jax import lax
from jax.experimental import pallas as pl
from jax.experimental.pallas import tpu as pltpu
from jax.sharding import Mesh
from jax.sharding import PartitionSpec as P

INTERPRET = False
STEPS = 14
AXES = ("zh", "zl", "yl", "c", "x", "yh")
DP = ("zh", "zl", "yl", "c")
GRP = ("x", "yh")
PLANE = ("yl", "x", "yh")
RING = ("zl", "yl", "x", "yh")
B = 128
F32 = jnp.float32
BF16 = jnp.bfloat16


def sub_segments(start, size, piece):
    done = 0
    while done < size:
        q, r = divmod(start + done, piece)
        n = min(piece - r, size - done)
        yield q, r, done, n
        done += n


def dot(a, b):
    return jnp.dot(a, b, preferred_element_type=F32)


def factor_kernel(nb, nq, core_ref, acts_ref, grads_ref, keep_ref, send_ref, t_ref):
    core = core_ref[0]
    piece = nb * (nb + 1) // 2 * B // nq
    acts = acts_ref[...]
    grads = grads_ref[...]
    for which, out in ((0, send_ref), (1, keep_ref)):
        own = (core == 0) if which else (core != 0)
        part = jnp.where(own, acts, grads)
        t_ref[...] = part.T
        for jj in range(nb // 2):
            cols = part[:, jj * 2 * B : (jj + 1) * 2 * B]
            res = dot(t_ref[: (jj + 1) * 2 * B, :], cols)
            for j in (2 * jj, 2 * jj + 1):
                lane = (j - 2 * jj) * B
                for q, r, at, n in sub_segments(j * (j + 1) // 2 * B, (j + 1) * B, piece):
                    out[q, r : r + n, :] = res[at : at + n, lane : lane + B]


def cross_kernel(nb, nz, ng, core_ref, acts_ref, grads_ref, keep_ref, send_ref, t_ref):
    core = core_ref[0]
    half = nb * B // 2
    grads = grads_ref[...]
    t_ref[...] = acts_ref[...].T
    rows = keep_ref.shape[2]
    runs = half // rows
    for which, out in ((0, send_ref), (1, keep_ref)):
        first = core * half if which else (1 - core) * half
        part = t_ref[pl.ds(pl.multiple_of(first, half), half), :]
        for jj in range(nb // 2):
            res = dot(part, grads[:, jj * 2 * B : (jj + 1) * 2 * B])
            for s in range(runs):
                zh, rest = divmod(s, runs // nz)
                for k in range(2):
                    out[zh, rest * ng + 2 * jj + k, :, :] = res[s * rows : s * rows + rows, k * B : k * B + B]


def turned_add_kernel(nz, at_ref, keep_ref, came_ref, *outs):
    for k, out in enumerate(outs):
        z = lax.rem(at_ref[0] + k, nz)
        out[...] = keep_ref[z] + came_ref[z]


def halves_kernel(at_ref, pieces_ref, keep_ref, send_ref, sum_ref):
    total = pieces_ref[0]
    for k in range(1, pieces_ref.shape[0]):
        total = total + pieces_ref[k]
    sum_ref[...] = total
    size = keep_ref.shape[0]
    at = at_ref[0]
    keep_ref[...] = sum_ref[pl.ds(pl.multiple_of(at * size, 8), size), :]
    send_ref[...] = sum_ref[pl.ds(pl.multiple_of((1 - at) * size, 8), size), :]


def outgoing_kernel(*refs):
    out = refs[-1]
    count = (len(refs) - 1) // 2
    factor = refs[0][...]
    for ref in refs[1:count]:
        factor = factor + ref[...]
    piece = factor.shape[0]
    for q in range(out.shape[0]):
        out[q, :piece, :] = factor
        cross = refs[count][q]
        for ref in refs[count + 1 : 2 * count]:
            cross = cross + ref[q]
        out[q, piece:, :] = cross


def last_kernel(at_ref, mine_ref, other_ref, *refs):
    out_ref, z_ref = refs[-2:]
    core, zl, yl = at_ref[0], at_ref[1], at_ref[2]
    own, came = refs[:4], refs[4]
    for d in range(4):
        dz, dy = divmod(d, 2)
        pz, py = jnp.bitwise_xor(zl, dz), jnp.bitwise_xor(yl, dy)
        for zh in range(z_ref.shape[1]):
            z_ref[core, zh, pz, py] = own[d][zh]
            z_ref[1 - core, zh, pz, py] = came[d, zh]
    rows = out_ref.shape[0]
    first = pl.multiple_of(yl * 2 * rows + core * rows, 8)
    mine = mine_ref[pl.ds(first, rows), :]
    other = other_ref[pl.ds(first, rows), :]
    hi, lo = split(jnp.where(core == 0, mine, other))
    zhi, zlo = split(z_ref[...].reshape(-1, B))
    out_ref[...] = (dot(hi, zlo) + dot(lo, zhi)) + dot(hi, zhi)


def split(v):
    hi = v.astype(BF16)
    return hi, (v - hi.astype(F32)).astype(BF16)


def inverse_kernel(nb, nq, scale, start_ref, damp_ref, packed_ref, out_ref, m_ref, hi_ref, lo_ref, s_ref, y_ref):
    width = nb * B
    damp = damp_ref[0]
    eye = (lax.broadcasted_iota(jnp.int32, (B, B), 0) == lax.broadcasted_iota(jnp.int32, (B, B), 1)).astype(F32)
    piece = nb * (nb + 1) // 2 * B // (2 * nq)
    for j in range(nb):
        base = j * (j + 1) // 2 * B
        for i in range(j + 1):
            parts = []
            for q, r, _, n in sub_segments(base + i * B, B, piece):
                parts.append(packed_ref[q % 2 * nq + q // 2, r : r + n, :])
            block = jnp.concatenate(parts, axis=0) * scale
            if i == j:
                block = block + damp * eye
            m_ref[i * B : (i + 1) * B, j * B : (j + 1) * B] = block
            if i != j:
                m_ref[j * B : (j + 1) * B, i * B : (i + 1) * B] = block.T
    total = jnp.zeros((8, width), F32)
    for i in range(nb):
        total = total + jnp.abs(m_ref[i * B : (i + 1) * B, :]).reshape(B // 8, 8, width).sum(axis=0)
    alpha = 1.0 / jnp.max(jnp.sum(total, axis=0, keepdims=True), axis=1, keepdims=True)
    for i in range(nb):
        rows = lax.broadcasted_iota(jnp.int32, (B, width), 0) + i * B
        ones = (rows == lax.broadcasted_iota(jnp.int32, (B, width), 1)).astype(F32)
        hi, lo = split(ones - alpha * m_ref[i * B : (i + 1) * B, :])
        hi_ref[i * B : (i + 1) * B, :] = hi
        lo_ref[i * B : (i + 1) * B, :] = lo
    start = pl.multiple_of(start_ref[0], B)
    rows = lax.broadcasted_iota(jnp.int32, (B, width), 0) + start
    ones = (rows == lax.broadcasted_iota(jnp.int32, (B, width), 1)).astype(F32)
    s_ref[...] = ones
    y_ref[...] = 2.0 * ones - alpha * m_ref[pl.ds(start, B), :]

    def step(_, carry):
        hi, lo = split(y_ref[...])
        both = jnp.concatenate([hi, lo], axis=0)
        first = dot(both, hi_ref[...])
        y_ref[...] = (dot(hi, lo_ref[...]) + first[B:]) + first[:B] + s_ref[...]
        return carry

    lax.fori_loop(0, STEPS, step, 0)
    out_ref[...] = alpha * y_ref[...]


def vmem(n):
    return [pl.BlockSpec(memory_space=pltpu.VMEM)] * n


def smem(n=1):
    return [pl.BlockSpec(memory_space=pltpu.SMEM)] * n


def call(kernel, scalars, arrays, outs, scratch=(), flops=0, limit=32):
    moved = sum(4 * math.prod(o) for o in outs) + sum(a.size * a.dtype.itemsize for a in arrays)
    shapes = [jax.ShapeDtypeStruct(o, F32) for o in outs]
    return pl.pallas_call(
        kernel,
        out_shape=shapes,
        in_specs=smem(len(scalars)) + vmem(len(arrays)),
        out_specs=vmem(len(outs)),
        scratch_shapes=list(scratch),
        cost_estimate=pl.CostEstimate(flops=flops, bytes_accessed=moved, transcendentals=0),
        compiler_params=pltpu.CompilerParams(vmem_limit_bytes=limit << 20),
        interpret=INTERPRET,
    )(*[jnp.atleast_1d(s) for s in scalars], *arrays)


def everywhere(array, axes):
    size = lax.axis_size(axes)
    return lax.all_to_all(jnp.broadcast_to(array[None], (size, *array.shape)), axes, 0, 0, tiled=True)


def swapped(array, axes):
    pairs = [(k, lax.axis_size(axes) - 1 - k) for k in range(lax.axis_size(axes))]
    return lax.ppermute(array, axes, pairs)


def shifted(array, axis, by):
    size = lax.axis_size(axis)
    return lax.ppermute(array, axis, [(k, (k + by) % size) for k in range(size)])


def program(acts, grads, damping):
    tokens, width = acts.shape
    nb = width // B
    nq, ng, nz = lax.axis_size(PLANE), lax.axis_size(GRP), lax.axis_size("zh")
    scale = 1.0 / (tokens * lax.axis_size(AXES))
    core, zh, zl, yl = (lax.axis_index(a) for a in ("c", "zh", "zl", "yl"))
    packed_rows = nb * (nb + 1) // 2 * B
    rows = width // lax.axis_size(DP)

    kept, sent = call(
        functools.partial(factor_kernel, nb, nq), [core], [acts, grads],
        [(nq, packed_rows // nq, B)] * 2, [pltpu.VMEM((width, tokens), BF16)], flops=2 * tokens * width * width,
    )
    cross_shape = (nz, 2 * nq, rows, B)
    cross_kept, cross_sent = call(
        functools.partial(cross_kernel, nb, nz, ng), [core], [acts, grads],
        [cross_shape] * 2, [pltpu.VMEM((width, tokens), BF16)], flops=2 * tokens * width * width,
    )
    plane = lax.all_to_all(kept + swapped(sent, "c"), PLANE, 0, 0, tiled=True)
    half_shape = (packed_rows // nq // 2, B)
    keep, send = call(halves_kernel, [zl], [plane], [half_shape] * 2, [pltpu.VMEM((2 * half_shape[0], B), F32)])
    factor = keep + swapped(send, "zl")
    factors = [factor] + [shifted(factor, "zh", k) for k in range(1, nz)]
    turned = call(
        functools.partial(turned_add_kernel, nz), [zh], [cross_kept, swapped(cross_sent, "c")],
        [cross_shape[1:]] * nz,
    )
    crosses = [turned[0]] + [shifted(turned[k], "zh", k) for k in range(1, nz)]
    (outgoing,) = call(outgoing_kernel, [], factors + crosses, [(2 * nq, half_shape[0] + rows, B)])
    pieces = lax.all_to_all(outgoing, RING, 0, 0, tiled=True)
    cross = pieces[:, half_shape[0] :, :].sum(axis=0) * scale
    cross_rows = everywhere(cross, ("zh", "x", "yh")).reshape(nz, ng, rows, B)
    height = zh * lax.axis_size("zl") + zl
    start = jnp.where(core == 0, height * B, lax.axis_index(GRP) * B).astype(jnp.int32)
    damp = jnp.where(core == 0, damping[0], damping[1])
    (mine,) = call(
        functools.partial(inverse_kernel, nb, nq, scale), [start, damp], [pieces], [(B, width)],
        [
            pltpu.VMEM((width, width), F32),
            pltpu.VMEM((width, width), BF16),
            pltpu.VMEM((width, width), BF16),
            pltpu.VMEM((B, width), F32),
            pltpu.VMEM((B, width), F32),
        ],
        flops=2 * 3 * STEPS * B * width * width,
    )
    other = swapped(mine, "c")
    right = jnp.where(core == 0, other, mine).reshape(B, ng, B)
    z = jnp.einsum(
        "zgrk,cgk->zrc", cross_rows, right, precision=lax.Precision.HIGHEST, preferred_element_type=F32
    )
    near = [z, swapped(z, "yl"), swapped(z, "zl"), swapped(z, ("zl", "yl"))]
    came = swapped(jnp.stack(near), "c")
    at = jnp.stack([core, zl, yl]).astype(jnp.int32)
    (out,) = call(
        last_kernel, [at], [mine, other, *near, came], [(rows, B)],
        [pltpu.VMEM((2, nz, 2, 2, rows, B), F32)],
    )
    return out


def solution(mesh):
    torus = Mesh(mesh.devices.reshape(4, 2, 2, 2, 4, 2), AXES)
    return jax.shard_map(
        program,
        mesh=torus,
        in_specs=(P(AXES, None), P(AXES, None), P()),
        out_specs=P(DP, GRP),
        check_vma=False,
    )
```

time: 199 us -> 178 us (0.89)
  blocking collectives: 92.7 us -> 0 us
  waiting for transfers between devices: 52.9 us -> 91.4 us
  starting transfers between devices: 12.4 us -> 45.8 us
  other arithmetic: 5.38 us -> 1.94 us
  local copies, waits for them, and re-layouts: 4.52 us -> 6.92 us
    all_to_all x3 -> x0, blocking collectives: 92.7 us -> none  [the longest x1 62.2 us: local(): plane = lax.all_to_all(chip, RING, 0, 0, tiled=True).sum(axis=0)]
    all_to_all x0 -> x2, waiting for transfers between devices: none -> 55.9 us  [the longest x1 34.2 us: program(): pieces = lax.all_to_all(outgoing, RING, 0, 0, tiled=True)]
    all_to_all x2 -> x1, waiting for transfers between devices: 45.2 us -> 0.01 us  [everywhere(): lax.all_to_all(jnp.broadcast_to(array[None], (size, *array.shape)), axes,...]
    ppermute x2 -> x14, waiting for transfers between devices: 7.74 us -> 35.6 us  [the longest x8 29.5 us: swapped(): return lax.ppermute(array, axes, pairs)]
    ppermute x2 -> x14, starting transfers between devices: 0.01 us -> 23.2 us  [the longest x6 16.8 us: shifted(): lax.ppermute(array, axis, [(k, (k + by) % size) for k in range(size)])]
    all_to_all x0 -> x2, starting transfers between devices: none -> 15 us  [the longest x1 7.5 us: program(): pieces = lax.all_to_all(outgoing, RING, 0, 0, tiled=True)]
    all_to_all x2 -> x1, starting transfers between devices: 12.4 us -> 7.61 us  [everywhere(): lax.all_to_all(jnp.broadcast_to(array[None], (size, *array.shape)), axes,...]
    unnamed x4 -> x10, local copies, waits for them, and re-layouts: 1.43 us -> 5.44 us
  transfers between devices with their start and end apart: 4 -> 17, of which waited for: 3 -> 12; matrix products, arithmetic and copies ran while one was open for 0% -> 1% of each run, Pallas kernels for 0% -> 12%
where the time goes in v2:
time: 178 us; the launch traced here: 177 us
  waiting for transfers between devices  91.4 us (51%)
  starting transfers between devices  45.8 us (26%)
  Pallas kernels  27.5 us (15%)
  local copies, waits for them, and re-layouts  6.92 us (4%)
  other arithmetic  1.94 us (1%)
    all_to_all x1, waiting for transfers between devices, program(): pieces = lax.all_to_all(outgoing, RING, 0, 0, tiled=True)  34.2 us
    ppermute x8, waiting for transfers between devices, swapped(): return lax.ppermute(array, axes, pairs)  29.5 us
    pallas_call x7, Pallas kernels, call(): pl.pallas_call(kernel, out_shape=shapes, in_specs=smem(len(scalars)) + vm...  27.5 us
    all_to_all x1, waiting for transfers between devices, program(): plane = lax.all_to_all(kept + swapped(sent, 'c'), PLANE, 0, 0, tiled=True)  21.7 us
    ppermute x6, starting transfers between devices, shifted(): lax.ppermute(array, axis, [(k, (k + by) % size) for k in range(size)])  16.8 us
    all_to_all x1, starting transfers between devices, everywhere(): lax.all_to_all(jnp.broadcast_to(array[None], (size, *array.shape)), axes,...  7.61 us
    all_to_all x1, starting transfers between devices, program(): pieces = lax.all_to_all(outgoing, RING, 0, 0, tiled=True)  7.5 us
    all_to_all x1, starting transfers between devices, program(): plane = lax.all_to_all(kept + swapped(sent, 'c'), PLANE, 0, 0, tiled=True)  7.48 us
  transfers between devices with their start and end apart: 17, of which 12 were waited for; matrix products, arithmetic and copies ran while one was open for 1% of the time, Pallas kernels for 12%

profile of v2, /device:TPU:2, one launch (start us, length us, event | category | flops | bytes accessed | tf_op | source)
XLA Modules:
  0.0 176.6 jit_solution(9900182682191038833)
XLA Ops:
  0.0 1.2 copy-done.2
  1.2 1.2 copy-done.3
  2.5 1.6 shard_map.37
  4.0 0.1 collective-permute-start
  4.1 2.4 %shard_map.39 = (f32[4,32,32,128]{3,2,1,0:T(8,128)S(1)}, f32[4,32,32,128]{3,2,1,0:T(8,128)}) custom-call(s32[1]{0:T(128)} %bitcast.core_ref, bf16[512,1024]{1,0:T(8,128)(2,1)S(1)} %copy-done.2, bf16[512,1024]{1,0:T(8,128)(2,1)S(1)} %copy-done.3), custom_call_target="tpu_custom_call" | custom-call | flops 1073741824 | bytes 6291456 | tf_op jit(solution)/shard_map/pallas_call | solution.py:184
  6.5 1.4 copy-done
  7.9 0.5 collective-permute-start.5
  8.4 0.2 collective-permute-done
  8.7 1.8 %add.14 = f32[16,288,128]{2,1,0:T(8,128)} add(f32[16,288,128]{2,1,0:T(8,128)S(1)} %get-tuple-element.15, f32[16,288,128]{2,1,0:T(8,128)S(1)} %collective-permute-done) | non-fusion elementwise | flops 589824 | bytes 7077888 | tf_op jit(solution)/shard_map/add | solution.py:229
  10.4 7.5 %all-to-all-start = ((f32[16,288,128]{2,1,0:T(8,128)}), f32[16,288,128]{2,1,0:T(8,128)S(1)}, u32[]{:S(2)}, u32[]{:S(2)}) async-start(f32[16,288,128]{2,1,0:T(8,128)} %add.14), calls=%async_computation | async-start | bytes 4718592 | tf_op jit(solution)/shard_map/all_to_all | solution.py:229
  17.9 0.0 collective-permute-done.5.came_ref
  17.9 1.6 copy-done.1
  19.5 2.9 %shard_map.40 = (f32[32,32,128]{2,1,0:T(8,128)S(1)}, f32[32,32,128]{2,1,0:T(8,128)}, f32[32,32,128]{2,1,0:T(8,128)}, f32[32,32,128]{2,1,0:T(8,128)}) custom-call(s32[1]{0:T(128)} %bitcast.7.at_ref, f32[4,32,32,128]{3,2,1,0:T(8,128)S(1)} %copy-done.1, f32[4,32,32,128]{3,2,1,0:T(8,128)} %collective-permute-done.5.came_ref), custom_call_target="tpu_custom_call" | custom-call | bytes 6291456 | tf_op jit(solution)/shard_map/pallas_call | solution.py:184
  22.4 3.3 %collective-permute-start.6 = (f32[32,32,128]{2,1,0:T(8,128)}, f32[32,32,128]{2,1,0:T(8,128)S(1)}, u32[]{:S(2)}, u32[]{:S(2)}) collective-permute-start(f32[32,32,128]{2,1,0:T(8,128)} %get-tuple-element.22), channel_id=1, source_target_pairs={{0,64},{64,128},{128,192},{192,0},{1,65},{65,129},{129,193},{193,1... | collective-permute-start | bytes 1572872 | tf_op jit(solution)/shard_map/ppermute | solution.py:208
  25.7 5.4 %collective-permute-start.7 = (f32[32,32,128]{2,1,0:T(8,128)}, f32[32,32,128]{2,1,0:T(8,128)}, u32[]{:S(2)}, u32[]{:S(2)}) collective-permute-start(f32[32,32,128]{2,1,0:T(8,128)} %get-tuple-element.23), channel_id=1, source_target_pairs={{0,128},{64,192},{128,0},{192,64},{1,129},{65,193},{129,1},{193,65... | collective-permute-start | bytes 1572872 | tf_op jit(solution)/shard_map/ppermute | solution.py:208
  31.1 2.7 %collective-permute-start.8 = (f32[32,32,128]{2,1,0:T(8,128)}, f32[32,32,128]{2,1,0:T(8,128)}, u32[]{:S(2)}, u32[]{:S(2)}) collective-permute-start(f32[32,32,128]{2,1,0:T(8,128)} %get-tuple-element.24), channel_id=1, source_target_pairs={{0,192},{64,0},{128,64},{192,128},{1,193},{65,1},{129,65},{193,129... | collective-permute-start | bytes 1572872 | tf_op jit(solution)/shard_map/ppermute | solution.py:208
  33.8 21.7 %all-to-all-done.pieces_ref = f32[16,288,128]{2,1,0:T(8,128)S(1)} async-done(((f32[16,288,128]{2,1,0:T(8,128)}), f32[16,288,128]{2,1,0:T(8,128)S(1)}, u32[]{:S(2)}, u32[]{:S(2)}) %all-to-all-start) | async-done | bytes 2359328 | tf_op jit(solution)/shard_map/all_to_all | solution.py:229
  55.5 0.1 shard_map.38
  55.6 2.0 %collective-permute-start.1 = (f32[144,128]{1,0:T(8,128)S(1)}, f32[144,128]{1,0:T(8,128)S(1)}, u32[]{:S(2)}, u32[]{:S(2)}) collective-permute-start(f32[144,128]{1,0:T(8,128)S(1)} %get-tuple-element.18), channel_id=1, source_target_pairs={{0,32},{32,0},{1,33},{33,1},{2,34},{34,2},{3,35},{35,3},{4,36},{36... | collective-permute-start | bytes 221192 | tf_op jit(solution)/shard_map/ppermute | solution.py:203
  57.6 20.8 %collective-permute-done.1 = f32[144,128]{1,0:T(8,128)S(1)} collective-permute-done((f32[144,128]{1,0:T(8,128)S(1)}, f32[144,128]{1,0:T(8,128)S(1)}, u32[]{:S(2)}, u32[]{:S(2)}) %collective-permute-start.1) | collective-permute-done | bytes 73760 | tf_op jit(solution)/shard_map/ppermute | solution.py:203
  78.4 0.7 collective-permute-start.2
  79.1 4.8 %collective-permute-start.3 = (f32[144,128]{1,0:T(8,128)S(1)}, f32[144,128]{1,0:T(8,128)S(1)}, u32[]{:S(2)}, u32[]{:S(2)}) collective-permute-start(f32[144,128]{1,0:T(8,128)S(1)} %add.15.refs_0_), channel_id=1, source_target_pairs={{0,128},{64,192},{128,0},{192,64},{1,129},{65,193},{129,1},{193,65... | collective-permute-start | bytes 221192 | tf_op jit(solution)/shard_map/ppermute | solution.py:208
  83.9 0.0 collective-permute-done.6.refs_5_
  83.9 0.0 collective-permute-done.8.refs_7_
  83.9 2.7 %collective-permute-done.2.refs_1_ = f32[144,128]{1,0:T(8,128)S(1)} collective-permute-done((f32[144,128]{1,0:T(8,128)S(1)}, f32[144,128]{1,0:T(8,128)S(1)}, u32[]{:S(2)}, u32[]{:S(2)}) %collective-permute-start.2) | collective-permute-done | bytes 73760 | tf_op jit(solution)/shard_map/ppermute | solution.py:208
  86.6 0.9 collective-permute-done.3.refs_2_
  87.5 2.5 %collective-permute-done.4.refs_3_ = f32[144,128]{1,0:T(8,128)S(1)} collective-permute-done((f32[144,128]{1,0:T(8,128)S(1)}, f32[144,128]{1,0:T(8,128)S(1)}, u32[]{:S(2)}, u32[]{:S(2)}) %collective-permute-start.4) | collective-permute-done | bytes 73760 | tf_op jit(solution)/shard_map/ppermute | solution.py:208
  90.0 3.0 %shard_map.41 = f32[32,176,128]{2,1,0:T(8,128)} custom-call(f32[144,128]{1,0:T(8,128)S(1)} %add.15.refs_0_, f32[144,128]{1,0:T(8,128)S(1)} %collective-permute-done.2.refs_1_, f32[144,128]{1,0:T(8,128)S(1)} %collective-permute-done.3.refs_2_, f32[144,128]{1,0:T(8,128)S(1)} %collective-permute-done.4.refs_3_, f32[32,32,128]{2,1,0:T(8,128)S(1)} %get-tuple-element.21.refs_4_, ...), custom_call_target="tpu_custom_call" | custom-call | bytes 5275648 | tf_op jit(solution)/shard_map/pallas_call | solution.py:184
  92.9 7.5 %all-to-all-start.1 = ((f32[32,176,128]{2,1,0:T(8,128)}), f32[32,176,128]{2,1,0:T(8,128)S(1)}, u32[]{:S(2)}, u32[]{:S(2)}) async-start(f32[32,176,128]{2,1,0:T(8,128)} %shard_map.41), calls=%async_computation.1 | async-start | bytes 5767168 | tf_op jit(solution)/shard_map/all_to_all | solution.py:240
  100.5 0.6 fusion.2
  102.4 34.2 %all-to-all-done.1.packed_ref = f32[32,176,128]{2,1,0:T(8,128)S(1)} async-done(((f32[32,176,128]{2,1,0:T(8,128)}), f32[32,176,128]{2,1,0:T(8,128)S(1)}, u32[]{:S(2)}, u32[]{:S(2)}) %all-to-all-start.1) | async-done | bytes 2883616 | tf_op jit(solution)/shard_map/all_to_all | solution.py:240
  136.6 0.9 broadcast_in_dim.23
  137.4 7.6 %all-to-all-start.2 = ((f32[32,32,128]{2,1,0:T(8,128)}), f32[32,32,128]{2,1,0:T(8,128)}, u32[]{:S(2)}, u32[]{:S(2)}) async-start(f32[32,32,128]{2,1,0:T(8,128)} %broadcast_in_dim.23), calls=%async_computation.2 | async-start | bytes 1048576 | tf_op jit(solution)/shard_map/all_to_all | solution.py:198
  145.1 16.1 %shard_map.42.mine_ref = f32[128,1024]{1,0:T(8,128)S(1)} custom-call(s32[1]{0:T(128)} %bitcast.3.start_ref, f32[1]{0:T(128)} %bitcast.6.damp_ref, f32[32,176,128]{2,1,0:T(8,128)S(1)} %all-to-all-done.1.packed_ref), custom_call_target="tpu_custom_call" | custom-call | flops 11274289152 | bytes 3407872 | tf_op jit(solution)/shard_map/pallas_call | solution.py:184
  161.2 0.1 collective-permute-start.9
  161.3 1.9 %collective-permute-done.9.other_ref = f32[128,1024]{1,0:T(8,128)S(1)} collective-permute-done((f32[128,1024]{1,0:T(8,128)S(1)}, f32[128,1024]{1,0:T(8,128)S(1)}, u32[]{:S(2)}, u32[]{:S(2)}) %collective-permute-start.9) | collective-permute-done | bytes 524320 | tf_op jit(solution)/shard_map/ppermute | solution.py:203
  163.2 0.0 all-to-all-done.2
  163.2 1.6 fusion
  164.8 1.5 collective-permute-start.10
  166.3 2.1 %collective-permute-start.11 = (f32[4,32,128]{2,1,0:T(8,128)S(1)}, f32[4,32,128]{2,1,0:T(8,128)S(1)}, u32[]{:S(2)}, u32[]{:S(2)}) collective-permute-start(f32[4,32,128]{2,1,0:T(8,128)S(1)} %bitcast.27), channel_id=1, source_target_pairs={{0,32},{32,0},{1,33},{33,1},{2,34},{34,2},{3,35},{35,3},{4,36},{36... | collective-permute-start | bytes 196616 | tf_op jit(solution)/shard_map/ppermute | solution.py:203
  168.4 0.0 collective-permute-start.12
  168.4 0.7 collective-permute-done.10.refs_1_
  169.1 1.7 collective-permute-done.11.refs_2_
  170.9 2.7 %collective-permute-done.12.refs_3_ = f32[4,32,128]{2,1,0:T(8,128)S(1)} collective-permute-done((f32[4,32,128]{2,1,0:T(8,128)S(1)}, f32[4,32,128]{2,1,0:T(8,128)S(1)}, u32[]{:S(2)}, u32[]{:S(2)}) %collective-permute-start.12) | collective-permute-done | bytes 65568 | tf_op jit(solution)/shard_map/ppermute | solution.py:203
  173.6 0.1 collective-permute-start.13
  173.7 0.1 pad_add_fusion.at_ref
  173.8 1.4 collective-permute-done.13.refs_4_
  175.2 1.4 shard_map.43
  (12 shorter events, 0.1 us)
Async XLA Ops:
  0.0 1.2 copy-start.2
  1.2 1.2 copy-start.3
  4.0 4.6 %collective-permute-start = (f32[16,288,128]{2,1,0:T(8,128)S(1)}, f32[16,288,128]{2,1,0:T(8,128)S(1)}, u32[]{:S(2)}, u32[]{:S(2)}) collective-permute-start(f32[16,288,128]{2,1,0:T(8,128)S(1)} %get-tuple-element.16), channel_id=1, source_target_pairs={{0,8},{8,0},{1,9},{9,1},{2,10},{10,2},{3,11},{11,3},{4,12},{12,4},... | collective-permute-start | bytes 7077896 | tf_op jit(solution)/shard_map/ppermute | solution.py:203
  6.5 1.4 copy-start
  7.9 10.0 %collective-permute-start.5 = (f32[4,32,32,128]{3,2,1,0:T(8,128)}, f32[4,32,32,128]{3,2,1,0:T(8,128)}, u32[]{:S(2)}, u32[]{:S(2)}) collective-permute-start(f32[4,32,32,128]{3,2,1,0:T(8,128)} %get-tuple-element.20), channel_id=1, source_target_pairs={{0,8},{8,0},{1,9},{9,1},{2,10},{10,2},{3,11},{11,3},{4,12},{12,4},... | collective-permute-start | bytes 6291464 | tf_op jit(solution)/shard_map/ppermute | solution.py:203
  10.4 45.0 %all-to-all-start = ((f32[16,288,128]{2,1,0:T(8,128)}), f32[16,288,128]{2,1,0:T(8,128)S(1)}, u32[]{:S(2)}, u32[]{:S(2)}) async-start(f32[16,288,128]{2,1,0:T(8,128)} %add.14), calls=%async_computation | async-start | bytes 4718592 | tf_op jit(solution)/shard_map/all_to_all | solution.py:229
  17.9 1.6 copy-start.1
  22.4 61.5 %collective-permute-start.6 = (f32[32,32,128]{2,1,0:T(8,128)}, f32[32,32,128]{2,1,0:T(8,128)S(1)}, u32[]{:S(2)}, u32[]{:S(2)}) collective-permute-start(f32[32,32,128]{2,1,0:T(8,128)} %get-tuple-element.22), channel_id=1, source_target_pairs={{0,64},{64,128},{128,192},{192,0},{1,65},{65,129},{129,193},{193,1... | collective-permute-start | bytes 1572872 | tf_op jit(solution)/shard_map/ppermute | solution.py:208
  25.7 58.2 %collective-permute-start.7 = (f32[32,32,128]{2,1,0:T(8,128)}, f32[32,32,128]{2,1,0:T(8,128)}, u32[]{:S(2)}, u32[]{:S(2)}) collective-permute-start(f32[32,32,128]{2,1,0:T(8,128)} %get-tuple-element.23), channel_id=1, source_target_pairs={{0,128},{64,192},{128,0},{192,64},{1,129},{65,193},{129,1},{193,65... | collective-permute-start | bytes 1572872 | tf_op jit(solution)/shard_map/ppermute | solution.py:208
  31.1 52.8 %collective-permute-start.8 = (f32[32,32,128]{2,1,0:T(8,128)}, f32[32,32,128]{2,1,0:T(8,128)}, u32[]{:S(2)}, u32[]{:S(2)}) collective-permute-start(f32[32,32,128]{2,1,0:T(8,128)} %get-tuple-element.24), channel_id=1, source_target_pairs={{0,192},{64,0},{128,64},{192,128},{1,193},{65,1},{129,65},{193,129... | collective-permute-start | bytes 1572872 | tf_op jit(solution)/shard_map/ppermute | solution.py:208
  55.6 22.8 %collective-permute-start.1 = (f32[144,128]{1,0:T(8,128)S(1)}, f32[144,128]{1,0:T(8,128)S(1)}, u32[]{:S(2)}, u32[]{:S(2)}) collective-permute-start(f32[144,128]{1,0:T(8,128)S(1)} %get-tuple-element.18), channel_id=1, source_target_pairs={{0,32},{32,0},{1,33},{33,1},{2,34},{34,2},{3,35},{35,3},{4,36},{36... | collective-permute-start | bytes 221192 | tf_op jit(solution)/shard_map/ppermute | solution.py:203
  78.4 8.1 %collective-permute-start.2 = (f32[144,128]{1,0:T(8,128)S(1)}, f32[144,128]{1,0:T(8,128)S(1)}, u32[]{:S(2)}, u32[]{:S(2)}) collective-permute-start(f32[144,128]{1,0:T(8,128)S(1)} %add.15.refs_0_), channel_id=1, source_target_pairs={{0,64},{64,128},{128,192},{192,0},{1,65},{65,129},{129,193},{193,1... | collective-permute-start | bytes 221192 | tf_op jit(solution)/shard_map/ppermute | solution.py:208
  79.1 8.4 %collective-permute-start.3 = (f32[144,128]{1,0:T(8,128)S(1)}, f32[144,128]{1,0:T(8,128)S(1)}, u32[]{:S(2)}, u32[]{:S(2)}) collective-permute-start(f32[144,128]{1,0:T(8,128)S(1)} %add.15.refs_0_), channel_id=1, source_target_pairs={{0,128},{64,192},{128,0},{192,64},{1,129},{65,193},{129,1},{193,65... | collective-permute-start | bytes 221192 | tf_op jit(solution)/shard_map/ppermute | solution.py:208
  83.9 6.0 %collective-permute-start.4 = (f32[144,128]{1,0:T(8,128)S(1)}, f32[144,128]{1,0:T(8,128)S(1)}, u32[]{:S(2)}, u32[]{:S(2)}) collective-permute-start(f32[144,128]{1,0:T(8,128)S(1)} %add.15.refs_0_), channel_id=1, source_target_pairs={{0,192},{64,0},{128,64},{192,128},{1,193},{65,1},{129,65},{193,129... | collective-permute-start | bytes 221192 | tf_op jit(solution)/shard_map/ppermute | solution.py:208
  92.9 7.5 %copy-start.4 = (f32[2]{0:T(128)S(1)}, f32[2]{0:T(128)}, u32[]{:S(2)}) copy-start(f32[2]{0:T(128)} %param.5) | copy-start | bytes 28
  92.9 43.6 %all-to-all-start.1 = ((f32[32,176,128]{2,1,0:T(8,128)}), f32[32,176,128]{2,1,0:T(8,128)S(1)}, u32[]{:S(2)}, u32[]{:S(2)}) async-start(f32[32,176,128]{2,1,0:T(8,128)} %shard_map.41), calls=%async_computation.1 | async-start | bytes 5767168 | tf_op jit(solution)/shard_map/all_to_all | solution.py:240
  137.4 25.7 %all-to-all-start.2 = ((f32[32,32,128]{2,1,0:T(8,128)}), f32[32,32,128]{2,1,0:T(8,128)}, u32[]{:S(2)}, u32[]{:S(2)}) async-start(f32[32,32,128]{2,1,0:T(8,128)} %broadcast_in_dim.23), calls=%async_computation.2 | async-start | bytes 1048576 | tf_op jit(solution)/shard_map/all_to_all | solution.py:198
  161.2 2.0 %collective-permute-start.9 = (f32[128,1024]{1,0:T(8,128)S(1)}, f32[128,1024]{1,0:T(8,128)S(1)}, u32[]{:S(2)}, u32[]{:S(2)}) collective-permute-start(f32[128,1024]{1,0:T(8,128)S(1)} %shard_map.42.mine_ref), channel_id=1, source_target_pairs={{0,8},{8,0},{1,9},{9,1},{2,10},{10,2},{3,11},{11,3},{4,12},{12,4},... | collective-permute-start | bytes 1572872 | tf_op jit(solution)/shard_map/ppermute | solution.py:203
  164.8 4.4 %collective-permute-start.10 = (f32[4,32,128]{2,1,0:T(8,128)S(1)}, f32[4,32,128]{2,1,0:T(8,128)S(1)}, u32[]{:S(2)}, u32[]{:S(2)}) collective-permute-start(f32[4,32,128]{2,1,0:T(8,128)S(1)} %bitcast.26), channel_id=1, source_target_pairs={{0,16},{16,0},{1,17},{17,1},{2,18},{18,2},{3,19},{19,3},{4,20},{20... | collective-permute-start | bytes 196616 | tf_op jit(solution)/shard_map/ppermute | solution.py:203
  166.3 4.6 %collective-permute-start.11 = (f32[4,32,128]{2,1,0:T(8,128)S(1)}, f32[4,32,128]{2,1,0:T(8,128)S(1)}, u32[]{:S(2)}, u32[]{:S(2)}) collective-permute-start(f32[4,32,128]{2,1,0:T(8,128)S(1)} %bitcast.27), channel_id=1, source_target_pairs={{0,32},{32,0},{1,33},{33,1},{2,34},{34,2},{3,35},{35,3},{4,36},{36... | collective-permute-start | bytes 196616 | tf_op jit(solution)/shard_map/ppermute | solution.py:203
  168.4 5.2 %collective-permute-start.12 = (f32[4,32,128]{2,1,0:T(8,128)S(1)}, f32[4,32,128]{2,1,0:T(8,128)S(1)}, u32[]{:S(2)}, u32[]{:S(2)}) collective-permute-start(f32[4,32,128]{2,1,0:T(8,128)S(1)} %bitcast.28), channel_id=1, source_target_pairs={{0,48},{16,32},{32,16},{48,0},{1,49},{17,33},{33,17},{49,1},{2,50}... | collective-permute-start | bytes 196616 | tf_op jit(solution)/shard_map/ppermute | solution.py:203
  173.6 1.6 collective-permute-start.13

commit v3 on v2

v3 whole, which is shorter than its diff:
```python
import functools
import math

import jax
import jax.numpy as jnp
from jax import lax
from jax.experimental import pallas as pl
from jax.experimental.pallas import tpu as pltpu
from jax.sharding import Mesh
from jax.sharding import PartitionSpec as P

INTERPRET = False
STEPS = 14
AXES = ("zh", "zl", "yl", "c", "x", "yh")
DP = ("zh", "zl", "yl", "c")
GRP = ("x", "yh")
Y = ("yl", "yh")
B = 128
F32 = jnp.float32
BF16 = jnp.bfloat16


def sub_segments(start, size, piece):
    done = 0
    while done < size:
        q, r = divmod(start + done, piece)
        n = min(piece - r, size - done)
        yield q, r, done, n
        done += n


def dot(a, b):
    return jnp.dot(a, b, preferred_element_type=F32)


def gram_kernel(nb, colour, core_ref, acts_ref, grads_ref, keep_ref, send_ref, t_ref):
    core = core_ref[0]
    part = nb * (nb + 1) // 2 * B // 2
    piece = part // 16
    strip = nb * B // 4
    rows = (keep_ref.shape[2] - piece) // 4
    acts = acts_ref[...]
    grads = grads_ref[...]
    t_ref[0] = acts.T
    t_ref[1] = grads.T
    for which, out in ((0, send_ref), (1, keep_ref)):
        slot = core if which else 1 - core
        right = jnp.where(slot == 0, acts, grads)
        for jj in range(nb // 2):
            spans = []
            for j in (2 * jj, 2 * jj + 1):
                base = j * (j + 1) // 2 * B
                lo, hi = max(base, colour * part), min(base + (j + 1) * B, (colour + 1) * part)
                if lo < hi:
                    spans.append((j, lo, hi, lo - base, hi - base))
            if not spans:
                continue
            low, high = min(s[3] for s in spans), max(s[4] for s in spans)
            res = dot(t_ref[slot, low:high, :], right[:, jj * 2 * B : (jj + 1) * 2 * B])
            for j, lo, hi, first, _ in spans:
                lane = (j - 2 * jj) * B
                for q, r, at, n in sub_segments(lo - colour * part, hi - lo, piece):
                    at = first - low + at
                    out[q // 4, q % 4, r : r + n, :] = res[at : at + n, lane : lane + B]
        begin = pl.multiple_of(slot * 2 * strip + colour * strip, strip)
        left = t_ref[0, pl.ds(begin, strip), :]
        for x in range(nb // 2):
            res = dot(left, grads[:, x * 2 * B : (x + 1) * 2 * B])
            for s in range(strip // rows):
                zh, yl = divmod(s, 2)
                for yh in range(2):
                    y = yh * 2 + yl
                    first, second = (y, x) if colour else (x, y)
                    at = piece + zh * rows
                    out[first, second, at : at + rows, :] = res[s * rows : s * rows + rows, yh * B : yh * B + B]


def turned_kernel(count, at_ref, *refs):
    ins, outs = refs[:count], refs[count:]
    for k, out in enumerate(outs):
        z = lax.rem(at_ref[0] + k, len(outs))
        total = ins[0][z]
        for ref in ins[1:]:
            total = total + ref[z]
        out[...] = total


def halves_kernel(at_ref, *refs):
    count = (len(refs) - 2) // 2
    sums = []
    for refs_of in (refs[:count], refs[count : 2 * count]):
        total = refs_of[0][...]
        for ref in refs_of[1:]:
            total = total + ref[...]
        sums.append(total)
    keep_ref, send_ref = refs[-2:]
    low = at_ref[0] == 0
    keep_ref[...] = jnp.where(low, sums[0], sums[1])
    send_ref[...] = jnp.where(low, sums[1], sums[0])


def ring_kernel(piece, at_ref, keep_ref, came_ref, *refs):
    outs, sum_ref = refs[:-1], refs[-1]
    sum_ref[...] = keep_ref[...] + came_ref[...]
    rows = outs[0].shape[0] - piece
    for k, out in enumerate(outs):
        z = lax.rem(at_ref[0] + k, len(outs))
        out[:piece, :] = sum_ref[:piece, :]
        out[piece:, :] = sum_ref[pl.ds(pl.multiple_of(piece + z * rows, 8), rows), :]


def total_kernel(scale, *refs):
    factor_ref, cross_ref = refs[-2:]
    total = refs[0][...]
    for ref in refs[1:-2]:
        total = total + ref[...]
    piece = factor_ref.shape[0]
    factor_ref[...] = total[:piece]
    cross_ref[...] = total[piece:] * scale


def colours_kernel(at_ref, mine_ref, other_ref, *outs):
    mine, other = mine_ref[...], other_ref[...]
    low = at_ref[0] == 0
    outs[0][...] = jnp.where(low, mine, other)
    outs[1][...] = jnp.where(low, other, mine)


def joined_kernel(*refs):
    outs = refs[-3:]
    count = (len(refs) - 4) // 2
    for k in range(count):
        outs[0][k] = refs[k][...]
        outs[1][k] = refs[count + k][...]
    cross = refs[2 * count][...]
    for q in range(outs[2].shape[0]):
        outs[2][q] = cross


def last_kernel(at_ref, mine_ref, other_ref, *refs):
    out_ref, z_ref = refs[-2:]
    core, zl, yl = at_ref[0], at_ref[1], at_ref[2]
    own, came = refs[:4], refs[4]
    for d in range(4):
        dz, dy = divmod(d, 2)
        pz, py = jnp.bitwise_xor(zl, dz), jnp.bitwise_xor(yl, dy)
        for zh in range(z_ref.shape[2]):
            z_ref[core, pz, zh, py] = own[d][zh]
            z_ref[1 - core, pz, zh, py] = came[d, zh]
    rows = out_ref.shape[0]
    first = pl.multiple_of(yl * 2 * rows + core * rows, 8)
    mine = mine_ref[pl.ds(first, rows), :]
    other = other_ref[pl.ds(first, rows), :]
    hi, lo = split(jnp.where(core == 0, mine, other))
    zhi, zlo = split(z_ref[...].reshape(-1, B))
    out_ref[...] = (dot(hi, zlo) + dot(lo, zhi)) + dot(hi, zhi)


def split(v):
    hi = v.astype(BF16)
    return hi, (v - hi.astype(F32)).astype(BF16)


def inverse_kernel(nb, scale, at_ref, damp_ref, *refs):
    out_ref, p_ref, m_ref, hi_ref, lo_ref, s_ref, y_ref = refs[-7:]
    width = nb * B
    damp = damp_ref[0]
    for colour in range(2):
        first, second = at_ref[1 + colour], at_ref[2 - colour]
        for k in range(4):
            for i in range(4):
                p = colour * 16 + lax.rem(first + 4 - k, 4) * 4 + lax.rem(second + 4 - i, 4)
                p_ref[p] = refs[colour * 4 + k][i]
    eye = (lax.broadcasted_iota(jnp.int32, (B, B), 0) == lax.broadcasted_iota(jnp.int32, (B, B), 1)).astype(F32)
    for j in range(nb):
        base = j * (j + 1) // 2 * B
        for i in range(j + 1):
            parts = []
            for q, r, _, n in sub_segments(base + i * B, B, p_ref.shape[1]):
                parts.append(p_ref[q, r : r + n, :])
            block = jnp.concatenate(parts, axis=0) * scale
            if i == j:
                block = block + damp * eye
            m_ref[i * B : (i + 1) * B, j * B : (j + 1) * B] = block
            if i != j:
                m_ref[j * B : (j + 1) * B, i * B : (i + 1) * B] = block.T
    total = jnp.zeros((8, width), F32)
    for i in range(nb):
        total = total + jnp.abs(m_ref[i * B : (i + 1) * B, :]).reshape(B // 8, 8, width).sum(axis=0)
    alpha = 1.0 / jnp.max(jnp.sum(total, axis=0, keepdims=True), axis=1, keepdims=True)
    for i in range(nb):
        rows = lax.broadcasted_iota(jnp.int32, (B, width), 0) + i * B
        ones = (rows == lax.broadcasted_iota(jnp.int32, (B, width), 1)).astype(F32)
        hi, lo = split(ones - alpha * m_ref[i * B : (i + 1) * B, :])
        hi_ref[i * B : (i + 1) * B, :] = hi
        lo_ref[i * B : (i + 1) * B, :] = lo
    start = pl.multiple_of(at_ref[0], B)
    rows = lax.broadcasted_iota(jnp.int32, (B, width), 0) + start
    ones = (rows == lax.broadcasted_iota(jnp.int32, (B, width), 1)).astype(F32)
    s_ref[...] = ones
    y_ref[...] = 2.0 * ones - alpha * m_ref[pl.ds(start, B), :]

    def step(_, carry):
        hi, lo = split(y_ref[...])
        both = jnp.concatenate([hi, lo], axis=0)
        first = dot(both, hi_ref[...])
        y_ref[...] = (dot(hi, lo_ref[...]) + first[B:]) + first[:B] + s_ref[...]
        return carry

    lax.fori_loop(0, STEPS, step, 0)
    out_ref[...] = alpha * y_ref[...]


def vmem(n):
    return [pl.BlockSpec(memory_space=pltpu.VMEM)] * n


def smem(n=1):
    return [pl.BlockSpec(memory_space=pltpu.SMEM)] * n


def call(kernel, scalars, arrays, outs, scratch=(), flops=0, limit=32):
    moved = sum(4 * math.prod(o) for o in outs) + sum(a.size * a.dtype.itemsize for a in arrays)
    shapes = [jax.ShapeDtypeStruct(o, F32) for o in outs]
    return pl.pallas_call(
        kernel,
        out_shape=shapes,
        in_specs=smem(len(scalars)) + vmem(len(arrays)),
        out_specs=vmem(len(outs)),
        scratch_shapes=list(scratch),
        cost_estimate=pl.CostEstimate(flops=flops, bytes_accessed=moved, transcendentals=0),
        compiler_params=pltpu.CompilerParams(vmem_limit_bytes=limit << 20),
        interpret=INTERPRET,
    )(*[jnp.atleast_1d(s) for s in scalars], *arrays)


def swapped(array, axes):
    pairs = [(k, lax.axis_size(axes) - 1 - k) for k in range(lax.axis_size(axes))]
    return lax.ppermute(array, axes, pairs)


def shifted(array, axis, by):
    size = lax.axis_size(axis)
    spots = [k % 2 * 2 + k // 2 for k in range(4)] if axis == Y else list(range(size))
    return lax.ppermute(array, axis, [(spots[k], spots[(k + by) % size]) for k in range(size)])


def program(acts, grads, damping):
    tokens, width = acts.shape
    nb = width // B
    ng, nz = lax.axis_size(GRP), lax.axis_size("zh")
    scale = 1.0 / (tokens * lax.axis_size(AXES))
    core, zh, zl, yl, x, yh = (lax.axis_index(a) for a in ("c", "zh", "zl", "yl", "x", "yh"))
    y = yh * 2 + yl
    rings = (("x", x), (Y, y))
    piece = nb * (nb + 1) // 2 * B // 32
    rows = width // lax.axis_size(DP)
    chunk = (piece + nz * rows, B)

    near = []
    for colour in range(2):
        kept, sent = call(
            functools.partial(gram_kernel, nb, colour), [core], [acts, grads],
            [(4, 4, *chunk)] * 2, [pltpu.VMEM((2, width, tokens), BF16)], flops=2 * tokens * width * width,
        )
        near.append([kept, swapped(sent, "c")])
    for depth in range(2):
        far = []
        for colour in range(2):
            ring, at = rings[depth ^ colour]
            shape = chunk if depth else (4, *chunk)
            turned = call(
                functools.partial(turned_kernel, len(near[colour])), [at], near[colour],
                [shape] * 4,
            )
            far.append([turned[0]] + [shifted(turned[k], ring, k) for k in (2, 1, 3)])
        near = far
    keep, send = call(halves_kernel, [zl], near[0] + near[1], [chunk] * 2)
    turned = call(
        functools.partial(ring_kernel, piece), [zh], [keep, swapped(send, "zl")],
        [(piece + rows, B)] * nz, [pltpu.VMEM(chunk, F32)],
    )
    around = [turned[0]] + [shifted(turned[k], "zh", k) for k in (2, 1, 3)]
    mine, cross = call(functools.partial(total_kernel, scale), [], around, [(piece, B), (rows, B)])
    stretches = call(colours_kernel, [zl], [mine, swapped(mine, "zl")], [(piece, B)] * 2)
    parts = []
    for colour in range(2):
        ring = rings[1 - colour][0]
        parts += [stretches[colour]] + [shifted(stretches[colour], ring, k) for k in (1, 2, 3)]
    spread = ("zh", "x", "yh")
    *joined, crosses = call(
        joined_kernel, [], [*parts, cross],
        [(4, piece, B), (4, piece, B), (lax.axis_size(spread), rows, B)],
    )
    pieces = []
    for colour in range(2):
        ring = rings[colour][0]
        moved = {k: shifted(joined[colour], ring, k) for k in (2, 1, 3)}
        pieces += [joined[colour]] + [moved[k] for k in (1, 2, 3)]
    cross_rows = lax.all_to_all(crosses, spread, 0, 0, tiled=True).reshape(nz, ng, rows, B)
    height = zh * lax.axis_size("zl") + zl
    start = jnp.where(core == 0, height * B, lax.axis_index(GRP) * B).astype(jnp.int32)
    damp = jnp.where(core == 0, damping[0], damping[1])
    (mine,) = call(
        functools.partial(inverse_kernel, nb, scale), [jnp.stack([start, x, y]), damp], pieces,
        [(B, width)],
        [
            pltpu.VMEM((32, piece, B), F32),
            pltpu.VMEM((width, width), F32),
            pltpu.VMEM((width, width), BF16),
            pltpu.VMEM((width, width), BF16),
            pltpu.VMEM((B, width), F32),
            pltpu.VMEM((B, width), F32),
        ],
        flops=2 * 3 * STEPS * B * width * width,
    )
    other = swapped(mine, "c")
    right = jnp.where(core == 0, other, mine).reshape(B, ng, B)
    z = jnp.einsum(
        "zgrk,cgk->zrc", cross_rows, right, precision=lax.Precision.HIGHEST, preferred_element_type=F32
    )
    slabs = [z, swapped(z, "yl"), swapped(z, "zl"), swapped(z, ("zl", "yl"))]
    came = swapped(jnp.stack(slabs), "c")
    (out,) = call(
        last_kernel, [jnp.stack([core, zl, yl])], [mine, other, *slabs, came], [(rows, B)],
        [pltpu.VMEM((2, 2, nz, 2, rows, B), F32)],
    )
    return out


def solution(mesh):
    torus = Mesh(mesh.devices.reshape(4, 2, 2, 2, 4, 2), AXES)
    return jax.shard_map(
        program,
        mesh=torus,
        in_specs=(P(AXES, None), P(AXES, None), P()),
        out_specs=P(DP, GRP),
        check_vma=False,
    )
```

time: 178 us -> 165 us (0.927)
  waiting for transfers between devices: 91.4 us -> 53.6 us
  starting transfers between devices: 45.8 us -> 70.6 us
  Pallas kernels: 27.5 us -> 31.6 us
    all_to_all x3 -> x1, waiting for transfers between devices: 55.9 us -> 0.01 us  [program(): lax.all_to_all(crosses, spread, 0, 0, tiled=True).reshape(nz, ng, rows, B)]
    ppermute x6 -> x27, waiting for transfers between devices: 6.03 us -> 40.4 us  [shifted(): lax.ppermute(array, axis, [(spots[k], spots[(k + by) % size]) for k in ra...]
    ppermute x6 -> x27, starting transfers between devices: 16.8 us -> 51.1 us  [shifted(): lax.ppermute(array, axis, [(spots[k], spots[(k + by) % size]) for k in ra...]
    ppermute x8 -> x9, waiting for transfers between devices: 29.5 us -> 13.2 us  [swapped(): return lax.ppermute(array, axes, pairs)]
    all_to_all x3 -> x1, starting transfers between devices: 22.6 us -> 11 us  [program(): lax.all_to_all(crosses, spread, 0, 0, tiled=True).reshape(nz, ng, rows, B)]
    pallas_call x7 -> x13, Pallas kernels: 27.5 us -> 31.6 us  [call(): pl.pallas_call(kernel, out_shape=shapes, in_specs=smem(len(scalars)) + vm...]
    ppermute x8 -> x9, starting transfers between devices: 6.38 us -> 8.54 us  [swapped(): return lax.ppermute(array, axes, pairs)]
    add x2 -> x0, other arithmetic: 1.8 us -> none  [the longest x1 1.79 us: program(): plane = lax.all_to_all(kept + swapped(sent, 'c'), PLANE, 0, 0, tiled=True)]
  transfers between devices with their start and end apart: 17 -> 37, of which waited for: 12 -> 18; matrix products, arithmetic and copies ran while one was open for 1% -> 0% of each run, Pallas kernels for 12% -> 16%
where the time goes in v3:
time: 165 us; the launch traced here: 164 us
  starting transfers between devices  70.6 us (43%)
  waiting for transfers between devices  53.6 us (32%)
  Pallas kernels  31.6 us (19%)
  local copies, waits for them, and re-layouts  6.03 us (4%)
    ppermute x27, starting transfers between devices, shifted(): lax.ppermute(array, axis, [(spots[k], spots[(k + by) % size]) for k in ra...  51.1 us
    ppermute x27, waiting for transfers between devices, shifted(): lax.ppermute(array, axis, [(spots[k], spots[(k + by) % size]) for k in ra...  40.4 us
    pallas_call x13, Pallas kernels, call(): pl.pallas_call(kernel, out_shape=shapes, in_specs=smem(len(scalars)) + vm...  31.6 us
    ppermute x9, waiting for transfers between devices, swapped(): return lax.ppermute(array, axes, pairs)  13.2 us
    all_to_all x1, starting transfers between devices, program(): lax.all_to_all(crosses, spread, 0, 0, tiled=True).reshape(nz, ng, rows, B)  11 us
    ppermute x9, starting transfers between devices, swapped(): return lax.ppermute(array, axes, pairs)  8.54 us
    unnamed x10, local copies, waits for them, and re-layouts  5.43 us
  transfers between devices with their start and end apart: 37, of which 18 were waited for; matrix products, arithmetic and copies ran while one was open for 0% of the time, Pallas kernels for 16%

profile of v3, /device:TPU:2, one launch (start us, length us, event | category | flops | bytes accessed | tf_op | source)
XLA Modules:
  0.0 164.0 jit_solution(1516355789858888884)
XLA Ops:
  0.0 1.2 copy-done.2
  1.2 1.2 copy-done.3
  2.5 3.0 %shard_map.40 = (f32[4,4,272,128]{3,2,1,0:T(8,128)S(1)}, f32[4,4,272,128]{3,2,1,0:T(8,128)}) custom-call(s32[1]{0:T(128)} %bitcast.core_ref, bf16[512,1024]{1,0:T(8,128)(2,1)S(1)} %copy-done.2, bf16[512,1024]{1,0:T(8,128)(2,1)S(1)} %copy-done.3), custom_call_target="tpu_custom_call" | custom-call | flops 1073741824 | bytes 6553600 | tf_op jit(solution)/shard_map/pallas_call | solution.py:225
  5.4 1.4 copy-done
  6.8 3.0 %shard_map.37 = (f32[4,4,272,128]{3,2,1,0:T(8,128)S(1)}, f32[4,4,272,128]{3,2,1,0:T(8,128)}) custom-call(s32[1]{0:T(128)} %bitcast.core_ref, bf16[512,1024]{1,0:T(8,128)(2,1)S(1)} %copy-done.2, bf16[512,1024]{1,0:T(8,128)(2,1)S(1)} %copy-done.3), custom_call_target="tpu_custom_call" | custom-call | flops 1073741824 | bytes 6553600 | tf_op jit(solution)/shard_map/pallas_call | solution.py:225
  10.3 1.2 collective-permute-done.7.refs_1_
  11.5 1.6 copy-done.1
  13.1 3.1 %shard_map.41 = (f32[4,272,128]{2,1,0:T(8,128)S(1)}, f32[4,272,128]{2,1,0:T(8,128)}, f32[4,272,128]{2,1,0:T(8,128)}, f32[4,272,128]{2,1,0:T(8,128)}) custom-call(s32[1]{0:T(128)} %bitcast.5.at_ref, f32[4,4,272,128]{3,2,1,0:T(8,128)S(1)} %copy-done.1, f32[4,4,272,128]{3,2,1,0:T(8,128)} %collective-permute-done.7.refs_1_), custom_call_target="tpu_custom_call" | custom-call | bytes 6684672 | tf_op jit(solution)/shard_map/pallas_call | solution.py:225
  16.2 3.0 %collective-permute-start.10 = (f32[4,272,128]{2,1,0:T(8,128)}, f32[4,272,128]{2,1,0:T(8,128)S(1)}, u32[]{:S(2)}, u32[]{:S(2)}) collective-permute-start(f32[4,272,128]{2,1,0:T(8,128)} %get-tuple-element.53), channel_id=1, source_target_pairs={{0,17},{16,0},{1,16},{17,1},{2,19},{18,2},{3,18},{19,3},{4,21},{20... | collective-permute-start | bytes 1671176 | tf_op jit(solution)/shard_map/ppermute | solution.py:245
  19.8 1.0 collective-permute-start.9
  20.8 1.9 %shard_map.38 = (f32[4,272,128]{2,1,0:T(8,128)S(1)}, f32[4,272,128]{2,1,0:T(8,128)S(1)}, f32[4,272,128]{2,1,0:T(8,128)S(1)}, f32[4,272,128]{2,1,0:T(8,128)S(1)}) custom-call(s32[1]{0:T(128)} %bitcast.4.at_ref, f32[4,4,272,128]{3,2,1,0:T(8,128)S(1)} %get-tuple-element.38.refs_0_, f32[4,4,272,128]{3,2,1,0:T(8,128)} %collective-permute-done.refs_1_), custom_call_target="tpu_custom_call" | custom-call | bytes 6684672 | tf_op jit(solution)/shard_map/pallas_call | solution.py:225
  22.6 2.2 %collective-permute-start.1 = (f32[4,272,128]{2,1,0:T(8,128)S(1)}, f32[4,272,128]{2,1,0:T(8,128)S(1)}, u32[]{:S(2)}, u32[]{:S(2)}) collective-permute-start(f32[4,272,128]{2,1,0:T(8,128)S(1)} %get-tuple-element.41), channel_id=1, source_target_pairs={{0,4},{2,6},{4,0},{6,2},{1,5},{3,7},{5,1},{7,3},{8,12},{10,14},{12... | collective-permute-start | bytes 1671176 | tf_op jit(solution)/shard_map/ppermute | solution.py:245
  24.8 18.8 %collective-permute-done.10.refs_3_ = f32[4,272,128]{2,1,0:T(8,128)S(1)} collective-permute-done((f32[4,272,128]{2,1,0:T(8,128)}, f32[4,272,128]{2,1,0:T(8,128)S(1)}, u32[]{:S(2)}, u32[]{:S(2)}) %collective-permute-start.10) | collective-permute-done | bytes 557088 | tf_op jit(solution)/shard_map/ppermute | solution.py:245
  43.6 3.7 %collective-permute-done.9.refs_2_ = f32[4,272,128]{2,1,0:T(8,128)} collective-permute-done((f32[4,272,128]{2,1,0:T(8,128)}, f32[4,272,128]{2,1,0:T(8,128)}, u32[]{:S(2)}, u32[]{:S(2)}) %collective-permute-start.9) | collective-permute-done | bytes 557088 | tf_op jit(solution)/shard_map/ppermute | solution.py:245
  47.3 1.3 shard_map.42
  48.6 2.2 %collective-permute-start.11 = (f32[272,128]{1,0:T(8,128)S(1)}, f32[272,128]{1,0:T(8,128)S(1)}, u32[]{:S(2)}, u32[]{:S(2)}) collective-permute-start(f32[272,128]{1,0:T(8,128)S(1)} %get-tuple-element.55), channel_id=1, source_target_pairs={{0,4},{2,6},{4,0},{6,2},{1,5},{3,7},{5,1},{7,3},{8,12},{10,14},{12... | collective-permute-start | bytes 417800 | tf_op jit(solution)/shard_map/ppermute | solution.py:245
  50.9 2.0 %collective-permute-start.13 = (f32[272,128]{1,0:T(8,128)S(1)}, f32[272,128]{1,0:T(8,128)S(1)}, u32[]{:S(2)}, u32[]{:S(2)}) collective-permute-start(f32[272,128]{1,0:T(8,128)S(1)} %get-tuple-element.57), channel_id=1, source_target_pairs={{0,6},{2,0},{4,2},{6,4},{1,7},{3,1},{5,3},{7,5},{8,14},{10,8},{12,... | collective-permute-start | bytes 417800 | tf_op jit(solution)/shard_map/ppermute | solution.py:245
  52.9 7.6 %collective-permute-done.3.refs_3_ = f32[4,272,128]{2,1,0:T(8,128)S(1)} collective-permute-done((f32[4,272,128]{2,1,0:T(8,128)S(1)}, f32[4,272,128]{2,1,0:T(8,128)S(1)}, u32[]{:S(2)}, u32[]{:S(2)}) %collective-permute-start.3) | collective-permute-done | bytes 557088 | tf_op jit(solution)/shard_map/ppermute | solution.py:245
  60.9 4.7 %collective-permute-start.5 = (f32[272,128]{1,0:T(8,128)S(1)}, f32[272,128]{1,0:T(8,128)S(1)}, u32[]{:S(2)}, u32[]{:S(2)}) collective-permute-start(f32[272,128]{1,0:T(8,128)S(1)} %get-tuple-element.46), channel_id=1, source_target_pairs={{0,16},{16,1},{1,17},{17,0},{2,18},{18,3},{3,19},{19,2},{4,20},{20... | collective-permute-start | bytes 417800 | tf_op jit(solution)/shard_map/ppermute | solution.py:245
  65.6 0.9 collective-permute-start.6
  66.5 1.0 collective-permute-done.4.refs_1_
  67.5 1.4 collective-permute-done.5.refs_2_
  68.9 1.7 %collective-permute-done.6.refs_3_ = f32[272,128]{1,0:T(8,128)S(1)} collective-permute-done((f32[272,128]{1,0:T(8,128)S(1)}, f32[272,128]{1,0:T(8,128)S(1)}, u32[]{:S(2)}, u32[]{:S(2)}) %collective-permute-start.6) | collective-permute-done | bytes 139296 | tf_op jit(solution)/shard_map/ppermute | solution.py:245
  70.7 2.0 %collective-permute-start.14 = (f32[272,128]{1,0:T(8,128)S(1)}, f32[272,128]{1,0:T(8,128)S(1)}, u32[]{:S(2)}, u32[]{:S(2)}) collective-permute-start(f32[272,128]{1,0:T(8,128)S(1)} %get-tuple-element.59), channel_id=1, source_target_pairs={{0,32},{32,0},{1,33},{33,1},{2,34},{34,2},{3,35},{35,3},{4,36},{36... | collective-permute-start | bytes 417800 | tf_op jit(solution)/shard_map/ppermute | solution.py:239
  72.7 3.1 %collective-permute-done.14.came_ref = f32[272,128]{1,0:T(8,128)S(1)} collective-permute-done((f32[272,128]{1,0:T(8,128)S(1)}, f32[272,128]{1,0:T(8,128)S(1)}, u32[]{:S(2)}, u32[]{:S(2)}) %collective-permute-start.14) | collective-permute-done | bytes 139296 | tf_op jit(solution)/shard_map/ppermute | solution.py:239
  75.9 7.9 %collective-permute-start.15 = (f32[176,128]{1,0:T(8,128)S(1)}, f32[176,128]{1,0:T(8,128)S(1)}, u32[]{:S(2)}, u32[]{:S(2)}) collective-permute-start(f32[176,128]{1,0:T(8,128)S(1)} %get-tuple-element.61), channel_id=1, source_target_pairs={{0,128},{64,192},{128,0},{192,64},{1,129},{65,193},{129,1},{193,65... | collective-permute-start | bytes 270344 | tf_op jit(solution)/shard_map/ppermute | solution.py:245
  83.8 2.4 %collective-permute-start.16 = (f32[176,128]{1,0:T(8,128)S(1)}, f32[176,128]{1,0:T(8,128)S(1)}, u32[]{:S(2)}, u32[]{:S(2)}) collective-permute-start(f32[176,128]{1,0:T(8,128)S(1)} %get-tuple-element.62), channel_id=1, source_target_pairs={{0,64},{64,128},{128,192},{192,0},{1,65},{65,129},{129,193},{193,1... | collective-permute-start | bytes 270344 | tf_op jit(solution)/shard_map/ppermute | solution.py:245
  86.2 1.7 %collective-permute-start.17 = (f32[176,128]{1,0:T(8,128)S(1)}, f32[176,128]{1,0:T(8,128)S(1)}, u32[]{:S(2)}, u32[]{:S(2)}) collective-permute-start(f32[176,128]{1,0:T(8,128)S(1)} %get-tuple-element.63), channel_id=1, source_target_pairs={{0,192},{64,0},{128,64},{192,128},{1,193},{65,1},{129,65},{193,129... | collective-permute-start | bytes 270344 | tf_op jit(solution)/shard_map/ppermute | solution.py:245
  87.9 3.5 %collective-permute-done.16.refs_2_ = f32[176,128]{1,0:T(8,128)S(1)} collective-permute-done((f32[176,128]{1,0:T(8,128)S(1)}, f32[176,128]{1,0:T(8,128)S(1)}, u32[]{:S(2)}, u32[]{:S(2)}) %collective-permute-start.16) | collective-permute-done | bytes 90144 | tf_op jit(solution)/shard_map/ppermute | solution.py:245
  91.7 2.2 %collective-permute-start.18 = (f32[144,128]{1,0:T(8,128)S(1)}, f32[144,128]{1,0:T(8,128)S(1)}, u32[]{:S(2)}, u32[]{:S(2)}) collective-permute-start(f32[144,128]{1,0:T(8,128)S(1)} %get-tuple-element.64.mine_ref), channel_id=1, source_target_pairs={{0,32},{32,0},{1,33},{33,1},{2,34},{34,2},{3,35},{35,3},{4,36},{36... | collective-permute-start | bytes 221192 | tf_op jit(solution)/shard_map/ppermute | solution.py:239
  93.9 2.3 %collective-permute-done.18.other_ref = f32[144,128]{1,0:T(8,128)S(1)} collective-permute-done((f32[144,128]{1,0:T(8,128)S(1)}, f32[144,128]{1,0:T(8,128)S(1)}, u32[]{:S(2)}, u32[]{:S(2)}) %collective-permute-start.18) | collective-permute-done | bytes 73760 | tf_op jit(solution)/shard_map/ppermute | solution.py:239
  97.2 2.2 %collective-permute-start.20 = (f32[144,128]{1,0:T(8,128)S(1)}, f32[144,128]{1,0:T(8,128)S(1)}, u32[]{:S(2)}, u32[]{:S(2)}) collective-permute-start(f32[144,128]{1,0:T(8,128)S(1)} %get-tuple-element.65.refs_0_), channel_id=1, source_target_pairs={{0,1},{16,17},{1,0},{17,16},{2,3},{18,19},{3,2},{19,18},{4,5},{20,... | collective-permute-start | bytes 221192 | tf_op jit(solution)/shard_map/ppermute | solution.py:245
  99.9 5.3 %collective-permute-start.23 = (f32[144,128]{1,0:T(8,128)S(1)}, f32[144,128]{1,0:T(8,128)S(1)}, u32[]{:S(2)}, u32[]{:S(2)}) collective-permute-start(f32[144,128]{1,0:T(8,128)S(1)} %get-tuple-element.66.refs_4_), channel_id=1, source_target_pairs={{0,4},{2,6},{4,0},{6,2},{1,5},{3,7},{5,1},{7,3},{8,12},{10,14},{12... | collective-permute-start | bytes 221192 | tf_op jit(solution)/shard_map/ppermute | solution.py:245
  105.3 2.6 %collective-permute-start.24 = (f32[144,128]{1,0:T(8,128)S(1)}, f32[144,128]{1,0:T(8,128)S(1)}, u32[]{:S(2)}, u32[]{:S(2)}) collective-permute-start(f32[144,128]{1,0:T(8,128)S(1)} %get-tuple-element.66.refs_4_), channel_id=1, source_target_pairs={{0,6},{2,0},{4,2},{6,4},{1,7},{3,1},{5,3},{7,5},{8,14},{10,8},{12,... | collective-permute-start | bytes 221192 | tf_op jit(solution)/shard_map/ppermute | solution.py:245
  108.4 2.0 %collective-permute-done.24.refs_7_ = f32[144,128]{1,0:T(8,128)S(1)} collective-permute-done((f32[144,128]{1,0:T(8,128)S(1)}, f32[144,128]{1,0:T(8,128)S(1)}, u32[]{:S(2)}, u32[]{:S(2)}) %collective-permute-start.24) | collective-permute-done | bytes 73760 | tf_op jit(solution)/shard_map/ppermute | solution.py:245
  110.4 0.9 shard_map.47
  111.3 1.6 %collective-permute-start.25 = (f32[4,144,128]{2,1,0:T(8,128)S(1)}, f32[4,144,128]{2,1,0:T(8,128)S(1)}, u32[]{:S(2)}, u32[]{:S(2)}) collective-permute-start(f32[4,144,128]{2,1,0:T(8,128)S(1)} %get-tuple-element.68.refs_0_), channel_id=1, source_target_pairs={{0,2},{2,4},{4,6},{6,0},{1,3},{3,5},{5,7},{7,1},{8,10},{10,12},{12... | collective-permute-start | bytes 884744 | tf_op jit(solution)/shard_map/ppermute | solution.py:245
  113.0 2.7 %collective-permute-start.26 = (f32[4,144,128]{2,1,0:T(8,128)S(1)}, f32[4,144,128]{2,1,0:T(8,128)S(1)}, u32[]{:S(2)}, u32[]{:S(2)}) collective-permute-start(f32[4,144,128]{2,1,0:T(8,128)S(1)} %get-tuple-element.68.refs_0_), channel_id=1, source_target_pairs={{0,4},{2,6},{4,0},{6,2},{1,5},{3,7},{5,1},{7,3},{8,12},{10,14},{12... | collective-permute-start | bytes 884744 | tf_op jit(solution)/shard_map/ppermute | solution.py:245
  115.6 2.6 %collective-permute-start.27 = (f32[4,144,128]{2,1,0:T(8,128)S(1)}, f32[4,144,128]{2,1,0:T(8,128)S(1)}, u32[]{:S(2)}, u32[]{:S(2)}) collective-permute-start(f32[4,144,128]{2,1,0:T(8,128)S(1)} %get-tuple-element.68.refs_0_), channel_id=1, source_target_pairs={{0,6},{2,0},{4,2},{6,4},{1,7},{3,1},{5,3},{7,5},{8,14},{10,8},{12,... | collective-permute-start | bytes 884744 | tf_op jit(solution)/shard_map/ppermute | solution.py:245
  118.3 1.3 collective-permute-start.29
  119.6 2.2 %collective-permute-start.30 = (f32[4,144,128]{2,1,0:T(8,128)S(1)}, f32[4,144,128]{2,1,0:T(8,128)S(1)}, u32[]{:S(2)}, u32[]{:S(2)}) collective-permute-start(f32[4,144,128]{2,1,0:T(8,128)S(1)} %get-tuple-element.69.refs_4_), channel_id=1, source_target_pairs={{0,17},{16,0},{1,16},{17,1},{2,19},{18,2},{3,18},{19,3},{4,21},{20... | collective-permute-start | bytes 884744 | tf_op jit(solution)/shard_map/ppermute | solution.py:245
  123.7 11.0 %all-to-all-start = ((f32[32,32,128]{2,1,0:T(8,128)}), f32[32,32,128]{2,1,0:T(8,128)S(1)}, u32[]{:S(2)}, u32[]{:S(2)}) async-start(f32[32,32,128]{2,1,0:T(8,128)} %get-tuple-element.70), calls=%async_computation | async-start | bytes 1048576 | tf_op jit(solution)/shard_map/all_to_all | solution.py:300
  134.7 16.8 %shard_map.48.mine_ref = f32[128,1024]{1,0:T(8,128)S(1)} custom-call(s32[3]{0:T(128)S(1)} %pad_add_fusion.1.at_ref, f32[1]{0:T(128)} %bitcast.8.damp_ref, f32[4,144,128]{2,1,0:T(8,128)S(1)} %get-tuple-element.68.refs_0_, f32[4,144,128]{2,1,0:T(8,128)S(1)} %collective-permute-done.25.refs_1_, f32[4,144,128]{2,1,0:T(8,128)S(1)} %collective-permute-done.26.refs_2_, ...), custom_call_target="tpu_custom_call" | custom-call | flops 11274289152 | bytes 2883584 | tf_op jit(solution)/shard_map/pallas_call | solution.py:225
  151.6 1.9 %collective-permute-done.31.other_ref = f32[128,1024]{1,0:T(8,128)S(1)} collective-permute-done((f32[128,1024]{1,0:T(8,128)S(1)}, f32[128,1024]{1,0:T(8,128)S(1)}, u32[]{:S(2)}, u32[]{:S(2)}) %collective-permute-start.31) | collective-permute-done | bytes 524320 | tf_op jit(solution)/shard_map/ppermute | solution.py:239
  154.3 3.4 %collective-permute-start.34 = (f32[4,32,128]{2,1,0:T(8,128)S(1)}, f32[4,32,128]{2,1,0:T(8,128)S(1)}, u32[]{:S(2)}, u32[]{:S(2)}) collective-permute-start(f32[4,32,128]{2,1,0:T(8,128)S(1)} %bitcast.30), channel_id=1, source_target_pairs={{0,48},{16,32},{32,16},{48,0},{1,49},{17,33},{33,17},{49,1},{2,50}... | collective-permute-start | bytes 196616 | tf_op jit(solution)/shard_map/ppermute | solution.py:239
  159.0 1.9 %collective-permute-done.34.refs_3_ = f32[4,32,128]{2,1,0:T(8,128)S(1)} collective-permute-done((f32[4,32,128]{2,1,0:T(8,128)S(1)}, f32[4,32,128]{2,1,0:T(8,128)S(1)}, u32[]{:S(2)}, u32[]{:S(2)}) %collective-permute-start.34) | collective-permute-done | bytes 65568 | tf_op jit(solution)/shard_map/ppermute | solution.py:239
  161.1 1.4 collective-permute-done.35.refs_4_
  162.6 1.4 shard_map.49
  (54 shorter events, 6.9 us)
Async XLA Ops:
  0.0 1.2 copy-start.2
  1.2 1.2 copy-start.3
  5.4 1.4 copy-start
  6.8 4.7 %collective-permute-start.7 = (f32[4,4,272,128]{3,2,1,0:T(8,128)}, f32[4,4,272,128]{3,2,1,0:T(8,128)}, u32[]{:S(2)}, u32[]{:S(2)}) collective-permute-start(f32[4,4,272,128]{3,2,1,0:T(8,128)} %get-tuple-element.49), channel_id=1, source_target_pairs={{0,8},{8,0},{1,9},{9,1},{2,10},{10,2},{3,11},{11,3},{4,12},{12,4},... | collective-permute-start | bytes 6684680 | tf_op jit(solution)/shard_map/ppermute | solution.py:239
  9.8 11.0 %collective-permute-start = (f32[4,4,272,128]{3,2,1,0:T(8,128)}, f32[4,4,272,128]{3,2,1,0:T(8,128)}, u32[]{:S(2)}, u32[]{:S(2)}) collective-permute-start(f32[4,4,272,128]{3,2,1,0:T(8,128)} %get-tuple-element.39), channel_id=1, source_target_pairs={{0,8},{8,0},{1,9},{9,1},{2,10},{10,2},{3,11},{11,3},{4,12},{12,4},... | collective-permute-start | bytes 6684680 | tf_op jit(solution)/shard_map/ppermute | solution.py:239
  11.5 1.6 copy-start.1
  16.2 27.4 %collective-permute-start.10 = (f32[4,272,128]{2,1,0:T(8,128)}, f32[4,272,128]{2,1,0:T(8,128)S(1)}, u32[]{:S(2)}, u32[]{:S(2)}) collective-permute-start(f32[4,272,128]{2,1,0:T(8,128)} %get-tuple-element.53), channel_id=1, source_target_pairs={{0,17},{16,0},{1,16},{17,1},{2,19},{18,2},{3,18},{19,3},{4,21},{20... | collective-permute-start | bytes 1671176 | tf_op jit(solution)/shard_map/ppermute | solution.py:245
  19.2 24.4 %collective-permute-start.8 = (f32[4,272,128]{2,1,0:T(8,128)}, f32[4,272,128]{2,1,0:T(8,128)}, u32[]{:S(2)}, u32[]{:S(2)}) collective-permute-start(f32[4,272,128]{2,1,0:T(8,128)} %get-tuple-element.51), channel_id=1, source_target_pairs={{0,1},{16,17},{1,0},{17,16},{2,3},{18,19},{3,2},{19,18},{4,5},{20,... | collective-permute-start | bytes 1671176 | tf_op jit(solution)/shard_map/ppermute | solution.py:245
  19.8 27.5 %collective-permute-start.9 = (f32[4,272,128]{2,1,0:T(8,128)}, f32[4,272,128]{2,1,0:T(8,128)}, u32[]{:S(2)}, u32[]{:S(2)}) collective-permute-start(f32[4,272,128]{2,1,0:T(8,128)} %get-tuple-element.52), channel_id=1, source_target_pairs={{0,16},{16,1},{1,17},{17,0},{2,18},{18,3},{3,19},{19,2},{4,20},{20... | collective-permute-start | bytes 1671176 | tf_op jit(solution)/shard_map/ppermute | solution.py:245
  22.6 28.2 %collective-permute-start.1 = (f32[4,272,128]{2,1,0:T(8,128)S(1)}, f32[4,272,128]{2,1,0:T(8,128)S(1)}, u32[]{:S(2)}, u32[]{:S(2)}) collective-permute-start(f32[4,272,128]{2,1,0:T(8,128)S(1)} %get-tuple-element.41), channel_id=1, source_target_pairs={{0,4},{2,6},{4,0},{6,2},{1,5},{3,7},{5,1},{7,3},{8,12},{10,14},{12... | collective-permute-start | bytes 1671176 | tf_op jit(solution)/shard_map/ppermute | solution.py:245
  24.8 28.0 %collective-permute-start.2 = (f32[4,272,128]{2,1,0:T(8,128)S(1)}, f32[4,272,128]{2,1,0:T(8,128)S(1)}, u32[]{:S(2)}, u32[]{:S(2)}) collective-permute-start(f32[4,272,128]{2,1,0:T(8,128)S(1)} %get-tuple-element.42), channel_id=1, source_target_pairs={{0,2},{2,4},{4,6},{6,0},{1,3},{3,5},{5,7},{7,1},{8,10},{10,12},{12... | collective-permute-start | bytes 1671176 | tf_op jit(solution)/shard_map/ppermute | solution.py:245
  43.6 16.9 %collective-permute-start.3 = (f32[4,272,128]{2,1,0:T(8,128)S(1)}, f32[4,272,128]{2,1,0:T(8,128)S(1)}, u32[]{:S(2)}, u32[]{:S(2)}) collective-permute-start(f32[4,272,128]{2,1,0:T(8,128)S(1)} %get-tuple-element.43), channel_id=1, source_target_pairs={{0,6},{2,0},{4,2},{6,4},{1,7},{3,1},{5,3},{7,5},{8,14},{10,8},{12,... | collective-permute-start | bytes 1671176 | tf_op jit(solution)/shard_map/ppermute | solution.py:245
  48.6 16.9 %collective-permute-start.11 = (f32[272,128]{1,0:T(8,128)S(1)}, f32[272,128]{1,0:T(8,128)S(1)}, u32[]{:S(2)}, u32[]{:S(2)}) collective-permute-start(f32[272,128]{1,0:T(8,128)S(1)} %get-tuple-element.55), channel_id=1, source_target_pairs={{0,4},{2,6},{4,0},{6,2},{1,5},{3,7},{5,1},{7,3},{8,12},{10,14},{12... | collective-permute-start | bytes 417800 | tf_op jit(solution)/shard_map/ppermute | solution.py:245
  50.9 15.7 %collective-permute-start.12 = (f32[272,128]{1,0:T(8,128)S(1)}, f32[272,128]{1,0:T(8,128)S(1)}, u32[]{:S(2)}, u32[]{:S(2)}) collective-permute-start(f32[272,128]{1,0:T(8,128)S(1)} %get-tuple-element.56), channel_id=1, source_target_pairs={{0,2},{2,4},{4,6},{6,0},{1,3},{3,5},{5,7},{7,1},{8,10},{10,12},{12... | collective-permute-start | bytes 417800 | tf_op jit(solution)/shard_map/ppermute | solution.py:245
  50.9 15.7 %collective-permute-start.13 = (f32[272,128]{1,0:T(8,128)S(1)}, f32[272,128]{1,0:T(8,128)S(1)}, u32[]{:S(2)}, u32[]{:S(2)}) collective-permute-start(f32[272,128]{1,0:T(8,128)S(1)} %get-tuple-element.57), channel_id=1, source_target_pairs={{0,6},{2,0},{4,2},{6,4},{1,7},{3,1},{5,3},{7,5},{8,14},{10,8},{12,... | collective-permute-start | bytes 417800 | tf_op jit(solution)/shard_map/ppermute | solution.py:245
  60.5 61.3 %copy-start.4 = (f32[2]{0:T(128)S(1)}, f32[2]{0:T(128)}, u32[]{:S(2)}) copy-start(f32[2]{0:T(128)} %param.5) | copy-start | bytes 28
  60.6 6.9 %collective-permute-start.4 = (f32[272,128]{1,0:T(8,128)S(1)}, f32[272,128]{1,0:T(8,128)S(1)}, u32[]{:S(2)}, u32[]{:S(2)}) collective-permute-start(f32[272,128]{1,0:T(8,128)S(1)} %get-tuple-element.45), channel_id=1, source_target_pairs={{0,1},{16,17},{1,0},{17,16},{2,3},{18,19},{3,2},{19,18},{4,5},{20,... | collective-permute-start | bytes 417800 | tf_op jit(solution)/shard_map/ppermute | solution.py:245
  60.9 8.0 %collective-permute-start.5 = (f32[272,128]{1,0:T(8,128)S(1)}, f32[272,128]{1,0:T(8,128)S(1)}, u32[]{:S(2)}, u32[]{:S(2)}) collective-permute-start(f32[272,128]{1,0:T(8,128)S(1)} %get-tuple-element.46), channel_id=1, source_target_pairs={{0,16},{16,1},{1,17},{17,0},{2,18},{18,3},{3,19},{19,2},{4,20},{20... | collective-permute-start | bytes 417800 | tf_op jit(solution)/shard_map/ppermute | solution.py:245
  65.6 5.1 %collective-permute-start.6 = (f32[272,128]{1,0:T(8,128)S(1)}, f32[272,128]{1,0:T(8,128)S(1)}, u32[]{:S(2)}, u32[]{:S(2)}) collective-permute-start(f32[272,128]{1,0:T(8,128)S(1)} %get-tuple-element.47), channel_id=1, source_target_pairs={{0,17},{16,0},{1,16},{17,1},{2,19},{18,2},{3,18},{19,3},{4,21},{20... | collective-permute-start | bytes 417800 | tf_op jit(solution)/shard_map/ppermute | solution.py:245
  70.7 5.1 %collective-permute-start.14 = (f32[272,128]{1,0:T(8,128)S(1)}, f32[272,128]{1,0:T(8,128)S(1)}, u32[]{:S(2)}, u32[]{:S(2)}) collective-permute-start(f32[272,128]{1,0:T(8,128)S(1)} %get-tuple-element.59), channel_id=1, source_target_pairs={{0,32},{32,0},{1,33},{33,1},{2,34},{34,2},{3,35},{35,3},{4,36},{36... | collective-permute-start | bytes 417800 | tf_op jit(solution)/shard_map/ppermute | solution.py:239
  75.9 12.0 %collective-permute-start.15 = (f32[176,128]{1,0:T(8,128)S(1)}, f32[176,128]{1,0:T(8,128)S(1)}, u32[]{:S(2)}, u32[]{:S(2)}) collective-permute-start(f32[176,128]{1,0:T(8,128)S(1)} %get-tuple-element.61), channel_id=1, source_target_pairs={{0,128},{64,192},{128,0},{192,64},{1,129},{65,193},{129,1},{193,65... | collective-permute-start | bytes 270344 | tf_op jit(solution)/shard_map/ppermute | solution.py:245
  83.8 7.6 %collective-permute-start.16 = (f32[176,128]{1,0:T(8,128)S(1)}, f32[176,128]{1,0:T(8,128)S(1)}, u32[]{:S(2)}, u32[]{:S(2)}) collective-permute-start(f32[176,128]{1,0:T(8,128)S(1)} %get-tuple-element.62), channel_id=1, source_target_pairs={{0,64},{64,128},{128,192},{192,0},{1,65},{65,129},{129,193},{193,1... | collective-permute-start | bytes 270344 | tf_op jit(solution)/shard_map/ppermute | solution.py:245
  86.2 5.4 %collective-permute-start.17 = (f32[176,128]{1,0:T(8,128)S(1)}, f32[176,128]{1,0:T(8,128)S(1)}, u32[]{:S(2)}, u32[]{:S(2)}) collective-permute-start(f32[176,128]{1,0:T(8,128)S(1)} %get-tuple-element.63), channel_id=1, source_target_pairs={{0,192},{64,0},{128,64},{192,128},{1,193},{65,1},{129,65},{193,129... | collective-permute-start | bytes 270344 | tf_op jit(solution)/shard_map/ppermute | solution.py:245
  91.7 4.6 %collective-permute-start.18 = (f32[144,128]{1,0:T(8,128)S(1)}, f32[144,128]{1,0:T(8,128)S(1)}, u32[]{:S(2)}, u32[]{:S(2)}) collective-permute-start(f32[144,128]{1,0:T(8,128)S(1)} %get-tuple-element.64.mine_ref), channel_id=1, source_target_pairs={{0,32},{32,0},{1,33},{33,1},{2,34},{34,2},{3,35},{35,3},{4,36},{36... | collective-permute-start | bytes 221192 | tf_op jit(solution)/shard_map/ppermute | solution.py:239
  96.3 9.0 %collective-permute-start.19 = (f32[144,128]{1,0:T(8,128)S(1)}, f32[144,128]{1,0:T(8,128)S(1)}, u32[]{:S(2)}, u32[]{:S(2)}) collective-permute-start(f32[144,128]{1,0:T(8,128)S(1)} %get-tuple-element.65.refs_0_), channel_id=1, source_target_pairs={{0,16},{16,1},{1,17},{17,0},{2,18},{18,3},{3,19},{19,2},{4,20},{20... | collective-permute-start | bytes 221192 | tf_op jit(solution)/shard_map/ppermute | solution.py:245
  97.2 10.8 %collective-permute-start.20 = (f32[144,128]{1,0:T(8,128)S(1)}, f32[144,128]{1,0:T(8,128)S(1)}, u32[]{:S(2)}, u32[]{:S(2)}) collective-permute-start(f32[144,128]{1,0:T(8,128)S(1)} %get-tuple-element.65.refs_0_), channel_id=1, source_target_pairs={{0,1},{16,17},{1,0},{17,16},{2,3},{18,19},{3,2},{19,18},{4,5},{20,... | collective-permute-start | bytes 221192 | tf_op jit(solution)/shard_map/ppermute | solution.py:245
  99.4 8.5 %collective-permute-start.21 = (f32[144,128]{1,0:T(8,128)S(1)}, f32[144,128]{1,0:T(8,128)S(1)}, u32[]{:S(2)}, u32[]{:S(2)}) collective-permute-start(f32[144,128]{1,0:T(8,128)S(1)} %get-tuple-element.65.refs_0_), channel_id=1, source_target_pairs={{0,17},{16,0},{1,16},{17,1},{2,19},{18,2},{3,18},{19,3},{4,21},{20... | collective-permute-start | bytes 221192 | tf_op jit(solution)/shard_map/ppermute | solution.py:245
  99.9 8.0 %collective-permute-start.22 = (f32[144,128]{1,0:T(8,128)S(1)}, f32[144,128]{1,0:T(8,128)S(1)}, u32[]{:S(2)}, u32[]{:S(2)}) collective-permute-start(f32[144,128]{1,0:T(8,128)S(1)} %get-tuple-element.66.refs_4_), channel_id=1, source_target_pairs={{0,2},{2,4},{4,6},{6,0},{1,3},{3,5},{5,7},{7,1},{8,10},{10,12},{12... | collective-permute-start | bytes 221192 | tf_op jit(solution)/shard_map/ppermute | solution.py:245
  99.9 8.5 %collective-permute-start.23 = (f32[144,128]{1,0:T(8,128)S(1)}, f32[144,128]{1,0:T(8,128)S(1)}, u32[]{:S(2)}, u32[]{:S(2)}) collective-permute-start(f32[144,128]{1,0:T(8,128)S(1)} %get-tuple-element.66.refs_4_), channel_id=1, source_target_pairs={{0,4},{2,6},{4,0},{6,2},{1,5},{3,7},{5,1},{7,3},{8,12},{10,14},{12... | collective-permute-start | bytes 221192 | tf_op jit(solution)/shard_map/ppermute | solution.py:245
  105.3 5.1 %collective-permute-start.24 = (f32[144,128]{1,0:T(8,128)S(1)}, f32[144,128]{1,0:T(8,128)S(1)}, u32[]{:S(2)}, u32[]{:S(2)}) collective-permute-start(f32[144,128]{1,0:T(8,128)S(1)} %get-tuple-element.66.refs_4_), channel_id=1, source_target_pairs={{0,6},{2,0},{4,2},{6,4},{1,7},{3,1},{5,3},{7,5},{8,14},{10,8},{12,... | collective-permute-start | bytes 221192 | tf_op jit(solution)/shard_map/ppermute | solution.py:245
  111.3 8.3 %collective-permute-start.25 = (f32[4,144,128]{2,1,0:T(8,128)S(1)}, f32[4,144,128]{2,1,0:T(8,128)S(1)}, u32[]{:S(2)}, u32[]{:S(2)}) collective-permute-start(f32[4,144,128]{2,1,0:T(8,128)S(1)} %get-tuple-element.68.refs_0_), channel_id=1, source_target_pairs={{0,2},{2,4},{4,6},{6,0},{1,3},{3,5},{5,7},{7,1},{8,10},{10,12},{12... | collective-permute-start | bytes 884744 | tf_op jit(solution)/shard_map/ppermute | solution.py:245
  113.0 21.7 %collective-permute-start.26 = (f32[4,144,128]{2,1,0:T(8,128)S(1)}, f32[4,144,128]{2,1,0:T(8,128)S(1)}, u32[]{:S(2)}, u32[]{:S(2)}) collective-permute-start(f32[4,144,128]{2,1,0:T(8,128)S(1)} %get-tuple-element.68.refs_0_), channel_id=1, source_target_pairs={{0,4},{2,6},{4,0},{6,2},{1,5},{3,7},{5,1},{7,3},{8,12},{10,14},{12... | collective-permute-start | bytes 884744 | tf_op jit(solution)/shard_map/ppermute | solution.py:245
  115.6 19.1 %collective-permute-start.27 = (f32[4,144,128]{2,1,0:T(8,128)S(1)}, f32[4,144,128]{2,1,0:T(8,128)S(1)}, u32[]{:S(2)}, u32[]{:S(2)}) collective-permute-start(f32[4,144,128]{2,1,0:T(8,128)S(1)} %get-tuple-element.68.refs_0_), channel_id=1, source_target_pairs={{0,6},{2,0},{4,2},{6,4},{1,7},{3,1},{5,3},{7,5},{8,14},{10,8},{12,... | collective-permute-start | bytes 884744 | tf_op jit(solution)/shard_map/ppermute | solution.py:245
  118.3 16.4 %collective-permute-start.28 = (f32[4,144,128]{2,1,0:T(8,128)S(1)}, f32[4,144,128]{2,1,0:T(8,128)S(1)}, u32[]{:S(2)}, u32[]{:S(2)}) collective-permute-start(f32[4,144,128]{2,1,0:T(8,128)S(1)} %get-tuple-element.69.refs_4_), channel_id=1, source_target_pairs={{0,16},{16,1},{1,17},{17,0},{2,18},{18,3},{3,19},{19,2},{4,20},{20... | collective-permute-start | bytes 884744 | tf_op jit(solution)/shard_map/ppermute | solution.py:245
  118.3 16.4 %collective-permute-start.29 = (f32[4,144,128]{2,1,0:T(8,128)S(1)}, f32[4,144,128]{2,1,0:T(8,128)S(1)}, u32[]{:S(2)}, u32[]{:S(2)}) collective-permute-start(f32[4,144,128]{2,1,0:T(8,128)S(1)} %get-tuple-element.69.refs_4_), channel_id=1, source_target_pairs={{0,1},{16,17},{1,0},{17,16},{2,3},{18,19},{3,2},{19,18},{4,5},{20,... | collective-permute-start | bytes 884744 | tf_op jit(solution)/shard_map/ppermute | solution.py:245
  119.6 15.1 %collective-permute-start.30 = (f32[4,144,128]{2,1,0:T(8,128)S(1)}, f32[4,144,128]{2,1,0:T(8,128)S(1)}, u32[]{:S(2)}, u32[]{:S(2)}) collective-permute-start(f32[4,144,128]{2,1,0:T(8,128)S(1)} %get-tuple-element.69.refs_4_), channel_id=1, source_target_pairs={{0,17},{16,0},{1,16},{17,1},{2,19},{18,2},{3,18},{19,3},{4,21},{20... | collective-permute-start | bytes 884744 | tf_op jit(solution)/shard_map/ppermute | solution.py:245
  123.7 29.9 %all-to-all-start = ((f32[32,32,128]{2,1,0:T(8,128)}), f32[32,32,128]{2,1,0:T(8,128)S(1)}, u32[]{:S(2)}, u32[]{:S(2)}) async-start(f32[32,32,128]{2,1,0:T(8,128)} %get-tuple-element.70), calls=%async_computation | async-start | bytes 1048576 | tf_op jit(solution)/shard_map/all_to_all | solution.py:300
  151.5 2.0 %collective-permute-start.31 = (f32[128,1024]{1,0:T(8,128)S(1)}, f32[128,1024]{1,0:T(8,128)S(1)}, u32[]{:S(2)}, u32[]{:S(2)}) collective-permute-start(f32[128,1024]{1,0:T(8,128)S(1)} %shard_map.48.mine_ref), channel_id=1, source_target_pairs={{0,8},{8,0},{1,9},{9,1},{2,10},{10,2},{3,11},{11,3},{4,12},{12,4},... | collective-permute-start | bytes 1572872 | tf_op jit(solution)/shard_map/ppermute | solution.py:239
  154.1 4.4 %collective-permute-start.32 = (f32[4,32,128]{2,1,0:T(8,128)S(1)}, f32[4,32,128]{2,1,0:T(8,128)S(1)}, u32[]{:S(2)}, u32[]{:S(2)}) collective-permute-start(f32[4,32,128]{2,1,0:T(8,128)S(1)} %bitcast.28), channel_id=1, source_target_pairs={{0,16},{16,0},{1,17},{17,1},{2,18},{18,2},{3,19},{19,3},{4,20},{20... | collective-permute-start | bytes 196616 | tf_op jit(solution)/shard_map/ppermute | solution.py:239
  154.3 4.7 %collective-permute-start.33 = (f32[4,32,128]{2,1,0:T(8,128)S(1)}, f32[4,32,128]{2,1,0:T(8,128)S(1)}, u32[]{:S(2)}, u32[]{:S(2)}) collective-permute-start(f32[4,32,128]{2,1,0:T(8,128)S(1)} %bitcast.29), channel_id=1, source_target_pairs={{0,32},{32,0},{1,33},{33,1},{2,34},{34,2},{3,35},{35,3},{4,36},{36... | collective-permute-start | bytes 196616 | tf_op jit(solution)/shard_map/ppermute | solution.py:239
  154.3 6.6 %collective-permute-start.34 = (f32[4,32,128]{2,1,0:T(8,128)S(1)}, f32[4,32,128]{2,1,0:T(8,128)S(1)}, u32[]{:S(2)}, u32[]{:S(2)}) collective-permute-start(f32[4,32,128]{2,1,0:T(8,128)S(1)} %bitcast.30), channel_id=1, source_target_pairs={{0,48},{16,32},{32,16},{48,0},{1,49},{17,33},{33,17},{49,1},{2,50}... | collective-permute-start | bytes 196616 | tf_op jit(solution)/shard_map/ppermute | solution.py:239
  161.0 1.6 collective-permute-start.35

commit v4 on v3

v4 whole, which is shorter than its diff:
```python
import functools
import math

import jax
import jax.numpy as jnp
from jax import lax
from jax.experimental import pallas as pl
from jax.experimental.pallas import tpu as pltpu
from jax.sharding import Mesh
from jax.sharding import PartitionSpec as P


INTERPRET = False
STEPS = 14
AXES = ("zh", "zl", "yl", "c", "x", "yh")
ZH, ZL, YL, CORE, X, YH = range(6)
DP = ("zh", "zl", "yl", "c")
GRP = ("x", "yh")
Y = ("yl", "yh")
PLANE = ("zl", "yl", "x", "yh")
B = 128
F32 = jnp.float32
BF16 = jnp.bfloat16


def ring_places(at_ref):
    return at_ref[X], at_ref[YH] * 2 + at_ref[YL]


def sub_segments(start, size, piece):
    done = 0
    while done < size:
        q, r = divmod(start + done, piece)
        n = min(piece - r, size - done)
        yield q, r, done, n
        done += n


def dot(a, b):
    return jnp.dot(a, b, preferred_element_type=F32)


def gram_terms(nb, colour, which, core, acts_ref, grads_ref, t_ref, out):
    part = nb * (nb + 1) // 2 * B // 2
    piece = part // 16
    strip = nb * B // 4
    rows = (out.shape[2] - piece) // 4
    grads = grads_ref[...]
    slot = core if which else 1 - core
    right = jnp.where(slot == 0, acts_ref[...], grads)
    for jj in range(nb // 2):
        spans = []
        for j in (2 * jj, 2 * jj + 1):
            base = j * (j + 1) // 2 * B
            lo, hi = max(base, colour * part), min(base + (j + 1) * B, (colour + 1) * part)
            if lo < hi:
                spans.append((j, lo, hi, lo - base, hi - base))
        if not spans:
            continue
        low, high = min(s[3] for s in spans), max(s[4] for s in spans)
        res = dot(t_ref[slot, low:high, :], right[:, jj * 2 * B : (jj + 1) * 2 * B])
        for j, lo, hi, first, _ in spans:
            lane = (j - 2 * jj) * B
            for q, r, at, n in sub_segments(lo - colour * part, hi - lo, piece):
                at = first - low + at
                out[q // 4, q % 4, r : r + n, :] = res[at : at + n, lane : lane + B]
    begin = pl.multiple_of(slot * 2 * strip + colour * strip, strip)
    left = t_ref[0, pl.ds(begin, strip), :]
    for x in range(nb // 2):
        res = dot(left, grads[:, x * 2 * B : (x + 1) * 2 * B])
        for s in range(strip // rows):
            zh, yl = divmod(s, 2)
            for yh in range(2):
                y = yh * 2 + yl
                first, second = (y, x) if colour else (x, y)
                at = piece + zh * rows
                out[first, second, at : at + rows, :] = res[s * rows : s * rows + rows, yh * B : yh * B + B]


def gram_kernel(nb, colour, which, at_ref, acts_ref, grads_ref, t_ref, out_ref):
    gram_terms(nb, colour, which, at_ref[CORE], acts_ref, grads_ref, t_ref, out_ref)


def first_kernel(nb, colour, at_ref, acts_ref, grads_ref, t_ref, out_ref):
    t_ref[0] = acts_ref[...].T
    t_ref[1] = grads_ref[...].T
    gram_terms(nb, colour, 0, at_ref[CORE], acts_ref, grads_ref, t_ref, out_ref)


def turned_kernel(count, colour, at_ref, *refs):
    ins, outs = refs[:count], refs[count:]
    for k, out in enumerate(outs):
        z = lax.rem(ring_places(at_ref)[colour] + k, len(outs))
        total = ins[0][z]
        for ref in ins[1:]:
            total = total + ref[z]
        out[...] = total


def sorted_kernel(at_ref, *refs):
    ins, outs = refs[:8], refs[8:]
    low = at_ref[ZL] == 0
    x, y = ring_places(at_ref)
    for k in range(4):
        sums = []
        for colour in range(2):
            z = lax.rem((y, x)[colour] + k, 4)
            total = ins[colour * 4][z]
            for ref in ins[colour * 4 + 1 : colour * 4 + 4]:
                total = total + ref[z]
            sums.append(total)
        outs[k][...] = jnp.where(low, sums[0], sums[1])
        outs[4 + k][...] = jnp.where(low, sums[1], sums[0])


def ring_kernel(piece, at_ref, *refs):
    ins, outs, sum_ref = refs[:8], refs[8:-1], refs[-1]
    total = ins[0][...]
    for ref in ins[1:]:
        total = total + ref[...]
    sum_ref[...] = total
    rows = outs[0].shape[0] - piece
    for k, out in enumerate(outs):
        z = lax.rem(at_ref[ZH] + k, len(outs))
        out[:piece, :] = sum_ref[:piece, :]
        out[piece:, :] = sum_ref[pl.ds(pl.multiple_of(piece + z * rows, 8), rows), :]


def total_kernel(scale, at_ref, *refs):
    factor_ref, cross_ref = refs[-2:]
    total = refs[0][...]
    for ref in refs[1:-2]:
        total = total + ref[...]
    piece = factor_ref.shape[0]
    factor_ref[...] = total[:piece]
    cross_ref[...] = total[piece:] * scale


def joined_kernel(at_ref, *refs):
    outs = refs[-3:]
    low = at_ref[ZL] == 0
    for k in range(4):
        own, other = refs[k][...], refs[4 + k][...]
        outs[0][k] = jnp.where(low, own, other)
        outs[1][k] = jnp.where(low, other, own)
    cross = refs[8][...]
    for q in range(outs[2].shape[0]):
        outs[2][q] = cross


def rows_kernel(at_ref, cross_ref, mine_ref, other_ref, out_ref, c_ref):
    count, rows, _ = cross_ref.shape
    groups = c_ref.shape[1] // B
    for k in range(count):
        zh, g = divmod(k, groups)
        c_ref[zh * rows : zh * rows + rows, g * B : g * B + B] = cross_ref[k]
    hi, lo = split(c_ref[...])
    rhi, rlo = split(jnp.where(at_ref[CORE] == 0, other_ref[...], mine_ref[...]))
    out_ref[...] = ((dot_t(hi, rlo) + dot_t(lo, rhi)) + dot_t(hi, rhi)).reshape(out_ref.shape)


def last_kernel(at_ref, mine_ref, other_ref, *refs):
    out_ref, z_ref = refs[-2:]
    core, zl, yl = at_ref[CORE], at_ref[ZL], at_ref[YL]
    own, came = refs[:4], refs[4]
    for d in range(4):
        dz, dy = divmod(d, 2)
        pz, py = jnp.bitwise_xor(zl, dz), jnp.bitwise_xor(yl, dy)
        for zh in range(z_ref.shape[2]):
            z_ref[core, pz, zh, py] = own[d][zh]
            z_ref[1 - core, pz, zh, py] = came[d, zh]
    rows = out_ref.shape[0]
    first = pl.multiple_of(yl * 2 * rows + core * rows, 8)
    mine = mine_ref[pl.ds(first, rows), :]
    other = other_ref[pl.ds(first, rows), :]
    hi, lo = split(jnp.where(core == 0, mine, other))
    zhi, zlo = split(z_ref[...].reshape(-1, B))
    out_ref[...] = (dot(hi, zlo) + dot(lo, zhi)) + dot(hi, zhi)


def dot_t(a, b):
    return lax.dot_general(a, b, (((1,), (1,)), ((), ())), preferred_element_type=F32)


def split(v):
    hi = v.astype(BF16)
    return hi, (v - hi.astype(F32)).astype(BF16)


def inverse_kernel(nb, scale, at_ref, damp_ref, *refs):
    out_ref, p_ref, m_ref, hi_ref, lo_ref, s_ref, y_ref = refs[-7:]
    width = nb * B
    core = at_ref[CORE]
    damp = jnp.where(core == 0, damp_ref[0], damp_ref[1])
    places = ring_places(at_ref)
    for colour in range(2):
        first, second = places[colour], places[1 - colour]
        for k in range(4):
            for i in range(4):
                p = colour * 16 + lax.rem(first + 4 - k, 4) * 4 + lax.rem(second + 4 - i, 4)
                p_ref[p] = refs[colour * 4 + k][i]
    eye = (lax.broadcasted_iota(jnp.int32, (B, B), 0) == lax.broadcasted_iota(jnp.int32, (B, B), 1)).astype(F32)
    for j in range(nb):
        base = j * (j + 1) // 2 * B
        for i in range(j + 1):
            parts = []
            for q, r, _, n in sub_segments(base + i * B, B, p_ref.shape[1]):
                parts.append(p_ref[q, r : r + n, :])
            block = jnp.concatenate(parts, axis=0) * scale
            if i == j:
                block = block + damp * eye
            m_ref[i * B : (i + 1) * B, j * B : (j + 1) * B] = block
            if i != j:
                m_ref[j * B : (j + 1) * B, i * B : (i + 1) * B] = block.T
    total = jnp.zeros((8, width), F32)
    for i in range(nb):
        total = total + jnp.abs(m_ref[i * B : (i + 1) * B, :]).reshape(B // 8, 8, width).sum(axis=0)
    alpha = 1.0 / jnp.max(jnp.sum(total, axis=0, keepdims=True), axis=1, keepdims=True)
    for i in range(nb):
        rows = lax.broadcasted_iota(jnp.int32, (B, width), 0) + i * B
        ones = (rows == lax.broadcasted_iota(jnp.int32, (B, width), 1)).astype(F32)
        hi, lo = split(ones - alpha * m_ref[i * B : (i + 1) * B, :])
        hi_ref[i * B : (i + 1) * B, :] = hi
        lo_ref[i * B : (i + 1) * B, :] = lo
    height = at_ref[ZH] * 2 + at_ref[ZL]
    side = at_ref[X] * 2 + at_ref[YH]
    start = pl.multiple_of(jnp.where(core == 0, height, side) * B, B)
    rows = lax.broadcasted_iota(jnp.int32, (B, width), 0) + start
    ones = (rows == lax.broadcasted_iota(jnp.int32, (B, width), 1)).astype(F32)
    s_ref[...] = ones
    y_ref[...] = 2.0 * ones - alpha * m_ref[pl.ds(start, B), :]

    def step(_, carry):
        hi, lo = split(y_ref[...])
        both = jnp.concatenate([hi, lo], axis=0)
        first = dot(both, hi_ref[...])
        y_ref[...] = (dot(hi, lo_ref[...]) + first[B:]) + first[:B] + s_ref[...]
        return carry

    lax.fori_loop(0, STEPS, step, 0)
    out_ref[...] = alpha * y_ref[...]


def vmem(n):
    return [pl.BlockSpec(memory_space=pltpu.VMEM)] * n


def smem(n=1):
    return [pl.BlockSpec(memory_space=pltpu.SMEM)] * n


def call(kernel, scalars, arrays, outs, scratch=(), flops=0, limit=20):
    shapes = [o if hasattr(o, "dtype") else jax.ShapeDtypeStruct(o, F32) for o in outs]
    moved = sum(math.prod(a.shape) * a.dtype.itemsize for a in [*arrays, *shapes])
    return pl.pallas_call(
        kernel,
        out_shape=shapes,
        in_specs=smem(len(scalars)) + vmem(len(arrays)),
        out_specs=vmem(len(outs)),
        scratch_shapes=list(scratch),
        cost_estimate=pl.CostEstimate(flops=flops, bytes_accessed=moved, transcendentals=0),
        compiler_params=pltpu.CompilerParams(vmem_limit_bytes=limit << 20),
        interpret=INTERPRET,
    )(*scalars, *arrays)


def swapped(array, axes):
    pairs = [(k, lax.axis_size(axes) - 1 - k) for k in range(lax.axis_size(axes))]
    return lax.ppermute(array, axes, pairs)


def shifted(array, axis, by):
    size = lax.axis_size(axis)
    spots = [k % 2 * 2 + k // 2 for k in range(4)] if axis == Y else list(range(size))
    return lax.ppermute(array, axis, [(spots[k], spots[(k + by) % size]) for k in range(size)])


def sent_across(array, by, flip, along_y):
    def place(zl, x, y):
        return ((zl * 2 + y % 2) * 4 + x) * 2 + y // 2

    pairs = []
    for zl in range(2):
        for x in range(4):
            for y in range(4):
                target = (x, (y + by) % 4) if zl == along_y else ((x + by) % 4, y)
                pairs.append((place(zl, x, y), place(zl ^ flip, *target)))
    return lax.ppermute(array, PLANE, pairs)


def program(acts, grads, damping):
    tokens, width = acts.shape
    nb = width // B
    nz = lax.axis_size("zh")
    scale = 1.0 / (tokens * lax.axis_size(AXES))
    bits = [lax.axis_size(a).bit_length() - 1 for a in AXES]
    shifts = jnp.array([sum(bits[k + 1 :]) for k in range(len(bits))], jnp.int32)
    masks = jnp.array([(1 << b) - 1 for b in bits], jnp.int32)
    at = (lax.axis_index(AXES) >> shifts) & masks
    rings = ("x", Y)
    piece = nb * (nb + 1) // 2 * B // 32
    rows = width // lax.axis_size(DP)
    chunk = (piece + nz * rows, B)

    terms = (4, 4, *chunk)
    gram_flops = tokens * width * width
    transposed, sent1 = call(
        functools.partial(first_kernel, nb, 1), [at], [acts, grads],
        [jax.ShapeDtypeStruct((2, width, tokens), BF16), terms], flops=gram_flops,
    )

    def grams(colour, which):
        kernel = functools.partial(gram_kernel, nb, colour, which)
        return call(kernel, [at], [acts, grads, transposed], [terms], flops=gram_flops)[0]

    sent0 = grams(0, 0)
    came = []
    for sent in (sent0, sent1):
        came.append(swapped(sent, "c"))
    far = []
    for colour in (0, 1):
        ring = rings[colour]
        kept = grams(colour, 1)
        turned = call(functools.partial(turned_kernel, 2, colour), [at], [kept, came[colour]], [(4, *chunk)] * 4)
        far += [turned[0]] + [shifted(turned[k], ring, k) for k in (2, 1, 3)]
    sides = call(sorted_kernel, [at], far, [chunk] * 8)
    summands = [sides[0]]
    summands += [sent_across(sides[4 + k], k, 1, 1) for k in (2, 1, 3, 0)]
    summands += [sent_across(sides[k], k, 0, 0) for k in (2, 1, 3)]
    turned = call(
        functools.partial(ring_kernel, piece), [at], summands, [(piece + rows, B)] * nz,
        [pltpu.VMEM(chunk, F32)],
    )
    around = [turned[0]] + [shifted(turned[k], "zh", k) for k in (2, 1, 3)]
    mine, cross = call(functools.partial(total_kernel, scale), [at], around, [(piece, B), (rows, B)])
    other = {k: sent_across(mine, k, 1, 0) for k in (2, 1, 3, 0)}
    same = {k: sent_across(mine, k, 0, 0) for k in (2, 1, 3)}
    spread = ("zh", "x", "yh")
    *joined, crosses = call(
        joined_kernel, [at], [mine, *(same[k] for k in (1, 2, 3)), *(other[k] for k in range(4)), cross],
        [(4, piece, B), (4, piece, B), (lax.axis_size(spread), rows, B)],
    )
    pieces = []
    for colour in range(2):
        ring = rings[colour]
        moved = {k: shifted(joined[colour], ring, k) for k in (2, 1, 3)}
        pieces += [joined[colour]] + [moved[k] for k in (1, 2, 3)]
    cross_rows = lax.all_to_all(crosses, spread, 0, 0, tiled=True)
    (mine,) = call(
        functools.partial(inverse_kernel, nb, scale), [at, damping], pieces,
        [(B, width)],
        [
            pltpu.VMEM((32, piece, B), F32),
            pltpu.VMEM((width, width), F32),
            pltpu.VMEM((width, width), BF16),
            pltpu.VMEM((width, width), BF16),
            pltpu.VMEM((B, width), F32),
            pltpu.VMEM((B, width), F32),
        ],
        flops=2 * 3 * STEPS * B * width * width,
        limit=24,
    )
    other = swapped(mine, "c")
    (z,) = call(rows_kernel, [at], [cross_rows, mine, other], [(nz, rows, B)], [pltpu.VMEM((nz * rows, width), F32)])
    slabs = [z, swapped(z, "yl"), swapped(z, "zl"), swapped(z, ("zl", "yl"))]
    came = swapped(jnp.stack(slabs), "c")
    (out,) = call(
        last_kernel, [at], [mine, other, *slabs, came], [(rows, B)],
        [pltpu.VMEM((2, 2, nz, 2, rows, B), F32)],
    )
    return out


def solution(mesh):
    torus = Mesh(mesh.devices.reshape(4, 2, 2, 2, 4, 2), AXES)
    return jax.shard_map(
        program,
        mesh=torus,
        in_specs=(P(AXES, None), P(AXES, None), P()),
        out_specs=P(DP, GRP),
        check_vma=False,
    )
```

time: 165 us -> 156 us (0.945)
  waiting for transfers between devices: 53.6 us -> 50.6 us
  starting transfers between devices: 70.6 us -> 67.8 us
  local copies, waits for them, and re-layouts: 6.03 us -> 4.14 us
    ppermute x0 -> x14, starting transfers between devices: none -> 19.7 us  [sent_across(): return lax.ppermute(array, PLANE, pairs)]
    ppermute x27 -> x15, starting transfers between devices: 51.1 us -> 31.7 us  [shifted(): lax.ppermute(array, axis, [(spots[k], spots[(k + by) % size]) for k in ra...]
    ppermute x0 -> x14, waiting for transfers between devices: none -> 14.8 us  [sent_across(): return lax.ppermute(array, PLANE, pairs)]
    ppermute x27 -> x15, waiting for transfers between devices: 40.4 us -> 27.6 us  [shifted(): lax.ppermute(array, axis, [(spots[k], spots[(k + by) % size]) for k in ra...]
    ppermute x9 -> x7, waiting for transfers between devices: 13.2 us -> 8.1 us  [swapped(): return lax.ppermute(array, axes, pairs)]
    ppermute x9 -> x7, starting transfers between devices: 8.54 us -> 4.43 us  [swapped(): return lax.ppermute(array, axes, pairs)]
    unnamed x10 -> x14, local copies, waits for them, and re-layouts: 5.43 us -> 4.14 us
  transfers between devices with their start and end apart: 37 -> 37, of which waited for: 18 -> 21; matrix products, arithmetic and copies ran while one was open for 0% -> 0% of each run, Pallas kernels for 16% -> 15%
where the time goes in v4:
time: 156 us; the launch traced here: 154 us
  starting transfers between devices  67.8 us (43%)
  waiting for transfers between devices  50.6 us (32%)
  Pallas kernels  30.2 us (19%)
  local copies, waits for them, and re-layouts  4.14 us (3%)
    ppermute x15, starting transfers between devices, shifted(): lax.ppermute(array, axis, [(spots[k], spots[(k + by) % size]) for k in ra...  31.7 us
    pallas_call x13, Pallas kernels, call(): pl.pallas_call(kernel, out_shape=shapes, in_specs=smem(len(scalars)) + vm...  30.2 us
    ppermute x15, waiting for transfers between devices, shifted(): lax.ppermute(array, axis, [(spots[k], spots[(k + by) % size]) for k in ra...  27.6 us
    ppermute x14, starting transfers between devices, sent_across(): return lax.ppermute(array, PLANE, pairs)  19.7 us
    ppermute x14, waiting for transfers between devices, sent_across(): return lax.ppermute(array, PLANE, pairs)  14.8 us
    all_to_all x1, starting transfers between devices, program(): cross_rows = lax.all_to_all(crosses, spread, 0, 0, tiled=True)  12 us
    ppermute x7, waiting for transfers between devices, swapped(): return lax.ppermute(array, axes, pairs)  8.1 us
    ppermute x7, starting transfers between devices, swapped(): return lax.ppermute(array, axes, pairs)  4.43 us
  transfers between devices with their start and end apart: 37, of which 21 were waited for; matrix products, arithmetic and copies ran while one was open for 0% of the time, Pallas kernels for 15%

profile of v4, /device:TPU:2, one launch (start us, length us, event | category | flops | bytes accessed | tf_op | source)
XLA Modules:
  0.0 153.7 jit_solution(3019802815047151720)
XLA Ops:
  0.7 1.2 copy-done
  1.9 1.2 copy-done.2
  3.1 1.9 %shard_map.55 = (bf16[2,1024,512]{2,1,0:T(8,128)(2,1)S(1)}, f32[4,4,272,128]{3,2,1,0:T(8,128)S(1)}) custom-call(s32[6]{0:T(128)S(1)} %shift-right-arithmetic_and_fusion.at_ref, bf16[512,1024]{1,0:T(8,128)(2,1)S(1)} %copy-done, bf16[512,1024]{1,0:T(8,128)(2,1)S(1)} %copy-done.2), custom_call_target="tpu_custom_call" | custom-call | flops 536870912 | bytes 6422528 | tf_op jit(solution)/shard_map/pallas_call | solution.py:255
  5.2 1.4 shard_map.57
  7.1 1.4 shard_map.59.refs_0_
  8.5 1.0 collective-permute-done.4.refs_1_
  10.3 3.3 %collective-permute-start.5 = (f32[4,272,128]{2,1,0:T(8,128)S(1)}, f32[4,272,128]{2,1,0:T(8,128)S(1)}, u32[]{:S(2)}, u32[]{:S(2)}) collective-permute-start(f32[4,272,128]{2,1,0:T(8,128)S(1)} %get-tuple-element.39), channel_id=1, source_target_pairs={{0,1},{16,17},{1,0},{17,16},{2,3},{18,19},{3,2},{19,18},{4,5},{20,... | collective-permute-start | bytes 1671176 | tf_op jit(solution)/shard_map/ppermute | solution.py:275
  13.6 1.4 shard_map.56.refs_0_
  15.7 2.6 %collective-permute-start.7 = (f32[4,272,128]{2,1,0:T(8,128)S(1)}, f32[4,272,128]{2,1,0:T(8,128)S(1)}, u32[]{:S(2)}, u32[]{:S(2)}) collective-permute-start(f32[4,272,128]{2,1,0:T(8,128)S(1)} %get-tuple-element.41), channel_id=1, source_target_pairs={{0,17},{16,0},{1,16},{17,1},{2,19},{18,2},{3,18},{19,3},{4,21},{20... | collective-permute-start | bytes 1671176 | tf_op jit(solution)/shard_map/ppermute | solution.py:275
  19.0 2.2 %collective-permute-start.1 = (f32[4,272,128]{2,1,0:T(8,128)S(1)}, f32[4,272,128]{2,1,0:T(8,128)S(1)}, u32[]{:S(2)}, u32[]{:S(2)}) collective-permute-start(f32[4,272,128]{2,1,0:T(8,128)S(1)} %get-tuple-element.34), channel_id=1, source_target_pairs={{0,4},{2,6},{4,0},{6,2},{1,5},{3,7},{5,1},{7,3},{8,12},{10,14},{12... | collective-permute-start | bytes 1671176 | tf_op jit(solution)/shard_map/ppermute | solution.py:275
  21.3 6.1 %collective-permute-done.5.refs_5_ = f32[4,272,128]{2,1,0:T(8,128)S(1)} collective-permute-done((f32[4,272,128]{2,1,0:T(8,128)S(1)}, f32[4,272,128]{2,1,0:T(8,128)S(1)}, u32[]{:S(2)}, u32[]{:S(2)}) %collective-permute-start.5) | collective-permute-done | bytes 557088 | tf_op jit(solution)/shard_map/ppermute | solution.py:275
  27.4 2.3 %collective-permute-start.3 = (f32[4,272,128]{2,1,0:T(8,128)S(1)}, f32[4,272,128]{2,1,0:T(8,128)S(1)}, u32[]{:S(2)}, u32[]{:S(2)}) collective-permute-start(f32[4,272,128]{2,1,0:T(8,128)S(1)} %get-tuple-element.36), channel_id=1, source_target_pairs={{0,6},{2,0},{4,2},{6,4},{1,7},{3,1},{5,3},{7,5},{8,14},{10,8},{12,... | collective-permute-start | bytes 1671176 | tf_op jit(solution)/shard_map/ppermute | solution.py:275
  29.7 8.8 %collective-permute-done.6.refs_6_ = f32[4,272,128]{2,1,0:T(8,128)S(1)} collective-permute-done((f32[4,272,128]{2,1,0:T(8,128)S(1)}, f32[4,272,128]{2,1,0:T(8,128)S(1)}, u32[]{:S(2)}, u32[]{:S(2)}) %collective-permute-start.6) | collective-permute-done | bytes 557088 | tf_op jit(solution)/shard_map/ppermute | solution.py:275
  38.9 7.6 %collective-permute-done.2.refs_2_ = f32[4,272,128]{2,1,0:T(8,128)S(1)} collective-permute-done((f32[4,272,128]{2,1,0:T(8,128)S(1)}, f32[4,272,128]{2,1,0:T(8,128)S(1)}, u32[]{:S(2)}, u32[]{:S(2)}) %collective-permute-start.2) | collective-permute-done | bytes 557088 | tf_op jit(solution)/shard_map/ppermute | solution.py:275
  46.5 0.9 shard_map.61
  47.4 1.9 %collective-permute-start.10 = (f32[272,128]{1,0:T(8,128)S(1)}, f32[272,128]{1,0:T(8,128)S(1)}, u32[]{:S(2)}, u32[]{:S(2)}) collective-permute-start(f32[272,128]{1,0:T(8,128)S(1)} %get-tuple-element.45), channel_id=1, source_target_pairs={{0,38},{16,54},{1,39},{17,55},{2,32},{18,48},{3,33},{19,49},{4,34}... | collective-permute-start | bytes 417800 | tf_op jit(solution)/shard_map/ppermute | solution.py:288
  49.5 0.9 collective-permute-start.12
  50.9 2.7 %collective-permute-start.14 = (f32[272,128]{1,0:T(8,128)S(1)}, f32[272,128]{1,0:T(8,128)S(1)}, u32[]{:S(2)}, u32[]{:S(2)}) collective-permute-start(f32[272,128]{1,0:T(8,128)S(1)} %get-tuple-element.49), channel_id=1, source_target_pairs={{0,17},{16,0},{1,16},{17,1},{2,19},{18,2},{3,18},{19,3},{4,21},{20... | collective-permute-start | bytes 417800 | tf_op jit(solution)/shard_map/ppermute | solution.py:288
  53.6 1.3 collective-permute-done.10.refs_3_
  54.9 5.7 %collective-permute-start.8 = (f32[272,128]{1,0:T(8,128)S(1)}, f32[272,128]{1,0:T(8,128)S(1)}, u32[]{:S(2)}, u32[]{:S(2)}) collective-permute-start(f32[272,128]{1,0:T(8,128)S(1)} %get-tuple-element.43), channel_id=1, source_target_pairs={{0,36},{16,52},{1,37},{17,53},{2,38},{18,54},{3,39},{19,55},{4,32}... | collective-permute-start | bytes 417800 | tf_op jit(solution)/shard_map/ppermute | solution.py:288
  60.7 2.1 %collective-permute-done.14.refs_7_ = f32[272,128]{1,0:T(8,128)S(1)} collective-permute-done((f32[272,128]{1,0:T(8,128)S(1)}, f32[272,128]{1,0:T(8,128)S(1)}, u32[]{:S(2)}, u32[]{:S(2)}) %collective-permute-start.14) | collective-permute-done | bytes 139296 | tf_op jit(solution)/shard_map/ppermute | solution.py:288
  63.2 4.6 %collective-permute-done.9.refs_2_ = f32[272,128]{1,0:T(8,128)S(1)} collective-permute-done((f32[272,128]{1,0:T(8,128)S(1)}, f32[272,128]{1,0:T(8,128)S(1)}, u32[]{:S(2)}, u32[]{:S(2)}) %collective-permute-start.9) | collective-permute-done | bytes 139296 | tf_op jit(solution)/shard_map/ppermute | solution.py:288
  68.4 8.0 %collective-permute-start.15 = (f32[176,128]{1,0:T(8,128)S(1)}, f32[176,128]{1,0:T(8,128)S(1)}, u32[]{:S(2)}, u32[]{:S(2)}) collective-permute-start(f32[176,128]{1,0:T(8,128)S(1)} %get-tuple-element.51), channel_id=1, source_target_pairs={{0,128},{64,192},{128,0},{192,64},{1,129},{65,193},{129,1},{193,65... | collective-permute-start | bytes 270344 | tf_op jit(solution)/shard_map/ppermute | solution.py:275
  76.3 0.9 collective-permute-start.16
  77.3 3.2 %collective-permute-start.17 = (f32[176,128]{1,0:T(8,128)S(1)}, f32[176,128]{1,0:T(8,128)S(1)}, u32[]{:S(2)}, u32[]{:S(2)}) collective-permute-start(f32[176,128]{1,0:T(8,128)S(1)} %get-tuple-element.53), channel_id=1, source_target_pairs={{0,192},{64,0},{128,64},{192,128},{1,193},{65,1},{129,65},{193,129... | collective-permute-start | bytes 270344 | tf_op jit(solution)/shard_map/ppermute | solution.py:275
  80.5 2.5 %collective-permute-done.16.refs_2_ = f32[176,128]{1,0:T(8,128)S(1)} collective-permute-done((f32[176,128]{1,0:T(8,128)S(1)}, f32[176,128]{1,0:T(8,128)S(1)}, u32[]{:S(2)}, u32[]{:S(2)}) %collective-permute-start.16) | collective-permute-done | bytes 90144 | tf_op jit(solution)/shard_map/ppermute | solution.py:275
  83.7 3.1 %collective-permute-start.20 = (f32[144,128]{1,0:T(8,128)S(1)}, f32[144,128]{1,0:T(8,128)S(1)}, u32[]{:S(2)}, u32[]{:S(2)}) collective-permute-start(f32[144,128]{1,0:T(8,128)S(1)} %get-tuple-element.54.refs_0_), channel_id=1, source_target_pairs={{0,17},{16,0},{1,16},{17,1},{2,19},{18,2},{3,18},{19,3},{4,21},{20... | collective-permute-start | bytes 221192 | tf_op jit(solution)/shard_map/ppermute | solution.py:288
  87.6 1.6 %collective-permute-start.22 = (f32[144,128]{1,0:T(8,128)S(1)}, f32[144,128]{1,0:T(8,128)S(1)}, u32[]{:S(2)}, u32[]{:S(2)}) collective-permute-start(f32[144,128]{1,0:T(8,128)S(1)} %get-tuple-element.54.refs_0_), channel_id=1, source_target_pairs={{0,48},{16,33},{1,49},{17,32},{2,50},{18,35},{3,51},{19,34},{4,52}... | collective-permute-start | bytes 221192 | tf_op jit(solution)/shard_map/ppermute | solution.py:288
  90.0 1.3 collective-permute-start.23
  91.3 0.9 collective-permute-start.24
  92.1 1.4 collective-permute-done.22.refs_5_
  93.5 3.4 %collective-permute-done.23.refs_6_ = f32[144,128]{1,0:T(8,128)S(1)} collective-permute-done((f32[144,128]{1,0:T(8,128)S(1)}, f32[144,128]{1,0:T(8,128)S(1)}, u32[]{:S(2)}, u32[]{:S(2)}) %collective-permute-start.23) | collective-permute-done | bytes 73760 | tf_op jit(solution)/shard_map/ppermute | solution.py:288
  97.7 1.4 shard_map.64
  99.5 2.9 %collective-permute-start.26 = (f32[4,144,128]{2,1,0:T(8,128)S(1)}, f32[4,144,128]{2,1,0:T(8,128)S(1)}, u32[]{:S(2)}, u32[]{:S(2)}) collective-permute-start(f32[4,144,128]{2,1,0:T(8,128)S(1)} %get-tuple-element.56.refs_0_), channel_id=1, source_target_pairs={{0,4},{2,6},{4,0},{6,2},{1,5},{3,7},{5,1},{7,3},{8,12},{10,14},{12... | collective-permute-start | bytes 884744 | tf_op jit(solution)/shard_map/ppermute | solution.py:275
  102.5 2.4 %collective-permute-start.27 = (f32[4,144,128]{2,1,0:T(8,128)S(1)}, f32[4,144,128]{2,1,0:T(8,128)S(1)}, u32[]{:S(2)}, u32[]{:S(2)}) collective-permute-start(f32[4,144,128]{2,1,0:T(8,128)S(1)} %get-tuple-element.56.refs_0_), channel_id=1, source_target_pairs={{0,6},{2,0},{4,2},{6,4},{1,7},{3,1},{5,3},{7,5},{8,14},{10,8},{12,... | collective-permute-start | bytes 884744 | tf_op jit(solution)/shard_map/ppermute | solution.py:275
  104.8 2.1 %collective-permute-start.29 = (f32[4,144,128]{2,1,0:T(8,128)S(1)}, f32[4,144,128]{2,1,0:T(8,128)S(1)}, u32[]{:S(2)}, u32[]{:S(2)}) collective-permute-start(f32[4,144,128]{2,1,0:T(8,128)S(1)} %get-tuple-element.57.refs_4_), channel_id=1, source_target_pairs={{0,1},{16,17},{1,0},{17,16},{2,3},{18,19},{3,2},{19,18},{4,5},{20,... | collective-permute-start | bytes 884744 | tf_op jit(solution)/shard_map/ppermute | solution.py:275
  106.9 2.1 %collective-permute-done.25.refs_1_ = f32[4,144,128]{2,1,0:T(8,128)S(1)} collective-permute-done((f32[4,144,128]{2,1,0:T(8,128)S(1)}, f32[4,144,128]{2,1,0:T(8,128)S(1)}, u32[]{:S(2)}, u32[]{:S(2)}) %collective-permute-start.25) | collective-permute-done | bytes 294944 | tf_op jit(solution)/shard_map/ppermute | solution.py:275
  109.9 12.0 %all-to-all-start = ((f32[32,32,128]{2,1,0:T(8,128)}), f32[32,32,128]{2,1,0:T(8,128)S(1)}, u32[]{:S(2)}, u32[]{:S(2)}) async-start(f32[32,32,128]{2,1,0:T(8,128)} %get-tuple-element.58), calls=%async_computation | async-start | bytes 1048576 | tf_op jit(solution)/shard_map/all_to_all | solution.py:348
  122.6 1.0 copy-done.5
  123.6 16.8 %shard_map.65.mine_ref = f32[128,1024]{1,0:T(8,128)S(1)} custom-call(s32[6]{0:T(128)S(1)} %shift-right-arithmetic_and_fusion.at_ref, f32[2]{0:T(128)S(1)} %copy-done.6, f32[4,144,128]{2,1,0:T(8,128)S(1)} %get-tuple-element.56.refs_0_, f32[4,144,128]{2,1,0:T(8,128)S(1)} %collective-permute-done.25.refs_1_, ...), custom_call_target="tpu_custom_call" | custom-call | flops 11274289152 | bytes 2883584 | tf_op jit(solution)/shard_map/pallas_call | solution.py:255
  140.5 1.9 %collective-permute-done.31.other_ref = f32[128,1024]{1,0:T(8,128)S(1)} collective-permute-done((f32[128,1024]{1,0:T(8,128)S(1)}, f32[128,1024]{1,0:T(8,128)S(1)}, u32[]{:S(2)}, u32[]{:S(2)}) %collective-permute-start.31) | collective-permute-done | bytes 524320 | tf_op jit(solution)/shard_map/ppermute | solution.py:269
  142.4 0.9 shard_map.66.refs_0_
  143.3 1.5 collective-permute-start.32
  145.5 1.5 collective-permute-start.34
  147.7 1.6 %collective-permute-done.33.refs_2_ = f32[4,32,128]{2,1,0:T(8,128)S(1)} collective-permute-done((f32[4,32,128]{2,1,0:T(8,128)S(1)}, f32[4,32,128]{2,1,0:T(8,128)S(1)}, u32[]{:S(2)}, u32[]{:S(2)}) %collective-permute-start.33) | collective-permute-done | bytes 65568 | tf_op jit(solution)/shard_map/ppermute | solution.py:269
  149.3 1.3 collective-permute-done.34.refs_3_
  150.7 1.5 collective-permute-done.35.refs_4_
  152.3 1.4 shard_map.67
  (55 shorter events, 12.6 us)
Async XLA Ops:
  0.7 1.2 copy-start
  1.9 1.2 copy-start.2
  5.1 4.4 %collective-permute-start.4 = (f32[4,4,272,128]{3,2,1,0:T(8,128)S(1)}, f32[4,4,272,128]{3,2,1,0:T(8,128)S(1)}, u32[]{:S(2)}, u32[]{:S(2)}) collective-permute-start(f32[4,4,272,128]{3,2,1,0:T(8,128)S(1)} %get-tuple-element.37), channel_id=1, source_target_pairs={{0,8},{8,0},{1,9},{9,1},{2,10},{10,2},{3,11},{11,3},{4,12},{12,4},... | collective-permute-start | bytes 6684680 | tf_op jit(solution)/shard_map/ppermute | solution.py:269
  6.5 11.7 %collective-permute-start = (f32[4,4,272,128]{3,2,1,0:T(8,128)S(1)}, f32[4,4,272,128]{3,2,1,0:T(8,128)S(1)}, u32[]{:S(2)}, u32[]{:S(2)}) collective-permute-start(f32[4,4,272,128]{3,2,1,0:T(8,128)S(1)} %shard_map.57), channel_id=1, source_target_pairs={{0,8},{8,0},{1,9},{9,1},{2,10},{10,2},{3,11},{11,3},{4,12},{12,4},... | collective-permute-start | bytes 6684680 | tf_op jit(solution)/shard_map/ppermute | solution.py:269
  8.5 5.1 %copy-start.1 = (bf16[512,1024]{1,0:T(8,128)(2,1)S(1)}, bf16[512,1024]{1,0:T(8,128)(2,1)}, u32[]{:S(2)}) copy-start(bf16[512,1024]{1,0:T(8,128)(2,1)} %acts_ref.7) | copy-start | bytes 3145732
  8.5 5.1 %copy-start.3 = (bf16[512,1024]{1,0:T(8,128)(2,1)S(1)}, bf16[512,1024]{1,0:T(8,128)(2,1)}, u32[]{:S(2)}) copy-start(bf16[512,1024]{1,0:T(8,128)(2,1)} %grads_ref.7) | copy-start | bytes 3145732
  10.3 17.1 %collective-permute-start.5 = (f32[4,272,128]{2,1,0:T(8,128)S(1)}, f32[4,272,128]{2,1,0:T(8,128)S(1)}, u32[]{:S(2)}, u32[]{:S(2)}) collective-permute-start(f32[4,272,128]{2,1,0:T(8,128)S(1)} %get-tuple-element.39), channel_id=1, source_target_pairs={{0,1},{16,17},{1,0},{17,16},{2,3},{18,19},{3,2},{19,18},{4,5},{20,... | collective-permute-start | bytes 1671176 | tf_op jit(solution)/shard_map/ppermute | solution.py:275
  14.9 23.5 %collective-permute-start.6 = (f32[4,272,128]{2,1,0:T(8,128)S(1)}, f32[4,272,128]{2,1,0:T(8,128)S(1)}, u32[]{:S(2)}, u32[]{:S(2)}) collective-permute-start(f32[4,272,128]{2,1,0:T(8,128)S(1)} %get-tuple-element.40), channel_id=1, source_target_pairs={{0,16},{16,1},{1,17},{17,0},{2,18},{18,3},{3,19},{19,2},{4,20},{20... | collective-permute-start | bytes 1671176 | tf_op jit(solution)/shard_map/ppermute | solution.py:275
  15.7 23.2 %collective-permute-start.7 = (f32[4,272,128]{2,1,0:T(8,128)S(1)}, f32[4,272,128]{2,1,0:T(8,128)S(1)}, u32[]{:S(2)}, u32[]{:S(2)}) collective-permute-start(f32[4,272,128]{2,1,0:T(8,128)S(1)} %get-tuple-element.41), channel_id=1, source_target_pairs={{0,17},{16,0},{1,16},{17,1},{2,19},{18,2},{3,18},{19,3},{4,21},{20... | collective-permute-start | bytes 1671176 | tf_op jit(solution)/shard_map/ppermute | solution.py:275
  19.0 19.8 %collective-permute-start.1 = (f32[4,272,128]{2,1,0:T(8,128)S(1)}, f32[4,272,128]{2,1,0:T(8,128)S(1)}, u32[]{:S(2)}, u32[]{:S(2)}) collective-permute-start(f32[4,272,128]{2,1,0:T(8,128)S(1)} %get-tuple-element.34), channel_id=1, source_target_pairs={{0,4},{2,6},{4,0},{6,2},{1,5},{3,7},{5,1},{7,3},{8,12},{10,14},{12... | collective-permute-start | bytes 1671176 | tf_op jit(solution)/shard_map/ppermute | solution.py:275
  21.2 25.2 %collective-permute-start.2 = (f32[4,272,128]{2,1,0:T(8,128)S(1)}, f32[4,272,128]{2,1,0:T(8,128)S(1)}, u32[]{:S(2)}, u32[]{:S(2)}) collective-permute-start(f32[4,272,128]{2,1,0:T(8,128)S(1)} %get-tuple-element.35), channel_id=1, source_target_pairs={{0,2},{2,4},{4,6},{6,0},{1,3},{3,5},{5,7},{7,1},{8,10},{10,12},{12... | collective-permute-start | bytes 1671176 | tf_op jit(solution)/shard_map/ppermute | solution.py:275
  27.4 19.1 %collective-permute-start.3 = (f32[4,272,128]{2,1,0:T(8,128)S(1)}, f32[4,272,128]{2,1,0:T(8,128)S(1)}, u32[]{:S(2)}, u32[]{:S(2)}) collective-permute-start(f32[4,272,128]{2,1,0:T(8,128)S(1)} %get-tuple-element.36), channel_id=1, source_target_pairs={{0,6},{2,0},{4,2},{6,4},{1,7},{3,1},{5,3},{7,5},{8,14},{10,8},{12,... | collective-permute-start | bytes 1671176 | tf_op jit(solution)/shard_map/ppermute | solution.py:275
  47.3 75.3 %copy-start.6 = (f32[2]{0:T(128)S(1)}, f32[2]{0:T(128)}, u32[]{:S(2)}) copy-start(f32[2]{0:T(128)} %damp_ref.1) | copy-start | bytes 28
  47.4 7.5 %collective-permute-start.10 = (f32[272,128]{1,0:T(8,128)S(1)}, f32[272,128]{1,0:T(8,128)S(1)}, u32[]{:S(2)}, u32[]{:S(2)}) collective-permute-start(f32[272,128]{1,0:T(8,128)S(1)} %get-tuple-element.45), channel_id=1, source_target_pairs={{0,38},{16,54},{1,39},{17,55},{2,32},{18,48},{3,33},{19,49},{4,34}... | collective-permute-start | bytes 417800 | tf_op jit(solution)/shard_map/ppermute | solution.py:288
  49.3 11.3 %collective-permute-start.11 = (f32[272,128]{1,0:T(8,128)S(1)}, f32[272,128]{1,0:T(8,128)S(1)}, u32[]{:S(2)}, u32[]{:S(2)}) collective-permute-start(f32[272,128]{1,0:T(8,128)S(1)} %get-tuple-element.46), channel_id=1, source_target_pairs={{0,32},{16,48},{1,33},{17,49},{2,34},{18,50},{3,35},{19,51},{4,36}... | collective-permute-start | bytes 417800 | tf_op jit(solution)/shard_map/ppermute | solution.py:288
  49.5 11.1 %collective-permute-start.12 = (f32[272,128]{1,0:T(8,128)S(1)}, f32[272,128]{1,0:T(8,128)S(1)}, u32[]{:S(2)}, u32[]{:S(2)}) collective-permute-start(f32[272,128]{1,0:T(8,128)S(1)} %get-tuple-element.47), channel_id=1, source_target_pairs={{0,1},{16,17},{1,0},{17,16},{2,3},{18,19},{3,2},{19,18},{4,5},{20,... | collective-permute-start | bytes 417800 | tf_op jit(solution)/shard_map/ppermute | solution.py:288
  50.3 10.3 %collective-permute-start.13 = (f32[272,128]{1,0:T(8,128)S(1)}, f32[272,128]{1,0:T(8,128)S(1)}, u32[]{:S(2)}, u32[]{:S(2)}) collective-permute-start(f32[272,128]{1,0:T(8,128)S(1)} %get-tuple-element.48), channel_id=1, source_target_pairs={{0,16},{16,1},{1,17},{17,0},{2,18},{18,3},{3,19},{19,2},{4,20},{20... | collective-permute-start | bytes 417800 | tf_op jit(solution)/shard_map/ppermute | solution.py:288
  50.9 11.9 %collective-permute-start.14 = (f32[272,128]{1,0:T(8,128)S(1)}, f32[272,128]{1,0:T(8,128)S(1)}, u32[]{:S(2)}, u32[]{:S(2)}) collective-permute-start(f32[272,128]{1,0:T(8,128)S(1)} %get-tuple-element.49), channel_id=1, source_target_pairs={{0,17},{16,0},{1,16},{17,1},{2,19},{18,2},{3,18},{19,3},{4,21},{20... | collective-permute-start | bytes 417800 | tf_op jit(solution)/shard_map/ppermute | solution.py:288
  54.9 8.3 %collective-permute-start.8 = (f32[272,128]{1,0:T(8,128)S(1)}, f32[272,128]{1,0:T(8,128)S(1)}, u32[]{:S(2)}, u32[]{:S(2)}) collective-permute-start(f32[272,128]{1,0:T(8,128)S(1)} %get-tuple-element.43), channel_id=1, source_target_pairs={{0,36},{16,52},{1,37},{17,53},{2,38},{18,54},{3,39},{19,55},{4,32}... | collective-permute-start | bytes 417800 | tf_op jit(solution)/shard_map/ppermute | solution.py:288
  60.6 7.2 %collective-permute-start.9 = (f32[272,128]{1,0:T(8,128)S(1)}, f32[272,128]{1,0:T(8,128)S(1)}, u32[]{:S(2)}, u32[]{:S(2)}) collective-permute-start(f32[272,128]{1,0:T(8,128)S(1)} %get-tuple-element.44), channel_id=1, source_target_pairs={{0,34},{16,50},{1,35},{17,51},{2,36},{18,52},{3,37},{19,53},{4,38}... | collective-permute-start | bytes 417800 | tf_op jit(solution)/shard_map/ppermute | solution.py:288
  68.4 12.1 %collective-permute-start.15 = (f32[176,128]{1,0:T(8,128)S(1)}, f32[176,128]{1,0:T(8,128)S(1)}, u32[]{:S(2)}, u32[]{:S(2)}) collective-permute-start(f32[176,128]{1,0:T(8,128)S(1)} %get-tuple-element.51), channel_id=1, source_target_pairs={{0,128},{64,192},{128,0},{192,64},{1,129},{65,193},{129,1},{193,65... | collective-permute-start | bytes 270344 | tf_op jit(solution)/shard_map/ppermute | solution.py:275
  76.3 6.6 %collective-permute-start.16 = (f32[176,128]{1,0:T(8,128)S(1)}, f32[176,128]{1,0:T(8,128)S(1)}, u32[]{:S(2)}, u32[]{:S(2)}) collective-permute-start(f32[176,128]{1,0:T(8,128)S(1)} %get-tuple-element.52), channel_id=1, source_target_pairs={{0,64},{64,128},{128,192},{192,0},{1,65},{65,129},{129,193},{193,1... | collective-permute-start | bytes 270344 | tf_op jit(solution)/shard_map/ppermute | solution.py:275
  77.3 5.7 %collective-permute-start.17 = (f32[176,128]{1,0:T(8,128)S(1)}, f32[176,128]{1,0:T(8,128)S(1)}, u32[]{:S(2)}, u32[]{:S(2)}) collective-permute-start(f32[176,128]{1,0:T(8,128)S(1)} %get-tuple-element.53), channel_id=1, source_target_pairs={{0,192},{64,0},{128,64},{192,128},{1,193},{65,1},{129,65},{193,129... | collective-permute-start | bytes 270344 | tf_op jit(solution)/shard_map/ppermute | solution.py:275
  83.5 6.4 %collective-permute-start.18 = (f32[144,128]{1,0:T(8,128)S(1)}, f32[144,128]{1,0:T(8,128)S(1)}, u32[]{:S(2)}, u32[]{:S(2)}) collective-permute-start(f32[144,128]{1,0:T(8,128)S(1)} %get-tuple-element.54.refs_0_), channel_id=1, source_target_pairs={{0,16},{16,1},{1,17},{17,0},{2,18},{18,3},{3,19},{19,2},{4,20},{20... | collective-permute-start | bytes 221192 | tf_op jit(solution)/shard_map/ppermute | solution.py:288
  83.6 7.6 %collective-permute-start.19 = (f32[144,128]{1,0:T(8,128)S(1)}, f32[144,128]{1,0:T(8,128)S(1)}, u32[]{:S(2)}, u32[]{:S(2)}) collective-permute-start(f32[144,128]{1,0:T(8,128)S(1)} %get-tuple-element.54.refs_0_), channel_id=1, source_target_pairs={{0,1},{16,17},{1,0},{17,16},{2,3},{18,19},{3,2},{19,18},{4,5},{20,... | collective-permute-start | bytes 221192 | tf_op jit(solution)/shard_map/ppermute | solution.py:288
  83.7 8.4 %collective-permute-start.20 = (f32[144,128]{1,0:T(8,128)S(1)}, f32[144,128]{1,0:T(8,128)S(1)}, u32[]{:S(2)}, u32[]{:S(2)}) collective-permute-start(f32[144,128]{1,0:T(8,128)S(1)} %get-tuple-element.54.refs_0_), channel_id=1, source_target_pairs={{0,17},{16,0},{1,16},{17,1},{2,19},{18,2},{3,18},{19,3},{4,21},{20... | collective-permute-start | bytes 221192 | tf_op jit(solution)/shard_map/ppermute | solution.py:288
  86.9 5.3 %collective-permute-start.21 = (f32[144,128]{1,0:T(8,128)S(1)}, f32[144,128]{1,0:T(8,128)S(1)}, u32[]{:S(2)}, u32[]{:S(2)}) collective-permute-start(f32[144,128]{1,0:T(8,128)S(1)} %get-tuple-element.54.refs_0_), channel_id=1, source_target_pairs={{0,32},{16,48},{1,33},{17,49},{2,34},{18,50},{3,35},{19,51},{4,36}... | collective-permute-start | bytes 221192 | tf_op jit(solution)/shard_map/ppermute | solution.py:288
  87.6 5.9 %collective-permute-start.22 = (f32[144,128]{1,0:T(8,128)S(1)}, f32[144,128]{1,0:T(8,128)S(1)}, u32[]{:S(2)}, u32[]{:S(2)}) collective-permute-start(f32[144,128]{1,0:T(8,128)S(1)} %get-tuple-element.54.refs_0_), channel_id=1, source_target_pairs={{0,48},{16,33},{1,49},{17,32},{2,50},{18,35},{3,51},{19,34},{4,52}... | collective-permute-start | bytes 221192 | tf_op jit(solution)/shard_map/ppermute | solution.py:288
  90.0 7.0 %collective-permute-start.23 = (f32[144,128]{1,0:T(8,128)S(1)}, f32[144,128]{1,0:T(8,128)S(1)}, u32[]{:S(2)}, u32[]{:S(2)}) collective-permute-start(f32[144,128]{1,0:T(8,128)S(1)} %get-tuple-element.54.refs_0_), channel_id=1, source_target_pairs={{0,33},{16,49},{1,32},{17,48},{2,35},{18,51},{3,34},{19,50},{4,37}... | collective-permute-start | bytes 221192 | tf_op jit(solution)/shard_map/ppermute | solution.py:288
  91.3 6.5 %collective-permute-start.24 = (f32[144,128]{1,0:T(8,128)S(1)}, f32[144,128]{1,0:T(8,128)S(1)}, u32[]{:S(2)}, u32[]{:S(2)}) collective-permute-start(f32[144,128]{1,0:T(8,128)S(1)} %get-tuple-element.54.refs_0_), channel_id=1, source_target_pairs={{0,49},{16,32},{1,48},{17,33},{2,51},{18,34},{3,50},{19,35},{4,53}... | collective-permute-start | bytes 221192 | tf_op jit(solution)/shard_map/ppermute | solution.py:288
  99.2 9.9 %collective-permute-start.25 = (f32[4,144,128]{2,1,0:T(8,128)S(1)}, f32[4,144,128]{2,1,0:T(8,128)S(1)}, u32[]{:S(2)}, u32[]{:S(2)}) collective-permute-start(f32[4,144,128]{2,1,0:T(8,128)S(1)} %get-tuple-element.56.refs_0_), channel_id=1, source_target_pairs={{0,2},{2,4},{4,6},{6,0},{1,3},{3,5},{5,7},{7,1},{8,10},{10,12},{12... | collective-permute-start | bytes 884744 | tf_op jit(solution)/shard_map/ppermute | solution.py:275
  99.5 22.3 %collective-permute-start.26 = (f32[4,144,128]{2,1,0:T(8,128)S(1)}, f32[4,144,128]{2,1,0:T(8,128)S(1)}, u32[]{:S(2)}, u32[]{:S(2)}) collective-permute-start(f32[4,144,128]{2,1,0:T(8,128)S(1)} %get-tuple-element.56.refs_0_), channel_id=1, source_target_pairs={{0,4},{2,6},{4,0},{6,2},{1,5},{3,7},{5,1},{7,3},{8,12},{10,14},{12... | collective-permute-start | bytes 884744 | tf_op jit(solution)/shard_map/ppermute | solution.py:275
  102.5 19.4 %collective-permute-start.27 = (f32[4,144,128]{2,1,0:T(8,128)S(1)}, f32[4,144,128]{2,1,0:T(8,128)S(1)}, u32[]{:S(2)}, u32[]{:S(2)}) collective-permute-start(f32[4,144,128]{2,1,0:T(8,128)S(1)} %get-tuple-element.56.refs_0_), channel_id=1, source_target_pairs={{0,6},{2,0},{4,2},{6,4},{1,7},{3,1},{5,3},{7,5},{8,14},{10,8},{12,... | collective-permute-start | bytes 884744 | tf_op jit(solution)/shard_map/ppermute | solution.py:275
  104.8 17.0 %collective-permute-start.28 = (f32[4,144,128]{2,1,0:T(8,128)S(1)}, f32[4,144,128]{2,1,0:T(8,128)S(1)}, u32[]{:S(2)}, u32[]{:S(2)}) collective-permute-start(f32[4,144,128]{2,1,0:T(8,128)S(1)} %get-tuple-element.57.refs_4_), channel_id=1, source_target_pairs={{0,16},{16,1},{1,17},{17,0},{2,18},{18,3},{3,19},{19,2},{4,20},{20... | collective-permute-start | bytes 884744 | tf_op jit(solution)/shard_map/ppermute | solution.py:275
  104.8 17.0 %collective-permute-start.29 = (f32[4,144,128]{2,1,0:T(8,128)S(1)}, f32[4,144,128]{2,1,0:T(8,128)S(1)}, u32[]{:S(2)}, u32[]{:S(2)}) collective-permute-start(f32[4,144,128]{2,1,0:T(8,128)S(1)} %get-tuple-element.57.refs_4_), channel_id=1, source_target_pairs={{0,1},{16,17},{1,0},{17,16},{2,3},{18,19},{3,2},{19,18},{4,5},{20,... | collective-permute-start | bytes 884744 | tf_op jit(solution)/shard_map/ppermute | solution.py:275
  109.0 12.8 %collective-permute-start.30 = (f32[4,144,128]{2,1,0:T(8,128)S(1)}, f32[4,144,128]{2,1,0:T(8,128)S(1)}, u32[]{:S(2)}, u32[]{:S(2)}) collective-permute-start(f32[4,144,128]{2,1,0:T(8,128)S(1)} %get-tuple-element.57.refs_4_), channel_id=1, source_target_pairs={{0,17},{16,0},{1,16},{17,1},{2,19},{18,2},{3,18},{19,3},{4,21},{20... | collective-permute-start | bytes 884744 | tf_op jit(solution)/shard_map/ppermute | solution.py:275
  109.9 32.5 %all-to-all-start = ((f32[32,32,128]{2,1,0:T(8,128)}), f32[32,32,128]{2,1,0:T(8,128)S(1)}, u32[]{:S(2)}, u32[]{:S(2)}) async-start(f32[32,32,128]{2,1,0:T(8,128)} %get-tuple-element.58), calls=%async_computation | async-start | bytes 1048576 | tf_op jit(solution)/shard_map/all_to_all | solution.py:348
  121.9 0.7 copy-start.4
  122.6 1.0 copy-start.5
  140.4 2.0 %collective-permute-start.31 = (f32[128,1024]{1,0:T(8,128)S(1)}, f32[128,1024]{1,0:T(8,128)S(1)}, u32[]{:S(2)}, u32[]{:S(2)}) collective-permute-start(f32[128,1024]{1,0:T(8,128)S(1)} %shard_map.65.mine_ref), channel_id=1, source_target_pairs={{0,8},{8,0},{1,9},{9,1},{2,10},{10,2},{3,11},{11,3},{4,12},{12,4},... | collective-permute-start | bytes 1572872 | tf_op jit(solution)/shard_map/ppermute | solution.py:269
  143.3 4.4 %collective-permute-start.32 = (f32[4,32,128]{2,1,0:T(8,128)S(1)}, f32[4,32,128]{2,1,0:T(8,128)S(1)}, u32[]{:S(2)}, u32[]{:S(2)}) collective-permute-start(f32[4,32,128]{2,1,0:T(8,128)S(1)} %shard_map.66.refs_0_), channel_id=1, source_target_pairs={{0,16},{16,0},{1,17},{17,1},{2,18},{18,2},{3,19},{19,3},{4,20},{20... | collective-permute-start | bytes 196616 | tf_op jit(solution)/shard_map/ppermute | solution.py:269
  144.8 4.5 %collective-permute-start.33 = (f32[4,32,128]{2,1,0:T(8,128)S(1)}, f32[4,32,128]{2,1,0:T(8,128)S(1)}, u32[]{:S(2)}, u32[]{:S(2)}) collective-permute-start(f32[4,32,128]{2,1,0:T(8,128)S(1)} %shard_map.66.refs_0_), channel_id=1, source_target_pairs={{0,32},{32,0},{1,33},{33,1},{2,34},{34,2},{3,35},{35,3},{4,36},{36... | collective-permute-start | bytes 196616 | tf_op jit(solution)/shard_map/ppermute | solution.py:269
  145.5 5.2 %collective-permute-start.34 = (f32[4,32,128]{2,1,0:T(8,128)S(1)}, f32[4,32,128]{2,1,0:T(8,128)S(1)}, u32[]{:S(2)}, u32[]{:S(2)}) collective-permute-start(f32[4,32,128]{2,1,0:T(8,128)S(1)} %shard_map.66.refs_0_), channel_id=1, source_target_pairs={{0,48},{16,32},{32,16},{48,0},{1,49},{17,33},{33,17},{49,1},{2,50}... | collective-permute-start | bytes 196616 | tf_op jit(solution)/shard_map/ppermute | solution.py:269
  150.6 1.6 %collective-permute-start.35 = (f32[4,4,32,128]{3,2,1,0:T(8,128)S(1)}, f32[4,4,32,128]{3,2,1,0:T(8,128)S(1)}, u32[]{:S(2)}, u32[]{:S(2)}) collective-permute-start(f32[4,4,32,128]{3,2,1,0:T(8,128)S(1)} %pad_maximum_fusion), channel_id=1, source_target_pairs={{0,8},{8,0},{1,9},{9,1},{2,10},{10,2},{3,11},{11,3},{4,12},{12,4},... | collective-permute-start | bytes 786440 | tf_op jit(solution)/shard_map/ppermute | solution.py:269

commit v5 on v4

--- a/solution.py
+++ b/solution.py
@@ -40,14 +40,11 @@
     return jnp.dot(a, b, preferred_element_type=F32)
 
 
-def gram_terms(nb, colour, which, core, acts_ref, grads_ref, t_ref, out):
+def factor_terms(nb, colour, which, core, acts_ref, grads_ref, t_ref, out):
     part = nb * (nb + 1) // 2 * B // 2
-    piece = part // 16
-    strip = nb * B // 4
-    rows = (out.shape[2] - piece) // 4
-    grads = grads_ref[...]
+    piece = out.shape[2]
     slot = core if which else 1 - core
-    right = jnp.where(slot == 0, acts_ref[...], grads)
+    right = jnp.where(slot == 0, acts_ref[...], grads_ref[...])
     for jj in range(nb // 2):
         spans = []
         for j in (2 * jj, 2 * jj + 1):
@@ -64,79 +61,100 @@
             for q, r, at, n in sub_segments(lo - colour * part, hi - lo, piece):
                 at = first - low + at
                 out[q // 4, q % 4, r : r + n, :] = res[at : at + n, lane : lane + B]
-    begin = pl.multiple_of(slot * 2 * strip + colour * strip, strip)
-    left = t_ref[0, pl.ds(begin, strip), :]
+
+
+def factor_kernel(nb, colour, which, at_ref, acts_ref, grads_ref, t_ref, out_ref):
+    factor_terms(nb, colour, which, at_ref[CORE], acts_ref, grads_ref, t_ref, out_ref)
+
+
+def cross_kernel(nb, which, at_ref, grads_ref, t_ref, out):
+    core = at_ref[CORE]
+    slot = core if which else 1 - core
+    half = nb * B // 2
+    _, _, nz, rows, _ = out.shape
+    left = t_ref[0, pl.ds(pl.multiple_of(slot * half, half), half), :]
     for x in range(nb // 2):
-        res = dot(left, grads[:, x * 2 * B : (x + 1) * 2 * B])
-        for s in range(strip // rows):
-            zh, yl = divmod(s, 2)
+        res = dot(left, grads_ref[:, x * 2 * B : (x + 1) * 2 * B])
+        for s in range(half // rows):
+            zl, rest = divmod(s, nz * 2)
+            zh, yl = divmod(rest, 2)
             for yh in range(2):
-                y = yh * 2 + yl
-                first, second = (y, x) if colour else (x, y)
-                at = piece + zh * rows
-                out[first, second, at : at + rows, :] = res[s * rows : s * rows + rows, yh * B : yh * B + B]
-
-
-def gram_kernel(nb, colour, which, at_ref, acts_ref, grads_ref, t_ref, out_ref):
-    gram_terms(nb, colour, which, at_ref[CORE], acts_ref, grads_ref, t_ref, out_ref)
+                block = res[s * rows : s * rows + rows, yh * B : yh * B + B]
+                out[zl, (yl * (nb // 2) + x) * 2 + yh, zh, :, :] = block
 
 
 def first_kernel(nb, colour, at_ref, acts_ref, grads_ref, t_ref, out_ref):
     t_ref[0] = acts_ref[...].T
     t_ref[1] = grads_ref[...].T
-    gram_terms(nb, colour, 0, at_ref[CORE], acts_ref, grads_ref, t_ref, out_ref)
-
-
-def turned_kernel(count, colour, at_ref, *refs):
+    factor_terms(nb, colour, 0, at_ref[CORE], acts_ref, grads_ref, t_ref, out_ref)
+
+
+def turned_kernel(count, axis, at_ref, *refs):
     ins, outs = refs[:count], refs[count:]
     for k, out in enumerate(outs):
-        z = lax.rem(ring_places(at_ref)[colour] + k, len(outs))
-        total = ins[0][z]
+        z = lax.rem(ring_places(at_ref)[axis] + k, len(outs))
+
+        def add(i, out=out, z=z):
+            total = ins[0][z, i]
+            for ref in ins[1:]:
+                total = total + ref[z, i]
+            out[i] = total
+
+        if out.ndim == 3:
+            pl.loop(0, out.shape[0])(add)
+        else:
+            total = ins[0][z]
+            for ref in ins[1:]:
+                total = total + ref[z]
+            out[...] = total
+
+
+def parted_kernel(at_ref, kept_ref, came_ref, keep_ref, send_ref):
+    zl = at_ref[ZL]
+
+    @pl.loop(0, keep_ref.shape[0])
+    def _(i):
+        keep_ref[i] = kept_ref[zl, i] + came_ref[zl, i]
+        send_ref[i] = kept_ref[1 - zl, i] + came_ref[1 - zl, i]
+
+
+def halves_kernel(at_ref, *refs):
+    keep_ref, send_ref = refs[-2:]
+    sums = []
+    for ins in (refs[:4], refs[4:8]):
+        total = ins[0][...]
         for ref in ins[1:]:
-            total = total + ref[z]
-        out[...] = total
-
-
-def sorted_kernel(at_ref, *refs):
-    ins, outs = refs[:8], refs[8:]
+            total = total + ref[...]
+        sums.append(total)
     low = at_ref[ZL] == 0
-    x, y = ring_places(at_ref)
-    for k in range(4):
-        sums = []
-        for colour in range(2):
-            z = lax.rem((y, x)[colour] + k, 4)
-            total = ins[colour * 4][z]
-            for ref in ins[colour * 4 + 1 : colour * 4 + 4]:
-                total = total + ref[z]
-            sums.append(total)
-        outs[k][...] = jnp.where(low, sums[0], sums[1])
-        outs[4 + k][...] = jnp.where(low, sums[1], sums[0])
-
-
-def ring_kernel(piece, at_ref, *refs):
-    ins, outs, sum_ref = refs[:8], refs[8:-1], refs[-1]
-    total = ins[0][...]
-    for ref in ins[1:]:
+    keep_ref[...] = jnp.where(low, sums[0], sums[1])
+    send_ref[...] = jnp.where(low, sums[1], sums[0])
+
+
+def plus_kernel(a_ref, b_ref, out_ref):
+    @pl.loop(0, out_ref.shape[0])
+    def _(i):
+        out_ref[i] = a_ref[i] + b_ref[i]
+
+
+def total_kernel(*refs):
+    total = refs[0][...]
+    for ref in refs[1:-1]:
         total = total + ref[...]
+    refs[-1][...] = total
+
+
+def summed_kernel(at_ref, pieces_ref, *refs):
+    outs, sum_ref = refs[:-1], refs[-1]
+    total = pieces_ref[0]
+    for q in range(1, pieces_ref.shape[0]):
+        total = total + pieces_ref[q]
     sum_ref[...] = total
-    rows = outs[0].shape[0] - piece
     for k, out in enumerate(outs):
-        z = lax.rem(at_ref[ZH] + k, len(outs))
-        out[:piece, :] = sum_ref[:piece, :]
-        out[piece:, :] = sum_ref[pl.ds(pl.multiple_of(piece + z * rows, 8), rows), :]
-
-
-def total_kernel(scale, at_ref, *refs):
-    factor_ref, cross_ref = refs[-2:]
-    total = refs[0][...]
-    for ref in refs[1:-2]:
-        total = total + ref[...]
-    piece = factor_ref.shape[0]
-    factor_ref[...] = total[:piece]
-    cross_ref[...] = total[piece:] * scale
-
-
-def joined_kernel(at_ref, *refs):
+        out[...] = sum_ref[lax.rem(at_ref[ZH] + k, len(outs))]
+
+
+def joined_kernel(scale, at_ref, *refs):
     outs = refs[-3:]
     low = at_ref[ZL] == 0
     for k in range(4):
@@ -144,6 +162,9 @@
         outs[0][k] = jnp.where(low, own, other)
         outs[1][k] = jnp.where(low, other, own)
     cross = refs[8][...]
+    for ref in refs[9:-3]:
+        cross = cross + ref[...]
+    cross = cross * scale
     for q in range(outs[2].shape[0]):
         outs[2][q] = cross
 
@@ -249,19 +270,25 @@
     return [pl.BlockSpec(memory_space=pltpu.SMEM)] * n
 
 
-def call(kernel, scalars, arrays, outs, scratch=(), flops=0, limit=20):
+def call(kernel, scalars, arrays, outs, scratch=(), flops=0, limit=20, after=()):
+    if after:
+        count, inner = len(scalars) + len(arrays), kernel
+
+        def kernel(*refs):
+            inner(*refs[:count], *refs[count + len(after) :])
+
     shapes = [o if hasattr(o, "dtype") else jax.ShapeDtypeStruct(o, F32) for o in outs]
     moved = sum(math.prod(a.shape) * a.dtype.itemsize for a in [*arrays, *shapes])
     return pl.pallas_call(
         kernel,
         out_shape=shapes,
-        in_specs=smem(len(scalars)) + vmem(len(arrays)),
+        in_specs=smem(len(scalars)) + vmem(len(arrays)) + [pl.BlockSpec(memory_space=pl.ANY)] * len(after),
         out_specs=vmem(len(outs)),
         scratch_shapes=list(scratch),
         cost_estimate=pl.CostEstimate(flops=flops, bytes_accessed=moved, transcendentals=0),
         compiler_params=pltpu.CompilerParams(vmem_limit_bytes=limit << 20),
         interpret=INTERPRET,
-    )(*scalars, *arrays)
+    )(*scalars, *arrays, *after)
 
 
 def swapped(array, axes):
@@ -300,44 +327,62 @@
     rings = ("x", Y)
     piece = nb * (nb + 1) // 2 * B // 32
     rows = width // lax.axis_size(DP)
-    chunk = (piece + nz * rows, B)
-
-    terms = (4, 4, *chunk)
+    chunk = (piece, B)
     gram_flops = tokens * width * width
     transposed, sent1 = call(
         functools.partial(first_kernel, nb, 1), [at], [acts, grads],
-        [jax.ShapeDtypeStruct((2, width, tokens), BF16), terms], flops=gram_flops,
+        [jax.ShapeDtypeStruct((2, width, tokens), BF16), (4, 4, *chunk)], flops=gram_flops,
     )
 
-    def grams(colour, which):
-        kernel = functools.partial(gram_kernel, nb, colour, which)
-        return call(kernel, [at], [acts, grads, transposed], [terms], flops=gram_flops)[0]
-
-    sent0 = grams(0, 0)
+    def factors(colour, which):
+        kernel = functools.partial(factor_kernel, nb, colour, which)
+        arrays = [acts, grads, transposed]
+        return call(kernel, [at], arrays, [(4, 4, *chunk)], flops=gram_flops // 2)[0]
+
+    def crosses_of(which, after):
+        shape = (2, 16, nz, rows, B)
+        kernel = functools.partial(cross_kernel, nb, which)
+        return call(kernel, [at], [grads, transposed], [shape], flops=gram_flops, after=after)[0]
+
+    sent0 = factors(0, 0)
     came = []
     for sent in (sent0, sent1):
         came.append(swapped(sent, "c"))
-    far = []
-    for colour in (0, 1):
-        ring = rings[colour]
-        kept = grams(colour, 1)
-        turned = call(functools.partial(turned_kernel, 2, colour), [at], [kept, came[colour]], [(4, *chunk)] * 4)
-        far += [turned[0]] + [shifted(turned[k], ring, k) for k in (2, 1, 3)]
-    sides = call(sorted_kernel, [at], far, [chunk] * 8)
-    summands = [sides[0]]
-    summands += [sent_across(sides[4 + k], k, 1, 1) for k in (2, 1, 3, 0)]
-    summands += [sent_across(sides[k], k, 0, 0) for k in (2, 1, 3)]
-    turned = call(
-        functools.partial(ring_kernel, piece), [at], summands, [(piece + rows, B)] * nz,
-        [pltpu.VMEM(chunk, F32)],
-    )
-    around = [turned[0]] + [shifted(turned[k], "zh", k) for k in (2, 1, 3)]
-    mine, cross = call(functools.partial(total_kernel, scale), [at], around, [(piece, B), (rows, B)])
+    near = []
+    for colour in range(2):
+        near.append([factors(colour, 1), came[colour]])
+    sent2 = crosses_of(0, [near[0][0], near[1][0]])
+    cross_came = swapped(sent2, "c")
+    for depth in range(2):
+        far = []
+        for colour in range(2):
+            axis = depth ^ colour
+            turned = call(
+                functools.partial(turned_kernel, len(near[colour]), axis), [at],
+                near[colour], [chunk if depth else (4, *chunk)] * 4,
+            )
+            far.append([turned[0]] + [shifted(turned[k], rings[axis], k) for k in (2, 1, 3)])
+        near = far
+        if depth == 0:
+            begun = [near[0][0], near[1][0]]
+    cross_kept = crosses_of(1, begun)
+    cross_keep, cross_send = call(parted_kernel, [at], [cross_kept, cross_came], [(16, nz, rows, B)] * 2)
+    cross_came = swapped(cross_send, "zl")
+    keep, send = call(halves_kernel, [at], near[0] + near[1], [chunk] * 2)
+    arrived = swapped(send, "zl")
+    (cross_half,) = call(plus_kernel, [], [cross_keep, cross_came], [(16, nz, rows, B)], after=[send])
+    cross_pieces = lax.all_to_all(cross_half, PLANE[1:], 0, 0, tiled=True)
+    (half,) = call(total_kernel, [], [keep, arrived], [chunk])
+    around = [half] + [shifted(half, "zh", k) for k in (2, 1, 3)]
+    (mine,) = call(total_kernel, [], around, [chunk])
+    turned = call(summed_kernel, [at], [cross_pieces], [(rows, B)] * nz, [pltpu.VMEM((nz, rows, B), F32)])
+    crosses = [turned[0]] + [shifted(turned[k], "zh", k) for k in (2, 1, 3)]
     other = {k: sent_across(mine, k, 1, 0) for k in (2, 1, 3, 0)}
     same = {k: sent_across(mine, k, 0, 0) for k in (2, 1, 3)}
     spread = ("zh", "x", "yh")
-    *joined, crosses = call(
-        joined_kernel, [at], [mine, *(same[k] for k in (1, 2, 3)), *(other[k] for k in range(4)), cross],
+    *joined, sent_rows = call(
+        functools.partial(joined_kernel, scale), [at],
+        [mine, *(same[k] for k in (1, 2, 3)), *(other[k] for k in range(4)), *crosses],
         [(4, piece, B), (4, piece, B), (lax.axis_size(spread), rows, B)],
     )
     pieces = []
@@ -345,7 +390,7 @@
         ring = rings[colour]
         moved = {k: shifted(joined[colour], ring, k) for k in (2, 1, 3)}
         pieces += [joined[colour]] + [moved[k] for k in (1, 2, 3)]
-    cross_rows = lax.all_to_all(crosses, spread, 0, 0, tiled=True)
+    cross_rows = lax.all_to_all(sent_rows, spread, 0, 0, tiled=True)
     (mine,) = call(
         functools.partial(inverse_kernel, nb, scale), [at, damping], pieces,
         [(B, width)],

time: 156 us -> 167 us (1.071)
  starting transfers between devices: 67.8 us -> 85.5 us
  waiting for transfers between devices: 50.6 us -> 41.2 us
  Pallas kernels: 30.2 us -> 33.9 us
    ppermute x15 -> x24, starting transfers between devices: 31.7 us -> 46.1 us  [shifted(): lax.ppermute(array, axis, [(spots[k], spots[(k + by) % size]) for k in ra...]
    ppermute x14 -> x7, waiting for transfers between devices: 14.8 us -> 0.61 us  [sent_across(): return lax.ppermute(array, PLANE, pairs)]
    all_to_all x1 -> x2, starting transfers between devices: 12 us -> 22.5 us  [the longest x1 13.8 us: program(): cross_rows = lax.all_to_all(sent_rows, spread, 0, 0, tiled=True)]
    ppermute x14 -> x7, starting transfers between devices: 19.7 us -> 10.2 us  [sent_across(): return lax.ppermute(array, PLANE, pairs)]
    ppermute x7 -> x10, waiting for transfers between devices: 8.1 us -> 16.3 us  [swapped(): return lax.ppermute(array, axes, pairs)]
    pallas_call x13 -> x20, Pallas kernels: 30.2 us -> 33.9 us  [call(): pl.pallas_call(kernel, out_shape=shapes, in_specs=smem(len(scalars)) + vm...]
    ppermute x15 -> x24, waiting for transfers between devices: 27.6 us -> 24.3 us  [shifted(): lax.ppermute(array, axis, [(spots[k], spots[(k + by) % size]) for k in ra...]
    ppermute x7 -> x10, starting transfers between devices: 4.43 us -> 6.81 us  [swapped(): return lax.ppermute(array, axes, pairs)]
  transfers between devices with their start and end apart: 37 -> 43, of which waited for: 21 -> 18; matrix products, arithmetic and copies ran while one was open for 0% -> 0% of each run, Pallas kernels for 15% -> 14%
where the time goes in v5:
time: 167 us; the launch traced here: 166 us
  starting transfers between devices  85.5 us (51%)
  waiting for transfers between devices  41.2 us (25%)
  Pallas kernels  33.9 us (20%)
  local copies, waits for them, and re-layouts  4.26 us (3%)
    ppermute x24, starting transfers between devices, shifted(): lax.ppermute(array, axis, [(spots[k], spots[(k + by) % size]) for k in ra...  46.1 us
    pallas_call x20, Pallas kernels, call(): pl.pallas_call(kernel, out_shape=shapes, in_specs=smem(len(scalars)) + vm...  33.9 us
    ppermute x24, waiting for transfers between devices, shifted(): lax.ppermute(array, axis, [(spots[k], spots[(k + by) % size]) for k in ra...  24.3 us
    ppermute x10, waiting for transfers between devices, swapped(): return lax.ppermute(array, axes, pairs)  16.3 us
    all_to_all x1, starting transfers between devices, program(): cross_rows = lax.all_to_all(sent_rows, spread, 0, 0, tiled=True)  13.8 us
    ppermute x7, starting transfers between devices, sent_across(): return lax.ppermute(array, PLANE, pairs)  10.2 us
    all_to_all x1, starting transfers between devices, program(): cross_pieces = lax.all_to_all(cross_half, PLANE[1:], 0, 0, tiled=True)  8.67 us
    ppermute x10, starting transfers between devices, swapped(): return lax.ppermute(array, axes, pairs)  6.81 us
  transfers between devices with their start and end apart: 43, of which 18 were waited for; matrix products, arithmetic and copies ran while one was open for 0% of the time, Pallas kernels for 14%

profile of v5, /device:TPU:2, one launch (start us, length us, event | category | flops | bytes accessed | tf_op | source)
XLA Modules:
  0.0 165.9 jit_solution(13868583194384470626)
XLA Ops:
  0.7 1.2 copy-done
  1.9 1.2 copy-done.2
  3.1 1.7 shard_map.55
  7.1 1.2 shard_map.67
  10.3 4.0 %collective-permute-done.refs_1_ = f32[4,4,144,128]{3,2,1,0:T(8,128)S(1)} collective-permute-done((f32[4,4,144,128]{3,2,1,0:T(8,128)S(1)}, f32[4,4,144,128]{3,2,1,0:T(8,128)S(1)}, u32[]{:S(2)}, u32[]{:S(2)}) %collective-permute-start) | collective-permute-done | bytes 1179680 | tf_op jit(solution)/shard_map/ppermute | solution.py:296
  16.7 1.2 shard_map.66.kept_ref
  18.8 2.0 %collective-permute-start.26 = (f32[16,4,32,128]{3,2,1,0:T(8,128)S(1)}, f32[16,4,32,128]{3,2,1,0:T(8,128)S(1)}, u32[]{:S(2)}, u32[]{:S(2)}) collective-permute-start(f32[16,4,32,128]{3,2,1,0:T(8,128)S(1)} %get-tuple-element.55), channel_id=1, source_target_pairs={{0,32},{32,0},{1,33},{33,1},{2,34},{34,2},{3,35},{35,3},{4,36},{36... | collective-permute-start | bytes 3145736 | tf_op jit(solution)/shard_map/ppermute | solution.py:296
  20.9 2.1 %collective-permute-start.1 = (f32[4,144,128]{2,1,0:T(8,128)S(1)}, f32[4,144,128]{2,1,0:T(8,128)S(1)}, u32[]{:S(2)}, u32[]{:S(2)}) collective-permute-start(f32[4,144,128]{2,1,0:T(8,128)S(1)} %get-tuple-element.36), channel_id=1, source_target_pairs={{0,4},{2,6},{4,0},{6,2},{1,5},{3,7},{5,1},{7,3},{8,12},{10,14},{12... | collective-permute-start | bytes 884744 | tf_op jit(solution)/shard_map/ppermute | solution.py:302
  23.0 2.0 %collective-permute-start.3 = (f32[4,144,128]{2,1,0:T(8,128)S(1)}, f32[4,144,128]{2,1,0:T(8,128)S(1)}, u32[]{:S(2)}, u32[]{:S(2)}) collective-permute-start(f32[4,144,128]{2,1,0:T(8,128)S(1)} %get-tuple-element.38), channel_id=1, source_target_pairs={{0,6},{2,0},{4,2},{6,4},{1,7},{3,1},{5,3},{7,5},{8,14},{10,8},{12,... | collective-permute-start | bytes 884744 | tf_op jit(solution)/shard_map/ppermute | solution.py:302
  25.0 3.2 %collective-permute-start.8 = (f32[4,144,128]{2,1,0:T(8,128)S(1)}, f32[4,144,128]{2,1,0:T(8,128)S(1)}, u32[]{:S(2)}, u32[]{:S(2)}) collective-permute-start(f32[4,144,128]{2,1,0:T(8,128)S(1)} %get-tuple-element.45), channel_id=1, source_target_pairs={{0,1},{16,17},{1,0},{17,16},{2,3},{18,19},{3,2},{19,18},{4,5},{20,... | collective-permute-start | bytes 884744 | tf_op jit(solution)/shard_map/ppermute | solution.py:302
  28.2 4.1 %collective-permute-done.1.refs_1_ = f32[4,144,128]{2,1,0:T(8,128)S(1)} collective-permute-done((f32[4,144,128]{2,1,0:T(8,128)S(1)}, f32[4,144,128]{2,1,0:T(8,128)S(1)}, u32[]{:S(2)}, u32[]{:S(2)}) %collective-permute-start.1) | collective-permute-done | bytes 294944 | tf_op jit(solution)/shard_map/ppermute | solution.py:302
  32.3 1.6 collective-permute-start.9
  33.9 3.7 %collective-permute-done.2.refs_2_ = f32[4,144,128]{2,1,0:T(8,128)S(1)} collective-permute-done((f32[4,144,128]{2,1,0:T(8,128)S(1)}, f32[4,144,128]{2,1,0:T(8,128)S(1)}, u32[]{:S(2)}, u32[]{:S(2)}) %collective-permute-start.2) | collective-permute-done | bytes 294944 | tf_op jit(solution)/shard_map/ppermute | solution.py:302
  37.5 3.0 %collective-permute-start.10 = (f32[4,144,128]{2,1,0:T(8,128)S(1)}, f32[4,144,128]{2,1,0:T(8,128)S(1)}, u32[]{:S(2)}, u32[]{:S(2)}) collective-permute-start(f32[4,144,128]{2,1,0:T(8,128)S(1)} %get-tuple-element.47), channel_id=1, source_target_pairs={{0,17},{16,0},{1,16},{17,1},{2,19},{18,2},{3,18},{19,3},{4,21},{20... | collective-permute-start | bytes 884744 | tf_op jit(solution)/shard_map/ppermute | solution.py:302
  42.8 2.3 %collective-permute-start.6 = (f32[144,128]{1,0:T(8,128)S(1)}, f32[144,128]{1,0:T(8,128)S(1)}, u32[]{:S(2)}, u32[]{:S(2)}) collective-permute-start(f32[144,128]{1,0:T(8,128)S(1)} %get-tuple-element.42), channel_id=1, source_target_pairs={{0,17},{16,0},{1,16},{17,1},{2,19},{18,2},{3,18},{19,3},{4,21},{20... | collective-permute-start | bytes 221192 | tf_op jit(solution)/shard_map/ppermute | solution.py:302
  45.1 3.3 %collective-permute-done.10.refs_3_ = f32[4,144,128]{2,1,0:T(8,128)S(1)} collective-permute-done((f32[4,144,128]{2,1,0:T(8,128)S(1)}, f32[4,144,128]{2,1,0:T(8,128)S(1)}, u32[]{:S(2)}, u32[]{:S(2)}) %collective-permute-start.10) | collective-permute-done | bytes 294944 | tf_op jit(solution)/shard_map/ppermute | solution.py:302
  49.3 2.9 %collective-permute-start.12 = (f32[144,128]{1,0:T(8,128)S(1)}, f32[144,128]{1,0:T(8,128)S(1)}, u32[]{:S(2)}, u32[]{:S(2)}) collective-permute-start(f32[144,128]{1,0:T(8,128)S(1)} %get-tuple-element.50), channel_id=1, source_target_pairs={{0,2},{2,4},{4,6},{6,0},{1,3},{3,5},{5,7},{7,1},{8,10},{10,12},{12... | collective-permute-start | bytes 221192 | tf_op jit(solution)/shard_map/ppermute | solution.py:302
  52.2 2.9 %collective-permute-done.11.refs_5_ = f32[144,128]{1,0:T(8,128)S(1)} collective-permute-done((f32[144,128]{1,0:T(8,128)S(1)}, f32[144,128]{1,0:T(8,128)S(1)}, u32[]{:S(2)}, u32[]{:S(2)}) %collective-permute-start.11) | collective-permute-done | bytes 73760 | tf_op jit(solution)/shard_map/ppermute | solution.py:302
  55.1 1.4 collective-permute-done.13.refs_7_
  57.1 1.2 shard_map.69
  58.3 8.7 %all-to-all-start = ((f32[16,4,32,128]{3,2,1,0:T(8,128)}), f32[16,4,32,128]{3,2,1,0:T(8,128)S(1)}, u32[]{:S(2)}, u32[]{:S(2)}) async-start(f32[16,4,32,128]{3,2,1,0:T(8,128)} %shard_map.69), calls=%async_computation | async-start | bytes 2097152 | tf_op jit(solution)/shard_map/all_to_all | solution.py:374
  67.2 4.8 %collective-permute-done.14.refs_1_ = f32[144,128]{1,0:T(8,128)S(1)} collective-permute-done((f32[144,128]{1,0:T(8,128)S(1)}, f32[144,128]{1,0:T(8,128)S(1)}, u32[]{:S(2)}, u32[]{:S(2)}) %collective-permute-start.14) | collective-permute-done | bytes 73760 | tf_op jit(solution)/shard_map/ppermute | solution.py:296
  72.1 5.3 %collective-permute-start.17 = (f32[144,128]{1,0:T(8,128)S(1)}, f32[144,128]{1,0:T(8,128)S(1)}, u32[]{:S(2)}, u32[]{:S(2)}) collective-permute-start(f32[144,128]{1,0:T(8,128)S(1)} %shard_map.64.refs_0_), channel_id=1, source_target_pairs={{0,192},{64,0},{128,64},{192,128},{1,193},{65,1},{129,65},{193,129... | collective-permute-start | bytes 221192 | tf_op jit(solution)/shard_map/ppermute | solution.py:302
  77.3 3.5 %collective-permute-start.15 = (f32[144,128]{1,0:T(8,128)S(1)}, f32[144,128]{1,0:T(8,128)S(1)}, u32[]{:S(2)}, u32[]{:S(2)}) collective-permute-start(f32[144,128]{1,0:T(8,128)S(1)} %shard_map.64.refs_0_), channel_id=1, source_target_pairs={{0,128},{64,192},{128,0},{192,64},{1,129},{65,193},{129,1},{193,65... | collective-permute-start | bytes 221192 | tf_op jit(solution)/shard_map/ppermute | solution.py:302
  80.9 3.8 %collective-permute-done.16.refs_2_ = f32[144,128]{1,0:T(8,128)S(1)} collective-permute-done((f32[144,128]{1,0:T(8,128)S(1)}, f32[144,128]{1,0:T(8,128)S(1)}, u32[]{:S(2)}, u32[]{:S(2)}) %collective-permute-start.16) | collective-permute-done | bytes 73760 | tf_op jit(solution)/shard_map/ppermute | solution.py:302
  84.7 1.9 %collective-permute-done.15.refs_1_ = f32[144,128]{1,0:T(8,128)S(1)} collective-permute-done((f32[144,128]{1,0:T(8,128)S(1)}, f32[144,128]{1,0:T(8,128)S(1)}, u32[]{:S(2)}, u32[]{:S(2)}) %collective-permute-start.15) | collective-permute-done | bytes 73760 | tf_op jit(solution)/shard_map/ppermute | solution.py:302
  86.6 3.9 %collective-permute-start.24 = (f32[144,128]{1,0:T(8,128)S(1)}, f32[144,128]{1,0:T(8,128)S(1)}, u32[]{:S(2)}, u32[]{:S(2)}) collective-permute-start(f32[144,128]{1,0:T(8,128)S(1)} %shard_map.65.refs_0_), channel_id=1, source_target_pairs={{0,49},{16,32},{1,48},{17,33},{2,51},{18,34},{3,50},{19,35},{4,53}... | collective-permute-start | bytes 221192 | tf_op jit(solution)/shard_map/ppermute | solution.py:315
  90.9 1.2 collective-permute-start.22
  92.1 2.2 %collective-permute-start.21 = (f32[144,128]{1,0:T(8,128)S(1)}, f32[144,128]{1,0:T(8,128)S(1)}, u32[]{:S(2)}, u32[]{:S(2)}) collective-permute-start(f32[144,128]{1,0:T(8,128)S(1)} %shard_map.65.refs_0_), channel_id=1, source_target_pairs={{0,32},{16,48},{1,33},{17,49},{2,34},{18,50},{3,35},{19,51},{4,36}... | collective-permute-start | bytes 221192 | tf_op jit(solution)/shard_map/ppermute | solution.py:315
  94.3 2.2 %collective-permute-start.20 = (f32[144,128]{1,0:T(8,128)S(1)}, f32[144,128]{1,0:T(8,128)S(1)}, u32[]{:S(2)}, u32[]{:S(2)}) collective-permute-start(f32[144,128]{1,0:T(8,128)S(1)} %shard_map.65.refs_0_), channel_id=1, source_target_pairs={{0,17},{16,0},{1,16},{17,1},{2,19},{18,2},{3,18},{19,3},{4,21},{20... | collective-permute-start | bytes 221192 | tf_op jit(solution)/shard_map/ppermute | solution.py:315
  98.0 4.2 %collective-permute-start.27 = (f32[32,128]{1,0:T(8,128)S(1)}, f32[32,128]{1,0:T(8,128)S(1)}, u32[]{:S(2)}, u32[]{:S(2)}) collective-permute-start(f32[32,128]{1,0:T(8,128)S(1)} %get-tuple-element.57), channel_id=1, source_target_pairs={{0,128},{64,192},{128,0},{192,64},{1,129},{65,193},{129,1},{193,65... | collective-permute-start | bytes 49160 | tf_op jit(solution)/shard_map/ppermute | solution.py:302
  102.2 2.7 %collective-permute-start.28 = (f32[32,128]{1,0:T(8,128)S(1)}, f32[32,128]{1,0:T(8,128)S(1)}, u32[]{:S(2)}, u32[]{:S(2)}) collective-permute-start(f32[32,128]{1,0:T(8,128)S(1)} %get-tuple-element.58), channel_id=1, source_target_pairs={{0,64},{64,128},{128,192},{192,0},{1,65},{65,129},{129,193},{193,1... | collective-permute-start | bytes 49160 | tf_op jit(solution)/shard_map/ppermute | solution.py:302
  104.9 1.4 collective-permute-start.29
  106.4 1.7 %collective-permute-done.28.refs_10_ = f32[32,128]{1,0:T(8,128)S(1)} collective-permute-done((f32[32,128]{1,0:T(8,128)S(1)}, f32[32,128]{1,0:T(8,128)S(1)}, u32[]{:S(2)}, u32[]{:S(2)}) %collective-permute-start.28) | collective-permute-done | bytes 16416 | tf_op jit(solution)/shard_map/ppermute | solution.py:302
  108.0 1.5 collective-permute-done.29.refs_11_
  109.6 1.5 shard_map.71
  111.0 2.2 %collective-permute-start.32 = (f32[4,144,128]{2,1,0:T(8,128)S(1)}, f32[4,144,128]{2,1,0:T(8,128)S(1)}, u32[]{:S(2)}, u32[]{:S(2)}) collective-permute-start(f32[4,144,128]{2,1,0:T(8,128)S(1)} %get-tuple-element.60.refs_0_), channel_id=1, source_target_pairs={{0,6},{2,0},{4,2},{6,4},{1,7},{3,1},{5,3},{7,5},{8,14},{10,8},{12,... | collective-permute-start | bytes 884744 | tf_op jit(solution)/shard_map/ppermute | solution.py:302
  113.2 1.3 collective-permute-start.31
  114.5 1.7 %collective-permute-start.30 = (f32[4,144,128]{2,1,0:T(8,128)S(1)}, f32[4,144,128]{2,1,0:T(8,128)S(1)}, u32[]{:S(2)}, u32[]{:S(2)}) collective-permute-start(f32[4,144,128]{2,1,0:T(8,128)S(1)} %get-tuple-element.60.refs_0_), channel_id=1, source_target_pairs={{0,2},{2,4},{4,6},{6,0},{1,3},{3,5},{5,7},{7,1},{8,10},{10,12},{12... | collective-permute-start | bytes 884744 | tf_op jit(solution)/shard_map/ppermute | solution.py:302
  116.2 3.2 %collective-permute-start.35 = (f32[4,144,128]{2,1,0:T(8,128)S(1)}, f32[4,144,128]{2,1,0:T(8,128)S(1)}, u32[]{:S(2)}, u32[]{:S(2)}) collective-permute-start(f32[4,144,128]{2,1,0:T(8,128)S(1)} %get-tuple-element.61.refs_4_), channel_id=1, source_target_pairs={{0,17},{16,0},{1,16},{17,1},{2,19},{18,2},{3,18},{19,3},{4,21},{20... | collective-permute-start | bytes 884744 | tf_op jit(solution)/shard_map/ppermute | solution.py:302
  120.9 13.8 %all-to-all-start.1 = ((f32[32,32,128]{2,1,0:T(8,128)}), f32[32,32,128]{2,1,0:T(8,128)S(1)}, u32[]{:S(2)}, u32[]{:S(2)}) async-start(f32[32,32,128]{2,1,0:T(8,128)} %get-tuple-element.62), calls=%async_computation.1 | async-start | bytes 1048576 | tf_op jit(solution)/shard_map/all_to_all | solution.py:393
  136.5 16.8 %shard_map.72.mine_ref = f32[128,1024]{1,0:T(8,128)S(1)} custom-call(s32[6]{0:T(128)S(1)} %shift-right-arithmetic_and_fusion.at_ref.refs_0_, f32[2]{0:T(128)S(1)} %copy-done.6, f32[4,144,128]{2,1,0:T(8,128)S(1)} %get-tuple-element.60.refs_0_, f32[4,144,128]{2,1,0:T(8,128)S(1)} %collective-permute-done.30.refs_1_, ...), custom_call_target="tpu_custom_call" | custom-call | flops 11274289152 | bytes 2883584 | tf_op jit(solution)/shard_map/pallas_call | solution.py:282
  153.4 1.9 %collective-permute-done.36.other_ref = f32[128,1024]{1,0:T(8,128)S(1)} collective-permute-done((f32[128,1024]{1,0:T(8,128)S(1)}, f32[128,1024]{1,0:T(8,128)S(1)}, u32[]{:S(2)}, u32[]{:S(2)}) %collective-permute-start.36) | collective-permute-done | bytes 524320 | tf_op jit(solution)/shard_map/ppermute | solution.py:296
  157.0 1.3 collective-permute-start.38
  158.3 1.5 collective-permute-start.37
  159.8 1.8 %collective-permute-done.39.refs_3_ = f32[4,32,128]{2,1,0:T(8,128)S(1)} collective-permute-done((f32[4,32,128]{2,1,0:T(8,128)S(1)}, f32[4,32,128]{2,1,0:T(8,128)S(1)}, u32[]{:S(2)}, u32[]{:S(2)}) %collective-permute-start.39) | collective-permute-done | bytes 65568 | tf_op jit(solution)/shard_map/ppermute | solution.py:296
  163.0 1.5 collective-permute-done.40.refs_4_
  164.5 1.4 shard_map.74
  (74 shorter events, 20.5 us)
Async XLA Ops:
  0.7 1.2 copy-start
  1.9 1.2 copy-start.2
  5.9 1.2 copy-start.1
  7.1 1.4 copy-start.3
  8.4 9.6 %collective-permute-start.25 = (f32[2,16,4,32,128]{4,3,2,1,0:T(8,128)S(1)}, f32[2,16,4,32,128]{4,3,2,1,0:T(8,128)S(1)}, u32[]{:S(2)}, u32[]{:S(2)}) collective-permute-start(f32[2,16,4,32,128]{4,3,2,1,0:T(8,128)S(1)} %shard_map.67), channel_id=1, source_target_pairs={{0,8},{8,0},{1,9},{9,1},{2,10},{10,2},{3,11},{11,3},{4,12},{12,4},... | collective-permute-start | bytes 6291464 | tf_op jit(solution)/shard_map/ppermute | solution.py:296
  9.6 4.7 %collective-permute-start = (f32[4,4,144,128]{3,2,1,0:T(8,128)S(1)}, f32[4,4,144,128]{3,2,1,0:T(8,128)S(1)}, u32[]{:S(2)}, u32[]{:S(2)}) collective-permute-start(f32[4,4,144,128]{3,2,1,0:T(8,128)S(1)} %shard_map.57), channel_id=1, source_target_pairs={{0,8},{8,0},{1,9},{9,1},{2,10},{10,2},{3,11},{11,3},{4,12},{12,4},... | collective-permute-start | bytes 3538952 | tf_op jit(solution)/shard_map/ppermute | solution.py:296
  10.2 5.8 %collective-permute-start.7 = (f32[4,4,144,128]{3,2,1,0:T(8,128)S(1)}, f32[4,4,144,128]{3,2,1,0:T(8,128)S(1)}, u32[]{:S(2)}, u32[]{:S(2)}) collective-permute-start(f32[4,4,144,128]{3,2,1,0:T(8,128)S(1)} %get-tuple-element.43), channel_id=1, source_target_pairs={{0,8},{8,0},{1,9},{9,1},{2,10},{10,2},{3,11},{11,3},{4,12},{12,4},... | collective-permute-start | bytes 3538952 | tf_op jit(solution)/shard_map/ppermute | solution.py:296
  18.8 38.2 %collective-permute-start.26 = (f32[16,4,32,128]{3,2,1,0:T(8,128)S(1)}, f32[16,4,32,128]{3,2,1,0:T(8,128)S(1)}, u32[]{:S(2)}, u32[]{:S(2)}) collective-permute-start(f32[16,4,32,128]{3,2,1,0:T(8,128)S(1)} %get-tuple-element.55), channel_id=1, source_target_pairs={{0,32},{32,0},{1,33},{33,1},{2,34},{34,2},{3,35},{35,3},{4,36},{36... | collective-permute-start | bytes 3145736 | tf_op jit(solution)/shard_map/ppermute | solution.py:296
  20.9 11.4 %collective-permute-start.1 = (f32[4,144,128]{2,1,0:T(8,128)S(1)}, f32[4,144,128]{2,1,0:T(8,128)S(1)}, u32[]{:S(2)}, u32[]{:S(2)}) collective-permute-start(f32[4,144,128]{2,1,0:T(8,128)S(1)} %get-tuple-element.36), channel_id=1, source_target_pairs={{0,4},{2,6},{4,0},{6,2},{1,5},{3,7},{5,1},{7,3},{8,12},{10,14},{12... | collective-permute-start | bytes 884744 | tf_op jit(solution)/shard_map/ppermute | solution.py:302
  23.0 14.5 %collective-permute-start.2 = (f32[4,144,128]{2,1,0:T(8,128)S(1)}, f32[4,144,128]{2,1,0:T(8,128)S(1)}, u32[]{:S(2)}, u32[]{:S(2)}) collective-permute-start(f32[4,144,128]{2,1,0:T(8,128)S(1)} %get-tuple-element.37), channel_id=1, source_target_pairs={{0,2},{2,4},{4,6},{6,0},{1,3},{3,5},{5,7},{7,1},{8,10},{10,12},{12... | collective-permute-start | bytes 884744 | tf_op jit(solution)/shard_map/ppermute | solution.py:302
  23.0 17.6 %collective-permute-start.3 = (f32[4,144,128]{2,1,0:T(8,128)S(1)}, f32[4,144,128]{2,1,0:T(8,128)S(1)}, u32[]{:S(2)}, u32[]{:S(2)}) collective-permute-start(f32[4,144,128]{2,1,0:T(8,128)S(1)} %get-tuple-element.38), channel_id=1, source_target_pairs={{0,6},{2,0},{4,2},{6,4},{1,7},{3,1},{5,3},{7,5},{8,14},{10,8},{12,... | collective-permute-start | bytes 884744 | tf_op jit(solution)/shard_map/ppermute | solution.py:302
  25.0 16.9 %collective-permute-start.8 = (f32[4,144,128]{2,1,0:T(8,128)S(1)}, f32[4,144,128]{2,1,0:T(8,128)S(1)}, u32[]{:S(2)}, u32[]{:S(2)}) collective-permute-start(f32[4,144,128]{2,1,0:T(8,128)S(1)} %get-tuple-element.45), channel_id=1, source_target_pairs={{0,1},{16,17},{1,0},{17,16},{2,3},{18,19},{3,2},{19,18},{4,5},{20,... | collective-permute-start | bytes 884744 | tf_op jit(solution)/shard_map/ppermute | solution.py:302
  32.3 10.6 %collective-permute-start.9 = (f32[4,144,128]{2,1,0:T(8,128)S(1)}, f32[4,144,128]{2,1,0:T(8,128)S(1)}, u32[]{:S(2)}, u32[]{:S(2)}) collective-permute-start(f32[4,144,128]{2,1,0:T(8,128)S(1)} %get-tuple-element.46), channel_id=1, source_target_pairs={{0,16},{16,1},{1,17},{17,0},{2,18},{18,3},{3,19},{19,2},{4,20},{20... | collective-permute-start | bytes 884744 | tf_op jit(solution)/shard_map/ppermute | solution.py:302
  37.5 10.9 %collective-permute-start.10 = (f32[4,144,128]{2,1,0:T(8,128)S(1)}, f32[4,144,128]{2,1,0:T(8,128)S(1)}, u32[]{:S(2)}, u32[]{:S(2)}) collective-permute-start(f32[4,144,128]{2,1,0:T(8,128)S(1)} %get-tuple-element.47), channel_id=1, source_target_pairs={{0,17},{16,0},{1,16},{17,1},{2,19},{18,2},{3,18},{19,3},{4,21},{20... | collective-permute-start | bytes 884744 | tf_op jit(solution)/shard_map/ppermute | solution.py:302
  41.1 8.1 %collective-permute-start.4 = (f32[144,128]{1,0:T(8,128)S(1)}, f32[144,128]{1,0:T(8,128)S(1)}, u32[]{:S(2)}, u32[]{:S(2)}) collective-permute-start(f32[144,128]{1,0:T(8,128)S(1)} %get-tuple-element.40), channel_id=1, source_target_pairs={{0,1},{16,17},{1,0},{17,16},{2,3},{18,19},{3,2},{19,18},{4,5},{20,... | collective-permute-start | bytes 221192 | tf_op jit(solution)/shard_map/ppermute | solution.py:302
  41.9 10.3 %collective-permute-start.5 = (f32[144,128]{1,0:T(8,128)S(1)}, f32[144,128]{1,0:T(8,128)S(1)}, u32[]{:S(2)}, u32[]{:S(2)}) collective-permute-start(f32[144,128]{1,0:T(8,128)S(1)} %get-tuple-element.41), channel_id=1, source_target_pairs={{0,16},{16,1},{1,17},{17,0},{2,18},{18,3},{3,19},{19,2},{4,20},{20... | collective-permute-start | bytes 221192 | tf_op jit(solution)/shard_map/ppermute | solution.py:302
  42.8 9.3 %collective-permute-start.6 = (f32[144,128]{1,0:T(8,128)S(1)}, f32[144,128]{1,0:T(8,128)S(1)}, u32[]{:S(2)}, u32[]{:S(2)}) collective-permute-start(f32[144,128]{1,0:T(8,128)S(1)} %get-tuple-element.42), channel_id=1, source_target_pairs={{0,17},{16,0},{1,16},{17,1},{2,19},{18,2},{3,18},{19,3},{4,21},{20... | collective-permute-start | bytes 221192 | tf_op jit(solution)/shard_map/ppermute | solution.py:302
  49.0 6.1 %collective-permute-start.11 = (f32[144,128]{1,0:T(8,128)S(1)}, f32[144,128]{1,0:T(8,128)S(1)}, u32[]{:S(2)}, u32[]{:S(2)}) collective-permute-start(f32[144,128]{1,0:T(8,128)S(1)} %get-tuple-element.49), channel_id=1, source_target_pairs={{0,4},{2,6},{4,0},{6,2},{1,5},{3,7},{5,1},{7,3},{8,12},{10,14},{12... | collective-permute-start | bytes 221192 | tf_op jit(solution)/shard_map/ppermute | solution.py:302
  49.3 5.8 %collective-permute-start.12 = (f32[144,128]{1,0:T(8,128)S(1)}, f32[144,128]{1,0:T(8,128)S(1)}, u32[]{:S(2)}, u32[]{:S(2)}) collective-permute-start(f32[144,128]{1,0:T(8,128)S(1)} %get-tuple-element.50), channel_id=1, source_target_pairs={{0,2},{2,4},{4,6},{6,0},{1,3},{3,5},{5,7},{7,1},{8,10},{10,12},{12... | collective-permute-start | bytes 221192 | tf_op jit(solution)/shard_map/ppermute | solution.py:302
  52.2 4.4 %collective-permute-start.13 = (f32[144,128]{1,0:T(8,128)S(1)}, f32[144,128]{1,0:T(8,128)S(1)}, u32[]{:S(2)}, u32[]{:S(2)}) collective-permute-start(f32[144,128]{1,0:T(8,128)S(1)} %get-tuple-element.51), channel_id=1, source_target_pairs={{0,6},{2,0},{4,2},{6,4},{1,7},{3,1},{5,3},{7,5},{8,14},{10,8},{12,... | collective-permute-start | bytes 221192 | tf_op jit(solution)/shard_map/ppermute | solution.py:302
  58.3 39.1 %all-to-all-start = ((f32[16,4,32,128]{3,2,1,0:T(8,128)}), f32[16,4,32,128]{3,2,1,0:T(8,128)S(1)}, u32[]{:S(2)}, u32[]{:S(2)}) async-start(f32[16,4,32,128]{3,2,1,0:T(8,128)} %shard_map.69), calls=%async_computation | async-start | bytes 2097152 | tf_op jit(solution)/shard_map/all_to_all | solution.py:374
  67.0 5.1 %collective-permute-start.14 = (f32[144,128]{1,0:T(8,128)S(1)}, f32[144,128]{1,0:T(8,128)S(1)}, u32[]{:S(2)}, u32[]{:S(2)}) collective-permute-start(f32[144,128]{1,0:T(8,128)S(1)} %get-tuple-element.53.refs_2_), channel_id=1, source_target_pairs={{0,32},{32,0},{1,33},{33,1},{2,34},{34,2},{3,35},{35,3},{4,36},{36... | collective-permute-start | bytes 221192 | tf_op jit(solution)/shard_map/ppermute | solution.py:296
  72.1 8.8 %collective-permute-start.17 = (f32[144,128]{1,0:T(8,128)S(1)}, f32[144,128]{1,0:T(8,128)S(1)}, u32[]{:S(2)}, u32[]{:S(2)}) collective-permute-start(f32[144,128]{1,0:T(8,128)S(1)} %shard_map.64.refs_0_), channel_id=1, source_target_pairs={{0,192},{64,0},{128,64},{192,128},{1,193},{65,1},{129,65},{193,129... | collective-permute-start | bytes 221192 | tf_op jit(solution)/shard_map/ppermute | solution.py:302
  77.3 7.3 %collective-permute-start.16 = (f32[144,128]{1,0:T(8,128)S(1)}, f32[144,128]{1,0:T(8,128)S(1)}, u32[]{:S(2)}, u32[]{:S(2)}) collective-permute-start(f32[144,128]{1,0:T(8,128)S(1)} %shard_map.64.refs_0_), channel_id=1, source_target_pairs={{0,64},{64,128},{128,192},{192,0},{1,65},{65,129},{129,193},{193,1... | collective-permute-start | bytes 221192 | tf_op jit(solution)/shard_map/ppermute | solution.py:302
  77.3 9.2 %collective-permute-start.15 = (f32[144,128]{1,0:T(8,128)S(1)}, f32[144,128]{1,0:T(8,128)S(1)}, u32[]{:S(2)}, u32[]{:S(2)}) collective-permute-start(f32[144,128]{1,0:T(8,128)S(1)} %shard_map.64.refs_0_), channel_id=1, source_target_pairs={{0,128},{64,192},{128,0},{192,64},{1,129},{65,193},{129,1},{193,65... | collective-permute-start | bytes 221192 | tf_op jit(solution)/shard_map/ppermute | solution.py:302
  86.6 48.9 %copy-start.6 = (f32[2]{0:T(128)S(1)}, f32[2]{0:T(128)}, u32[]{:S(2)}) copy-start(f32[2]{0:T(128)} %damp_ref.1) | copy-start | bytes 28
  86.6 9.9 %collective-permute-start.24 = (f32[144,128]{1,0:T(8,128)S(1)}, f32[144,128]{1,0:T(8,128)S(1)}, u32[]{:S(2)}, u32[]{:S(2)}) collective-permute-start(f32[144,128]{1,0:T(8,128)S(1)} %shard_map.65.refs_0_), channel_id=1, source_target_pairs={{0,49},{16,32},{1,48},{17,33},{2,51},{18,34},{3,50},{19,35},{4,53}... | collective-permute-start | bytes 221192 | tf_op jit(solution)/shard_map/ppermute | solution.py:315
  90.6 6.8 %collective-permute-start.23 = (f32[144,128]{1,0:T(8,128)S(1)}, f32[144,128]{1,0:T(8,128)S(1)}, u32[]{:S(2)}, u32[]{:S(2)}) collective-permute-start(f32[144,128]{1,0:T(8,128)S(1)} %shard_map.65.refs_0_), channel_id=1, source_target_pairs={{0,33},{16,49},{1,32},{17,48},{2,35},{18,51},{3,34},{19,50},{4,37}... | collective-permute-start | bytes 221192 | tf_op jit(solution)/shard_map/ppermute | solution.py:315
  90.9 7.2 %collective-permute-start.22 = (f32[144,128]{1,0:T(8,128)S(1)}, f32[144,128]{1,0:T(8,128)S(1)}, u32[]{:S(2)}, u32[]{:S(2)}) collective-permute-start(f32[144,128]{1,0:T(8,128)S(1)} %shard_map.65.refs_0_), channel_id=1, source_target_pairs={{0,48},{16,33},{1,49},{17,32},{2,50},{18,35},{3,51},{19,34},{4,52}... | collective-permute-start | bytes 221192 | tf_op jit(solution)/shard_map/ppermute | solution.py:315
  92.1 10.1 %collective-permute-start.21 = (f32[144,128]{1,0:T(8,128)S(1)}, f32[144,128]{1,0:T(8,128)S(1)}, u32[]{:S(2)}, u32[]{:S(2)}) collective-permute-start(f32[144,128]{1,0:T(8,128)S(1)} %shard_map.65.refs_0_), channel_id=1, source_target_pairs={{0,32},{16,48},{1,33},{17,49},{2,34},{18,50},{3,35},{19,51},{4,36}... | collective-permute-start | bytes 221192 | tf_op jit(solution)/shard_map/ppermute | solution.py:315
  94.3 10.6 %collective-permute-start.20 = (f32[144,128]{1,0:T(8,128)S(1)}, f32[144,128]{1,0:T(8,128)S(1)}, u32[]{:S(2)}, u32[]{:S(2)}) collective-permute-start(f32[144,128]{1,0:T(8,128)S(1)} %shard_map.65.refs_0_), channel_id=1, source_target_pairs={{0,17},{16,0},{1,16},{17,1},{2,19},{18,2},{3,18},{19,3},{4,21},{20... | collective-permute-start | bytes 221192 | tf_op jit(solution)/shard_map/ppermute | solution.py:315
  96.5 9.9 %collective-permute-start.19 = (f32[144,128]{1,0:T(8,128)S(1)}, f32[144,128]{1,0:T(8,128)S(1)}, u32[]{:S(2)}, u32[]{:S(2)}) collective-permute-start(f32[144,128]{1,0:T(8,128)S(1)} %shard_map.65.refs_0_), channel_id=1, source_target_pairs={{0,1},{16,17},{1,0},{17,16},{2,3},{18,19},{3,2},{19,18},{4,5},{20,... | collective-permute-start | bytes 221192 | tf_op jit(solution)/shard_map/ppermute | solution.py:315
  97.3 9.0 %collective-permute-start.18 = (f32[144,128]{1,0:T(8,128)S(1)}, f32[144,128]{1,0:T(8,128)S(1)}, u32[]{:S(2)}, u32[]{:S(2)}) collective-permute-start(f32[144,128]{1,0:T(8,128)S(1)} %shard_map.65.refs_0_), channel_id=1, source_target_pairs={{0,16},{16,1},{1,17},{17,0},{2,18},{18,3},{3,19},{19,2},{4,20},{20... | collective-permute-start | bytes 221192 | tf_op jit(solution)/shard_map/ppermute | solution.py:315
  98.0 8.3 %collective-permute-start.27 = (f32[32,128]{1,0:T(8,128)S(1)}, f32[32,128]{1,0:T(8,128)S(1)}, u32[]{:S(2)}, u32[]{:S(2)}) collective-permute-start(f32[32,128]{1,0:T(8,128)S(1)} %get-tuple-element.57), channel_id=1, source_target_pairs={{0,128},{64,192},{128,0},{192,64},{1,129},{65,193},{129,1},{193,65... | collective-permute-start | bytes 49160 | tf_op jit(solution)/shard_map/ppermute | solution.py:302
  102.2 5.8 %collective-permute-start.28 = (f32[32,128]{1,0:T(8,128)S(1)}, f32[32,128]{1,0:T(8,128)S(1)}, u32[]{:S(2)}, u32[]{:S(2)}) collective-permute-start(f32[32,128]{1,0:T(8,128)S(1)} %get-tuple-element.58), channel_id=1, source_target_pairs={{0,64},{64,128},{128,192},{192,0},{1,65},{65,129},{129,193},{193,1... | collective-permute-start | bytes 49160 | tf_op jit(solution)/shard_map/ppermute | solution.py:302
  104.9 4.6 %collective-permute-start.29 = (f32[32,128]{1,0:T(8,128)S(1)}, f32[32,128]{1,0:T(8,128)S(1)}, u32[]{:S(2)}, u32[]{:S(2)}) collective-permute-start(f32[32,128]{1,0:T(8,128)S(1)} %get-tuple-element.59), channel_id=1, source_target_pairs={{0,192},{64,0},{128,64},{192,128},{1,193},{65,1},{129,65},{193,129... | collective-permute-start | bytes 49160 | tf_op jit(solution)/shard_map/ppermute | solution.py:302
  111.0 9.2 %collective-permute-start.32 = (f32[4,144,128]{2,1,0:T(8,128)S(1)}, f32[4,144,128]{2,1,0:T(8,128)S(1)}, u32[]{:S(2)}, u32[]{:S(2)}) collective-permute-start(f32[4,144,128]{2,1,0:T(8,128)S(1)} %get-tuple-element.60.refs_0_), channel_id=1, source_target_pairs={{0,6},{2,0},{4,2},{6,4},{1,7},{3,1},{5,3},{7,5},{8,14},{10,8},{12,... | collective-permute-start | bytes 884744 | tf_op jit(solution)/shard_map/ppermute | solution.py:302
  113.2 21.5 %collective-permute-start.31 = (f32[4,144,128]{2,1,0:T(8,128)S(1)}, f32[4,144,128]{2,1,0:T(8,128)S(1)}, u32[]{:S(2)}, u32[]{:S(2)}) collective-permute-start(f32[4,144,128]{2,1,0:T(8,128)S(1)} %get-tuple-element.60.refs_0_), channel_id=1, source_target_pairs={{0,4},{2,6},{4,0},{6,2},{1,5},{3,7},{5,1},{7,3},{8,12},{10,14},{12... | collective-permute-start | bytes 884744 | tf_op jit(solution)/shard_map/ppermute | solution.py:302
  114.5 20.3 %collective-permute-start.30 = (f32[4,144,128]{2,1,0:T(8,128)S(1)}, f32[4,144,128]{2,1,0:T(8,128)S(1)}, u32[]{:S(2)}, u32[]{:S(2)}) collective-permute-start(f32[4,144,128]{2,1,0:T(8,128)S(1)} %get-tuple-element.60.refs_0_), channel_id=1, source_target_pairs={{0,2},{2,4},{4,6},{6,0},{1,3},{3,5},{5,7},{7,1},{8,10},{10,12},{12... | collective-permute-start | bytes 884744 | tf_op jit(solution)/shard_map/ppermute | solution.py:302
  116.2 18.6 %collective-permute-start.35 = (f32[4,144,128]{2,1,0:T(8,128)S(1)}, f32[4,144,128]{2,1,0:T(8,128)S(1)}, u32[]{:S(2)}, u32[]{:S(2)}) collective-permute-start(f32[4,144,128]{2,1,0:T(8,128)S(1)} %get-tuple-element.61.refs_4_), channel_id=1, source_target_pairs={{0,17},{16,0},{1,16},{17,1},{2,19},{18,2},{3,18},{19,3},{4,21},{20... | collective-permute-start | bytes 884744 | tf_op jit(solution)/shard_map/ppermute | solution.py:302
  119.4 15.3 %collective-permute-start.34 = (f32[4,144,128]{2,1,0:T(8,128)S(1)}, f32[4,144,128]{2,1,0:T(8,128)S(1)}, u32[]{:S(2)}, u32[]{:S(2)}) collective-permute-start(f32[4,144,128]{2,1,0:T(8,128)S(1)} %get-tuple-element.61.refs_4_), channel_id=1, source_target_pairs={{0,1},{16,17},{1,0},{17,16},{2,3},{18,19},{3,2},{19,18},{4,5},{20,... | collective-permute-start | bytes 884744 | tf_op jit(solution)/shard_map/ppermute | solution.py:302
  120.2 14.5 %collective-permute-start.33 = (f32[4,144,128]{2,1,0:T(8,128)S(1)}, f32[4,144,128]{2,1,0:T(8,128)S(1)}, u32[]{:S(2)}, u32[]{:S(2)}) collective-permute-start(f32[4,144,128]{2,1,0:T(8,128)S(1)} %get-tuple-element.61.refs_4_), channel_id=1, source_target_pairs={{0,16},{16,1},{1,17},{17,0},{2,18},{18,3},{3,19},{19,2},{4,20},{20... | collective-permute-start | bytes 884744 | tf_op jit(solution)/shard_map/ppermute | solution.py:302
  120.9 34.3 %all-to-all-start.1 = ((f32[32,32,128]{2,1,0:T(8,128)}), f32[32,32,128]{2,1,0:T(8,128)S(1)}, u32[]{:S(2)}, u32[]{:S(2)}) async-start(f32[32,32,128]{2,1,0:T(8,128)} %get-tuple-element.62), calls=%async_computation.1 | async-start | bytes 1048576 | tf_op jit(solution)/shard_map/all_to_all | solution.py:393
  153.3 2.0 %collective-permute-start.36 = (f32[128,1024]{1,0:T(8,128)S(1)}, f32[128,1024]{1,0:T(8,128)S(1)}, u32[]{:S(2)}, u32[]{:S(2)}) collective-permute-start(f32[128,1024]{1,0:T(8,128)S(1)} %shard_map.72.mine_ref), channel_id=1, source_target_pairs={{0,8},{8,0},{1,9},{9,1},{2,10},{10,2},{3,11},{11,3},{4,12},{12,4},... | collective-permute-start | bytes 1572872 | tf_op jit(solution)/shard_map/ppermute | solution.py:296
  156.2 5.4 %collective-permute-start.39 = (f32[4,32,128]{2,1,0:T(8,128)S(1)}, f32[4,32,128]{2,1,0:T(8,128)S(1)}, u32[]{:S(2)}, u32[]{:S(2)}) collective-permute-start(f32[4,32,128]{2,1,0:T(8,128)S(1)} %shard_map.73.refs_0_), channel_id=1, source_target_pairs={{0,48},{16,32},{32,16},{48,0},{1,49},{17,33},{33,17},{49,1},{2,50}... | collective-permute-start | bytes 196616 | tf_op jit(solution)/shard_map/ppermute | solution.py:296
  157.0 5.0 %collective-permute-start.38 = (f32[4,32,128]{2,1,0:T(8,128)S(1)}, f32[4,32,128]{2,1,0:T(8,128)S(1)}, u32[]{:S(2)}, u32[]{:S(2)}) collective-permute-start(f32[4,32,128]{2,1,0:T(8,128)S(1)} %shard_map.73.refs_0_), channel_id=1, source_target_pairs={{0,32},{32,0},{1,33},{33,1},{2,34},{34,2},{3,35},{35,3},{4,36},{36... | collective-permute-start | bytes 196616 | tf_op jit(solution)/shard_map/ppermute | solution.py:296
  158.3 4.5 %collective-permute-start.37 = (f32[4,32,128]{2,1,0:T(8,128)S(1)}, f32[4,32,128]{2,1,0:T(8,128)S(1)}, u32[]{:S(2)}, u32[]{:S(2)}) collective-permute-start(f32[4,32,128]{2,1,0:T(8,128)S(1)} %shard_map.73.refs_0_), channel_id=1, source_target_pairs={{0,16},{16,0},{1,17},{17,1},{2,18},{18,2},{3,19},{19,3},{4,20},{20... | collective-permute-start | bytes 196616 | tf_op jit(solution)/shard_map/ppermute | solution.py:296
  162.9 1.6 collective-permute-start.40
  (2 other events, 1.7 us)

commit v6 on v5

--- a/solution.py
+++ b/solution.py
@@ -144,29 +144,29 @@
     refs[-1][...] = total
 
 
-def summed_kernel(at_ref, pieces_ref, *refs):
-    outs, sum_ref = refs[:-1], refs[-1]
+def summed_kernel(pieces_ref, out_ref):
     total = pieces_ref[0]
     for q in range(1, pieces_ref.shape[0]):
         total = total + pieces_ref[q]
-    sum_ref[...] = total
-    for k, out in enumerate(outs):
-        out[...] = sum_ref[lax.rem(at_ref[ZH] + k, len(outs))]
-
-
-def joined_kernel(scale, at_ref, *refs):
-    outs = refs[-3:]
+    out_ref[...] = total
+
+
+def joined_kernel(at_ref, *refs):
+    outs = refs[-2:]
     low = at_ref[ZL] == 0
     for k in range(4):
         own, other = refs[k][...], refs[4 + k][...]
         outs[0][k] = jnp.where(low, own, other)
         outs[1][k] = jnp.where(low, other, own)
-    cross = refs[8][...]
-    for ref in refs[9:-3]:
-        cross = cross + ref[...]
+
+
+def repeated_kernel(scale, pieces_ref, out_ref):
+    cross = pieces_ref[0]
+    for k in range(1, pieces_ref.shape[0]):
+        cross = cross + pieces_ref[k]
     cross = cross * scale
-    for q in range(outs[2].shape[0]):
-        outs[2][q] = cross
+    for q in range(out_ref.shape[0]):
+        out_ref[q] = cross
 
 
 def rows_kernel(at_ref, cross_ref, mine_ref, other_ref, out_ref, c_ref):
@@ -375,21 +375,27 @@
     (half,) = call(total_kernel, [], [keep, arrived], [chunk])
     around = [half] + [shifted(half, "zh", k) for k in (2, 1, 3)]
     (mine,) = call(total_kernel, [], around, [chunk])
-    turned = call(summed_kernel, [at], [cross_pieces], [(rows, B)] * nz, [pltpu.VMEM((nz, rows, B), F32)])
-    crosses = [turned[0]] + [shifted(turned[k], "zh", k) for k in (2, 1, 3)]
+    (cross_sum,) = call(summed_kernel, [], [cross_pieces], [(nz, rows, B)])
     other = {k: sent_across(mine, k, 1, 0) for k in (2, 1, 3, 0)}
     same = {k: sent_across(mine, k, 0, 0) for k in (2, 1, 3)}
+    joined = call(
+        joined_kernel, [at], [mine, *(same[k] for k in (1, 2, 3)), *(other[k] for k in range(4))],
+        [(4, piece, B)] * 2,
+    )
+    cross_parts = lax.all_to_all(cross_sum, "zh", 0, 0, tiled=True)
     spread = ("zh", "x", "yh")
-    *joined, sent_rows = call(
-        functools.partial(joined_kernel, scale), [at],
-        [mine, *(same[k] for k in (1, 2, 3)), *(other[k] for k in range(4)), *crosses],
-        [(4, piece, B), (4, piece, B), (lax.axis_size(spread), rows, B)],
-    )
+    (sent_rows,) = call(
+        functools.partial(repeated_kernel, scale), [], [cross_parts],
+        [(lax.axis_size(spread), rows, B)],
+    )
+    moved = {}
+    for steps in ((2,), (1, 3)):
+        for colour in range(2):
+            for k in steps:
+                moved[colour, k] = shifted(joined[colour], rings[colour], k)
     pieces = []
     for colour in range(2):
-        ring = rings[colour]
-        moved = {k: shifted(joined[colour], ring, k) for k in (2, 1, 3)}
-        pieces += [joined[colour]] + [moved[k] for k in (1, 2, 3)]
+        pieces += [joined[colour]] + [moved[colour, k] for k in (1, 2, 3)]
     cross_rows = lax.all_to_all(sent_rows, spread, 0, 0, tiled=True)
     (mine,) = call(
         functools.partial(inverse_kernel, nb, scale), [at, damping], pieces,

time: 167 us -> 170 us (1.018)
  starting transfers between devices: 85.5 us -> 66.8 us
  waiting for transfers between devices: 41.2 us -> 54.1 us
  blocking collectives: 0 us -> 10.6 us
    ppermute x24 -> x21, starting transfers between devices: 46.1 us -> 32.1 us  [shifted(): lax.ppermute(array, axis, [(spots[k], spots[(k + by) % size]) for k in ra...]
    all_to_all x0 -> x1, blocking collectives: none -> 10.6 us  [program(): cross_parts = lax.all_to_all(cross_sum, 'zh', 0, 0, tiled=True)]
    ppermute x7, waiting for transfers between devices: 0.61 us -> 10.2 us  [sent_across(): return lax.ppermute(array, PLANE, pairs)]
    all_to_all x1, starting transfers between devices: 13.8 us -> 9.15 us  [program(): cross_rows = lax.all_to_all(sent_rows, spread, 0, 0, tiled=True)]
    ppermute x24 -> x21, waiting for transfers between devices: 24.3 us -> 26.8 us  [shifted(): lax.ppermute(array, axis, [(spots[k], spots[(k + by) % size]) for k in ra...]
    unnamed x14 -> x10, local copies, waits for them, and re-layouts: 4.26 us -> 2.58 us
    pallas_call x20 -> x21, Pallas kernels: 33.9 us -> 33.9 us  [call(): pl.pallas_call(kernel, out_shape=shapes, in_specs=smem(len(scalars)) + vm...]
  transfers between devices with their start and end apart: 43 -> 40, of which waited for: 18 -> 21; matrix products, arithmetic and copies ran while one was open for 0% -> 0% of each run, Pallas kernels for 14% -> 14%
where the time goes in v6:
time: 170 us; the launch traced here: 169 us
  starting transfers between devices  66.8 us (39%)
  waiting for transfers between devices  54.1 us (32%)
  Pallas kernels  33.9 us (20%)
  blocking collectives  10.6 us (6%)
  local copies, waits for them, and re-layouts  2.58 us (2%)
    pallas_call x21, Pallas kernels, call(): pl.pallas_call(kernel, out_shape=shapes, in_specs=smem(len(scalars)) + vm...  33.9 us
    ppermute x21, starting transfers between devices, shifted(): lax.ppermute(array, axis, [(spots[k], spots[(k + by) % size]) for k in ra...  32.1 us
    ppermute x21, waiting for transfers between devices, shifted(): lax.ppermute(array, axis, [(spots[k], spots[(k + by) % size]) for k in ra...  26.8 us
    ppermute x10, waiting for transfers between devices, swapped(): return lax.ppermute(array, axes, pairs)  17 us
    all_to_all x1, blocking collectives, program(): cross_parts = lax.all_to_all(cross_sum, 'zh', 0, 0, tiled=True)  10.6 us
    ppermute x7, waiting for transfers between devices, sent_across(): return lax.ppermute(array, PLANE, pairs)  10.2 us
    ppermute x7, starting transfers between devices, sent_across(): return lax.ppermute(array, PLANE, pairs)  10.1 us
    all_to_all x1, starting transfers between devices, program(): cross_rows = lax.all_to_all(sent_rows, spread, 0, 0, tiled=True)  9.15 us
  transfers between devices with their start and end apart: 40, of which 21 were waited for; matrix products, arithmetic and copies ran while one was open for 0% of the time, Pallas kernels for 14%

profile of v6, /device:TPU:2, one launch (start us, length us, event | category | flops | bytes accessed | tf_op | source)
XLA Modules:
  0.0 168.9 jit_solution(8743880942442008449)
XLA Ops:
  0.7 1.2 copy-done
  1.9 1.2 copy-done.2
  3.1 1.7 shard_map.55
  4.8 1.1 shard_map.60.refs_0_.refs_4_
  5.9 1.1 shard_map.56.refs_0_.refs_3_
  7.1 1.2 shard_map.69
  8.5 1.1 shard_map.57
  10.3 4.0 %collective-permute-done.refs_1_ = f32[4,4,144,128]{3,2,1,0:T(8,128)S(1)} collective-permute-done((f32[4,4,144,128]{3,2,1,0:T(8,128)S(1)}, f32[4,4,144,128]{3,2,1,0:T(8,128)S(1)}, u32[]{:S(2)}, u32[]{:S(2)}) %collective-permute-start) | collective-permute-done | bytes 1179680 | tf_op jit(solution)/shard_map/ppermute | solution.py:296
  16.7 1.2 shard_map.68.kept_ref
  18.8 2.0 %collective-permute-start.33 = (f32[16,4,32,128]{3,2,1,0:T(8,128)S(1)}, f32[16,4,32,128]{3,2,1,0:T(8,128)S(1)}, u32[]{:S(2)}, u32[]{:S(2)}) collective-permute-start(f32[16,4,32,128]{3,2,1,0:T(8,128)S(1)} %get-tuple-element.52), channel_id=1, source_target_pairs={{0,32},{32,0},{1,33},{33,1},{2,34},{34,2},{3,35},{35,3},{4,36},{36... | collective-permute-start | bytes 3145736 | tf_op jit(solution)/shard_map/ppermute | solution.py:296
  20.9 2.1 %collective-permute-start.1 = (f32[4,144,128]{2,1,0:T(8,128)S(1)}, f32[4,144,128]{2,1,0:T(8,128)S(1)}, u32[]{:S(2)}, u32[]{:S(2)}) collective-permute-start(f32[4,144,128]{2,1,0:T(8,128)S(1)} %get-tuple-element.31), channel_id=1, source_target_pairs={{0,4},{2,6},{4,0},{6,2},{1,5},{3,7},{5,1},{7,3},{8,12},{10,14},{12... | collective-permute-start | bytes 884744 | tf_op jit(solution)/shard_map/ppermute | solution.py:302
  23.0 2.0 %collective-permute-start.3 = (f32[4,144,128]{2,1,0:T(8,128)S(1)}, f32[4,144,128]{2,1,0:T(8,128)S(1)}, u32[]{:S(2)}, u32[]{:S(2)}) collective-permute-start(f32[4,144,128]{2,1,0:T(8,128)S(1)} %get-tuple-element.33), channel_id=1, source_target_pairs={{0,6},{2,0},{4,2},{6,4},{1,7},{3,1},{5,3},{7,5},{8,14},{10,8},{12,... | collective-permute-start | bytes 884744 | tf_op jit(solution)/shard_map/ppermute | solution.py:302
  25.0 3.2 %collective-permute-start.8 = (f32[4,144,128]{2,1,0:T(8,128)S(1)}, f32[4,144,128]{2,1,0:T(8,128)S(1)}, u32[]{:S(2)}, u32[]{:S(2)}) collective-permute-start(f32[4,144,128]{2,1,0:T(8,128)S(1)} %get-tuple-element.40), channel_id=1, source_target_pairs={{0,1},{16,17},{1,0},{17,16},{2,3},{18,19},{3,2},{19,18},{4,5},{20,... | collective-permute-start | bytes 884744 | tf_op jit(solution)/shard_map/ppermute | solution.py:302
  28.2 4.1 %collective-permute-done.1.refs_1_ = f32[4,144,128]{2,1,0:T(8,128)S(1)} collective-permute-done((f32[4,144,128]{2,1,0:T(8,128)S(1)}, f32[4,144,128]{2,1,0:T(8,128)S(1)}, u32[]{:S(2)}, u32[]{:S(2)}) %collective-permute-start.1) | collective-permute-done | bytes 294944 | tf_op jit(solution)/shard_map/ppermute | solution.py:302
  32.3 1.6 collective-permute-start.9
  33.9 3.7 %collective-permute-done.2.refs_2_ = f32[4,144,128]{2,1,0:T(8,128)S(1)} collective-permute-done((f32[4,144,128]{2,1,0:T(8,128)S(1)}, f32[4,144,128]{2,1,0:T(8,128)S(1)}, u32[]{:S(2)}, u32[]{:S(2)}) %collective-permute-start.2) | collective-permute-done | bytes 294944 | tf_op jit(solution)/shard_map/ppermute | solution.py:302
  37.5 3.0 %collective-permute-start.10 = (f32[4,144,128]{2,1,0:T(8,128)S(1)}, f32[4,144,128]{2,1,0:T(8,128)S(1)}, u32[]{:S(2)}, u32[]{:S(2)}) collective-permute-start(f32[4,144,128]{2,1,0:T(8,128)S(1)} %get-tuple-element.42), channel_id=1, source_target_pairs={{0,17},{16,0},{1,16},{17,1},{2,19},{18,2},{3,18},{19,3},{4,21},{20... | collective-permute-start | bytes 884744 | tf_op jit(solution)/shard_map/ppermute | solution.py:302
  41.9 1.0 collective-permute-start.5
  42.8 2.3 %collective-permute-start.6 = (f32[144,128]{1,0:T(8,128)S(1)}, f32[144,128]{1,0:T(8,128)S(1)}, u32[]{:S(2)}, u32[]{:S(2)}) collective-permute-start(f32[144,128]{1,0:T(8,128)S(1)} %get-tuple-element.37), channel_id=1, source_target_pairs={{0,17},{16,0},{1,16},{17,1},{2,19},{18,2},{3,18},{19,3},{4,21},{20... | collective-permute-start | bytes 221192 | tf_op jit(solution)/shard_map/ppermute | solution.py:302
  45.1 3.3 %collective-permute-done.10.refs_3_ = f32[4,144,128]{2,1,0:T(8,128)S(1)} collective-permute-done((f32[4,144,128]{2,1,0:T(8,128)S(1)}, f32[4,144,128]{2,1,0:T(8,128)S(1)}, u32[]{:S(2)}, u32[]{:S(2)}) %collective-permute-start.10) | collective-permute-done | bytes 294944 | tf_op jit(solution)/shard_map/ppermute | solution.py:302
  49.3 2.9 %collective-permute-start.12 = (f32[144,128]{1,0:T(8,128)S(1)}, f32[144,128]{1,0:T(8,128)S(1)}, u32[]{:S(2)}, u32[]{:S(2)}) collective-permute-start(f32[144,128]{1,0:T(8,128)S(1)} %get-tuple-element.45), channel_id=1, source_target_pairs={{0,2},{2,4},{4,6},{6,0},{1,3},{3,5},{5,7},{7,1},{8,10},{10,12},{12... | collective-permute-start | bytes 221192 | tf_op jit(solution)/shard_map/ppermute | solution.py:302
  52.2 2.9 %collective-permute-done.11.refs_5_ = f32[144,128]{1,0:T(8,128)S(1)} collective-permute-done((f32[144,128]{1,0:T(8,128)S(1)}, f32[144,128]{1,0:T(8,128)S(1)}, u32[]{:S(2)}, u32[]{:S(2)}) %collective-permute-start.11) | collective-permute-done | bytes 73760 | tf_op jit(solution)/shard_map/ppermute | solution.py:302
  55.1 1.4 collective-permute-done.13.refs_7_
  57.1 1.2 shard_map.71
  58.3 8.7 %all-to-all-start = ((f32[16,4,32,128]{3,2,1,0:T(8,128)}), f32[16,4,32,128]{3,2,1,0:T(8,128)S(1)}, u32[]{:S(2)}, u32[]{:S(2)}) async-start(f32[16,4,32,128]{3,2,1,0:T(8,128)} %shard_map.71), calls=%async_computation | async-start | bytes 2097152 | tf_op jit(solution)/shard_map/all_to_all | solution.py:374
  67.2 4.8 %collective-permute-done.14.refs_1_ = f32[144,128]{1,0:T(8,128)S(1)} collective-permute-done((f32[144,128]{1,0:T(8,128)S(1)}, f32[144,128]{1,0:T(8,128)S(1)}, u32[]{:S(2)}, u32[]{:S(2)}) %collective-permute-start.14) | collective-permute-done | bytes 73760 | tf_op jit(solution)/shard_map/ppermute | solution.py:296
  72.0 5.3 %collective-permute-start.17 = (f32[144,128]{1,0:T(8,128)S(1)}, f32[144,128]{1,0:T(8,128)S(1)}, u32[]{:S(2)}, u32[]{:S(2)}) collective-permute-start(f32[144,128]{1,0:T(8,128)S(1)} %shard_map.64.refs_0_), channel_id=1, source_target_pairs={{0,192},{64,0},{128,64},{192,128},{1,193},{65,1},{129,65},{193,129... | collective-permute-start | bytes 221192 | tf_op jit(solution)/shard_map/ppermute | solution.py:302
  77.3 3.5 %collective-permute-start.15 = (f32[144,128]{1,0:T(8,128)S(1)}, f32[144,128]{1,0:T(8,128)S(1)}, u32[]{:S(2)}, u32[]{:S(2)}) collective-permute-start(f32[144,128]{1,0:T(8,128)S(1)} %shard_map.64.refs_0_), channel_id=1, source_target_pairs={{0,128},{64,192},{128,0},{192,64},{1,129},{65,193},{129,1},{193,65... | collective-permute-start | bytes 221192 | tf_op jit(solution)/shard_map/ppermute | solution.py:302
  80.9 3.8 %collective-permute-done.16.refs_2_ = f32[144,128]{1,0:T(8,128)S(1)} collective-permute-done((f32[144,128]{1,0:T(8,128)S(1)}, f32[144,128]{1,0:T(8,128)S(1)}, u32[]{:S(2)}, u32[]{:S(2)}) %collective-permute-start.16) | collective-permute-done | bytes 73760 | tf_op jit(solution)/shard_map/ppermute | solution.py:302
  84.6 1.9 %collective-permute-done.15.refs_1_ = f32[144,128]{1,0:T(8,128)S(1)} collective-permute-done((f32[144,128]{1,0:T(8,128)S(1)}, f32[144,128]{1,0:T(8,128)S(1)}, u32[]{:S(2)}, u32[]{:S(2)}) %collective-permute-start.15) | collective-permute-done | bytes 73760 | tf_op jit(solution)/shard_map/ppermute | solution.py:302
  86.6 3.9 %collective-permute-start.24 = (f32[144,128]{1,0:T(8,128)S(1)}, f32[144,128]{1,0:T(8,128)S(1)}, u32[]{:S(2)}, u32[]{:S(2)}) collective-permute-start(f32[144,128]{1,0:T(8,128)S(1)} %shard_map.65.refs_0_), channel_id=1, source_target_pairs={{0,49},{16,32},{1,48},{17,33},{2,51},{18,34},{3,50},{19,35},{4,53}... | collective-permute-start | bytes 221192 | tf_op jit(solution)/shard_map/ppermute | solution.py:315
  90.8 1.2 collective-permute-start.22
  92.0 2.2 %collective-permute-start.21 = (f32[144,128]{1,0:T(8,128)S(1)}, f32[144,128]{1,0:T(8,128)S(1)}, u32[]{:S(2)}, u32[]{:S(2)}) collective-permute-start(f32[144,128]{1,0:T(8,128)S(1)} %shard_map.65.refs_0_), channel_id=1, source_target_pairs={{0,32},{16,48},{1,33},{17,49},{2,34},{18,50},{3,35},{19,51},{4,36}... | collective-permute-start | bytes 221192 | tf_op jit(solution)/shard_map/ppermute | solution.py:315
  94.3 2.2 %collective-permute-start.20 = (f32[144,128]{1,0:T(8,128)S(1)}, f32[144,128]{1,0:T(8,128)S(1)}, u32[]{:S(2)}, u32[]{:S(2)}) collective-permute-start(f32[144,128]{1,0:T(8,128)S(1)} %shard_map.65.refs_0_), channel_id=1, source_target_pairs={{0,17},{16,0},{1,16},{17,1},{2,19},{18,2},{3,18},{19,3},{4,21},{20... | collective-permute-start | bytes 221192 | tf_op jit(solution)/shard_map/ppermute | solution.py:315
  97.6 1.6 collective-permute-done.20.refs_3_
  99.3 3.7 %collective-permute-done.19.refs_2_ = f32[144,128]{1,0:T(8,128)S(1)} collective-permute-done((f32[144,128]{1,0:T(8,128)S(1)}, f32[144,128]{1,0:T(8,128)S(1)}, u32[]{:S(2)}, u32[]{:S(2)}) %collective-permute-start.19) | collective-permute-done | bytes 73760 | tf_op jit(solution)/shard_map/ppermute | solution.py:315
  102.9 4.0 %collective-permute-done.18.refs_1_ = f32[144,128]{1,0:T(8,128)S(1)} collective-permute-done((f32[144,128]{1,0:T(8,128)S(1)}, f32[144,128]{1,0:T(8,128)S(1)}, u32[]{:S(2)}, u32[]{:S(2)}) %collective-permute-start.18) | collective-permute-done | bytes 73760 | tf_op jit(solution)/shard_map/ppermute | solution.py:315
  107.6 1.6 collective-permute-start.26
  110.7 1.1 collective-permute-start.29
  111.8 5.7 %collective-permute-done.27.refs_3_ = f32[4,144,128]{2,1,0:T(8,128)S(1)} collective-permute-done((f32[4,144,128]{2,1,0:T(8,128)S(1)}, f32[4,144,128]{2,1,0:T(8,128)S(1)}, u32[]{:S(2)}, u32[]{:S(2)}) %collective-permute-start.27) | collective-permute-done | bytes 294944 | tf_op jit(solution)/shard_map/ppermute | solution.py:302
  117.6 10.6 %all_to_all.15.pieces_ref = f32[4,32,128]{2,1,0:T(8,128)S(1)} all-to-all(f32[4,32,128]{2,1,0:T(8,128)S(1)} %shard_map.72), channel_id=1, replica_groups=mesh['zh'=4,'zl'=2,'yl'=2,'c'=2,'x'=4,'yh'=2] {'zh'}, dimensions={0} | all-to-all | bytes 131072 | tf_op jit(solution)/shard_map/all_to_all | solution.py:385
  129.0 9.2 %all-to-all-start.2 = ((f32[32,32,128]{2,1,0:T(8,128)}), f32[32,32,128]{2,1,0:T(8,128)S(1)}, u32[]{:S(2)}, u32[]{:S(2)}) async-start(f32[32,32,128]{2,1,0:T(8,128)} %shard_map.73), calls=%async_computation.2 | async-start | bytes 1048576 | tf_op jit(solution)/shard_map/all_to_all | solution.py:399
  138.2 17.3 %shard_map.67.mine_ref = f32[128,1024]{1,0:T(8,128)S(1)} custom-call(s32[6]{0:T(128)S(1)} %shift-right-arithmetic_and_fusion.at_ref.refs_0_, f32[2]{0:T(128)S(1)} %copy-done.4, f32[4,144,128]{2,1,0:T(8,128)S(1)} %get-tuple-element.49.refs_0_, f32[4,144,128]{2,1,0:T(8,128)S(1)} %collective-permute-done.25.refs_1_, ...), custom_call_target="tpu_custom_call" | custom-call | flops 11274289152 | bytes 2883584 | tf_op jit(solution)/shard_map/pallas_call | solution.py:282
  155.7 1.9 %collective-permute-done.31.other_ref = f32[128,1024]{1,0:T(8,128)S(1)} collective-permute-done((f32[128,1024]{1,0:T(8,128)S(1)}, f32[128,1024]{1,0:T(8,128)S(1)}, u32[]{:S(2)}, u32[]{:S(2)}) %collective-permute-start.31) | collective-permute-done | bytes 524320 | tf_op jit(solution)/shard_map/ppermute | solution.py:296
  158.6 3.0 %collective-permute-start.35 = (f32[4,32,128]{2,1,0:T(8,128)S(1)}, f32[4,32,128]{2,1,0:T(8,128)S(1)}, u32[]{:S(2)}, u32[]{:S(2)}) collective-permute-start(f32[4,32,128]{2,1,0:T(8,128)S(1)} %shard_map.74.refs_0_), channel_id=1, source_target_pairs={{0,32},{32,0},{1,33},{33,1},{2,34},{34,2},{3,35},{35,3},{4,36},{36... | collective-permute-start | bytes 196616 | tf_op jit(solution)/shard_map/ppermute | solution.py:296
  162.1 2.3 %collective-permute-done.36.refs_3_ = f32[4,32,128]{2,1,0:T(8,128)S(1)} collective-permute-done((f32[4,32,128]{2,1,0:T(8,128)S(1)}, f32[4,32,128]{2,1,0:T(8,128)S(1)}, u32[]{:S(2)}, u32[]{:S(2)}) %collective-permute-start.36) | collective-permute-done | bytes 65568 | tf_op jit(solution)/shard_map/ppermute | solution.py:296
  166.0 1.5 collective-permute-done.37.refs_4_
  167.5 1.4 shard_map.75
  (66 shorter events, 15.7 us)
Async XLA Ops:
  0.7 1.2 copy-start
  1.9 1.2 copy-start.2
  5.9 1.2 copy-start.1
  7.1 1.4 copy-start.3
  8.4 9.6 %collective-permute-start.32 = (f32[2,16,4,32,128]{4,3,2,1,0:T(8,128)S(1)}, f32[2,16,4,32,128]{4,3,2,1,0:T(8,128)S(1)}, u32[]{:S(2)}, u32[]{:S(2)}) collective-permute-start(f32[2,16,4,32,128]{4,3,2,1,0:T(8,128)S(1)} %shard_map.69), channel_id=1, source_target_pairs={{0,8},{8,0},{1,9},{9,1},{2,10},{10,2},{3,11},{11,3},{4,12},{12,4},... | collective-permute-start | bytes 6291464 | tf_op jit(solution)/shard_map/ppermute | solution.py:296
  9.6 4.7 %collective-permute-start = (f32[4,4,144,128]{3,2,1,0:T(8,128)S(1)}, f32[4,4,144,128]{3,2,1,0:T(8,128)S(1)}, u32[]{:S(2)}, u32[]{:S(2)}) collective-permute-start(f32[4,4,144,128]{3,2,1,0:T(8,128)S(1)} %shard_map.57), channel_id=1, source_target_pairs={{0,8},{8,0},{1,9},{9,1},{2,10},{10,2},{3,11},{11,3},{4,12},{12,4},... | collective-permute-start | bytes 3538952 | tf_op jit(solution)/shard_map/ppermute | solution.py:296
  10.2 5.8 %collective-permute-start.7 = (f32[4,4,144,128]{3,2,1,0:T(8,128)S(1)}, f32[4,4,144,128]{3,2,1,0:T(8,128)S(1)}, u32[]{:S(2)}, u32[]{:S(2)}) collective-permute-start(f32[4,4,144,128]{3,2,1,0:T(8,128)S(1)} %get-tuple-element.38), channel_id=1, source_target_pairs={{0,8},{8,0},{1,9},{9,1},{2,10},{10,2},{3,11},{11,3},{4,12},{12,4},... | collective-permute-start | bytes 3538952 | tf_op jit(solution)/shard_map/ppermute | solution.py:296
  18.8 38.2 %collective-permute-start.33 = (f32[16,4,32,128]{3,2,1,0:T(8,128)S(1)}, f32[16,4,32,128]{3,2,1,0:T(8,128)S(1)}, u32[]{:S(2)}, u32[]{:S(2)}) collective-permute-start(f32[16,4,32,128]{3,2,1,0:T(8,128)S(1)} %get-tuple-element.52), channel_id=1, source_target_pairs={{0,32},{32,0},{1,33},{33,1},{2,34},{34,2},{3,35},{35,3},{4,36},{36... | collective-permute-start | bytes 3145736 | tf_op jit(solution)/shard_map/ppermute | solution.py:296
  20.9 11.4 %collective-permute-start.1 = (f32[4,144,128]{2,1,0:T(8,128)S(1)}, f32[4,144,128]{2,1,0:T(8,128)S(1)}, u32[]{:S(2)}, u32[]{:S(2)}) collective-permute-start(f32[4,144,128]{2,1,0:T(8,128)S(1)} %get-tuple-element.31), channel_id=1, source_target_pairs={{0,4},{2,6},{4,0},{6,2},{1,5},{3,7},{5,1},{7,3},{8,12},{10,14},{12... | collective-permute-start | bytes 884744 | tf_op jit(solution)/shard_map/ppermute | solution.py:302
  23.0 14.5 %collective-permute-start.2 = (f32[4,144,128]{2,1,0:T(8,128)S(1)}, f32[4,144,128]{2,1,0:T(8,128)S(1)}, u32[]{:S(2)}, u32[]{:S(2)}) collective-permute-start(f32[4,144,128]{2,1,0:T(8,128)S(1)} %get-tuple-element.32), channel_id=1, source_target_pairs={{0,2},{2,4},{4,6},{6,0},{1,3},{3,5},{5,7},{7,1},{8,10},{10,12},{12... | collective-permute-start | bytes 884744 | tf_op jit(solution)/shard_map/ppermute | solution.py:302
  23.0 17.6 %collective-permute-start.3 = (f32[4,144,128]{2,1,0:T(8,128)S(1)}, f32[4,144,128]{2,1,0:T(8,128)S(1)}, u32[]{:S(2)}, u32[]{:S(2)}) collective-permute-start(f32[4,144,128]{2,1,0:T(8,128)S(1)} %get-tuple-element.33), channel_id=1, source_target_pairs={{0,6},{2,0},{4,2},{6,4},{1,7},{3,1},{5,3},{7,5},{8,14},{10,8},{12,... | collective-permute-start | bytes 884744 | tf_op jit(solution)/shard_map/ppermute | solution.py:302
  25.0 16.9 %collective-permute-start.8 = (f32[4,144,128]{2,1,0:T(8,128)S(1)}, f32[4,144,128]{2,1,0:T(8,128)S(1)}, u32[]{:S(2)}, u32[]{:S(2)}) collective-permute-start(f32[4,144,128]{2,1,0:T(8,128)S(1)} %get-tuple-element.40), channel_id=1, source_target_pairs={{0,1},{16,17},{1,0},{17,16},{2,3},{18,19},{3,2},{19,18},{4,5},{20,... | collective-permute-start | bytes 884744 | tf_op jit(solution)/shard_map/ppermute | solution.py:302
  32.3 10.6 %collective-permute-start.9 = (f32[4,144,128]{2,1,0:T(8,128)S(1)}, f32[4,144,128]{2,1,0:T(8,128)S(1)}, u32[]{:S(2)}, u32[]{:S(2)}) collective-permute-start(f32[4,144,128]{2,1,0:T(8,128)S(1)} %get-tuple-element.41), channel_id=1, source_target_pairs={{0,16},{16,1},{1,17},{17,0},{2,18},{18,3},{3,19},{19,2},{4,20},{20... | collective-permute-start | bytes 884744 | tf_op jit(solution)/shard_map/ppermute | solution.py:302
  37.5 10.9 %collective-permute-start.10 = (f32[4,144,128]{2,1,0:T(8,128)S(1)}, f32[4,144,128]{2,1,0:T(8,128)S(1)}, u32[]{:S(2)}, u32[]{:S(2)}) collective-permute-start(f32[4,144,128]{2,1,0:T(8,128)S(1)} %get-tuple-element.42), channel_id=1, source_target_pairs={{0,17},{16,0},{1,16},{17,1},{2,19},{18,2},{3,18},{19,3},{4,21},{20... | collective-permute-start | bytes 884744 | tf_op jit(solution)/shard_map/ppermute | solution.py:302
  41.1 8.1 %collective-permute-start.4 = (f32[144,128]{1,0:T(8,128)S(1)}, f32[144,128]{1,0:T(8,128)S(1)}, u32[]{:S(2)}, u32[]{:S(2)}) collective-permute-start(f32[144,128]{1,0:T(8,128)S(1)} %get-tuple-element.35), channel_id=1, source_target_pairs={{0,1},{16,17},{1,0},{17,16},{2,3},{18,19},{3,2},{19,18},{4,5},{20,... | collective-permute-start | bytes 221192 | tf_op jit(solution)/shard_map/ppermute | solution.py:302
  41.9 10.3 %collective-permute-start.5 = (f32[144,128]{1,0:T(8,128)S(1)}, f32[144,128]{1,0:T(8,128)S(1)}, u32[]{:S(2)}, u32[]{:S(2)}) collective-permute-start(f32[144,128]{1,0:T(8,128)S(1)} %get-tuple-element.36), channel_id=1, source_target_pairs={{0,16},{16,1},{1,17},{17,0},{2,18},{18,3},{3,19},{19,2},{4,20},{20... | collective-permute-start | bytes 221192 | tf_op jit(solution)/shard_map/ppermute | solution.py:302
  42.8 9.3 %collective-permute-start.6 = (f32[144,128]{1,0:T(8,128)S(1)}, f32[144,128]{1,0:T(8,128)S(1)}, u32[]{:S(2)}, u32[]{:S(2)}) collective-permute-start(f32[144,128]{1,0:T(8,128)S(1)} %get-tuple-element.37), channel_id=1, source_target_pairs={{0,17},{16,0},{1,16},{17,1},{2,19},{18,2},{3,18},{19,3},{4,21},{20... | collective-permute-start | bytes 221192 | tf_op jit(solution)/shard_map/ppermute | solution.py:302
  49.0 6.1 %collective-permute-start.11 = (f32[144,128]{1,0:T(8,128)S(1)}, f32[144,128]{1,0:T(8,128)S(1)}, u32[]{:S(2)}, u32[]{:S(2)}) collective-permute-start(f32[144,128]{1,0:T(8,128)S(1)} %get-tuple-element.44), channel_id=1, source_target_pairs={{0,4},{2,6},{4,0},{6,2},{1,5},{3,7},{5,1},{7,3},{8,12},{10,14},{12... | collective-permute-start | bytes 221192 | tf_op jit(solution)/shard_map/ppermute | solution.py:302
  49.3 5.8 %collective-permute-start.12 = (f32[144,128]{1,0:T(8,128)S(1)}, f32[144,128]{1,0:T(8,128)S(1)}, u32[]{:S(2)}, u32[]{:S(2)}) collective-permute-start(f32[144,128]{1,0:T(8,128)S(1)} %get-tuple-element.45), channel_id=1, source_target_pairs={{0,2},{2,4},{4,6},{6,0},{1,3},{3,5},{5,7},{7,1},{8,10},{10,12},{12... | collective-permute-start | bytes 221192 | tf_op jit(solution)/shard_map/ppermute | solution.py:302
  52.2 4.4 %collective-permute-start.13 = (f32[144,128]{1,0:T(8,128)S(1)}, f32[144,128]{1,0:T(8,128)S(1)}, u32[]{:S(2)}, u32[]{:S(2)}) collective-permute-start(f32[144,128]{1,0:T(8,128)S(1)} %get-tuple-element.46), channel_id=1, source_target_pairs={{0,6},{2,0},{4,2},{6,4},{1,7},{3,1},{5,3},{7,5},{8,14},{10,8},{12,... | collective-permute-start | bytes 221192 | tf_op jit(solution)/shard_map/ppermute | solution.py:302
  58.3 59.2 %all-to-all-start = ((f32[16,4,32,128]{3,2,1,0:T(8,128)}), f32[16,4,32,128]{3,2,1,0:T(8,128)S(1)}, u32[]{:S(2)}, u32[]{:S(2)}) async-start(f32[16,4,32,128]{3,2,1,0:T(8,128)} %shard_map.71), calls=%async_computation | async-start | bytes 2097152 | tf_op jit(solution)/shard_map/all_to_all | solution.py:374
  66.9 5.1 %collective-permute-start.14 = (f32[144,128]{1,0:T(8,128)S(1)}, f32[144,128]{1,0:T(8,128)S(1)}, u32[]{:S(2)}, u32[]{:S(2)}) collective-permute-start(f32[144,128]{1,0:T(8,128)S(1)} %get-tuple-element.48.refs_2_), channel_id=1, source_target_pairs={{0,32},{32,0},{1,33},{33,1},{2,34},{34,2},{3,35},{35,3},{4,36},{36... | collective-permute-start | bytes 221192 | tf_op jit(solution)/shard_map/ppermute | solution.py:296
  72.0 8.8 %collective-permute-start.17 = (f32[144,128]{1,0:T(8,128)S(1)}, f32[144,128]{1,0:T(8,128)S(1)}, u32[]{:S(2)}, u32[]{:S(2)}) collective-permute-start(f32[144,128]{1,0:T(8,128)S(1)} %shard_map.64.refs_0_), channel_id=1, source_target_pairs={{0,192},{64,0},{128,64},{192,128},{1,193},{65,1},{129,65},{193,129... | collective-permute-start | bytes 221192 | tf_op jit(solution)/shard_map/ppermute | solution.py:302
  77.3 7.3 %collective-permute-start.16 = (f32[144,128]{1,0:T(8,128)S(1)}, f32[144,128]{1,0:T(8,128)S(1)}, u32[]{:S(2)}, u32[]{:S(2)}) collective-permute-start(f32[144,128]{1,0:T(8,128)S(1)} %shard_map.64.refs_0_), channel_id=1, source_target_pairs={{0,64},{64,128},{128,192},{192,0},{1,65},{65,129},{129,193},{193,1... | collective-permute-start | bytes 221192 | tf_op jit(solution)/shard_map/ppermute | solution.py:302
  77.3 9.2 %collective-permute-start.15 = (f32[144,128]{1,0:T(8,128)S(1)}, f32[144,128]{1,0:T(8,128)S(1)}, u32[]{:S(2)}, u32[]{:S(2)}) collective-permute-start(f32[144,128]{1,0:T(8,128)S(1)} %shard_map.64.refs_0_), channel_id=1, source_target_pairs={{0,128},{64,192},{128,0},{192,64},{1,129},{65,193},{129,1},{193,65... | collective-permute-start | bytes 221192 | tf_op jit(solution)/shard_map/ppermute | solution.py:302
  86.6 9.8 %collective-permute-start.24 = (f32[144,128]{1,0:T(8,128)S(1)}, f32[144,128]{1,0:T(8,128)S(1)}, u32[]{:S(2)}, u32[]{:S(2)}) collective-permute-start(f32[144,128]{1,0:T(8,128)S(1)} %shard_map.65.refs_0_), channel_id=1, source_target_pairs={{0,49},{16,32},{1,48},{17,33},{2,51},{18,34},{3,50},{19,35},{4,53}... | collective-permute-start | bytes 221192 | tf_op jit(solution)/shard_map/ppermute | solution.py:315
  90.5 6.9 %collective-permute-start.23 = (f32[144,128]{1,0:T(8,128)S(1)}, f32[144,128]{1,0:T(8,128)S(1)}, u32[]{:S(2)}, u32[]{:S(2)}) collective-permute-start(f32[144,128]{1,0:T(8,128)S(1)} %shard_map.65.refs_0_), channel_id=1, source_target_pairs={{0,33},{16,49},{1,32},{17,48},{2,35},{18,51},{3,34},{19,50},{4,37}... | collective-permute-start | bytes 221192 | tf_op jit(solution)/shard_map/ppermute | solution.py:315
  90.8 6.6 %collective-permute-start.22 = (f32[144,128]{1,0:T(8,128)S(1)}, f32[144,128]{1,0:T(8,128)S(1)}, u32[]{:S(2)}, u32[]{:S(2)}) collective-permute-start(f32[144,128]{1,0:T(8,128)S(1)} %shard_map.65.refs_0_), channel_id=1, source_target_pairs={{0,48},{16,33},{1,49},{17,32},{2,50},{18,35},{3,51},{19,34},{4,52}... | collective-permute-start | bytes 221192 | tf_op jit(solution)/shard_map/ppermute | solution.py:315
  92.0 5.6 %collective-permute-start.21 = (f32[144,128]{1,0:T(8,128)S(1)}, f32[144,128]{1,0:T(8,128)S(1)}, u32[]{:S(2)}, u32[]{:S(2)}) collective-permute-start(f32[144,128]{1,0:T(8,128)S(1)} %shard_map.65.refs_0_), channel_id=1, source_target_pairs={{0,32},{16,48},{1,33},{17,49},{2,34},{18,50},{3,35},{19,51},{4,36}... | collective-permute-start | bytes 221192 | tf_op jit(solution)/shard_map/ppermute | solution.py:315
  94.3 5.0 %collective-permute-start.20 = (f32[144,128]{1,0:T(8,128)S(1)}, f32[144,128]{1,0:T(8,128)S(1)}, u32[]{:S(2)}, u32[]{:S(2)}) collective-permute-start(f32[144,128]{1,0:T(8,128)S(1)} %shard_map.65.refs_0_), channel_id=1, source_target_pairs={{0,17},{16,0},{1,16},{17,1},{2,19},{18,2},{3,18},{19,3},{4,21},{20... | collective-permute-start | bytes 221192 | tf_op jit(solution)/shard_map/ppermute | solution.py:315
  96.4 6.5 %collective-permute-start.19 = (f32[144,128]{1,0:T(8,128)S(1)}, f32[144,128]{1,0:T(8,128)S(1)}, u32[]{:S(2)}, u32[]{:S(2)}) collective-permute-start(f32[144,128]{1,0:T(8,128)S(1)} %shard_map.65.refs_0_), channel_id=1, source_target_pairs={{0,1},{16,17},{1,0},{17,16},{2,3},{18,19},{3,2},{19,18},{4,5},{20,... | collective-permute-start | bytes 221192 | tf_op jit(solution)/shard_map/ppermute | solution.py:315
  97.4 9.5 %collective-permute-start.18 = (f32[144,128]{1,0:T(8,128)S(1)}, f32[144,128]{1,0:T(8,128)S(1)}, u32[]{:S(2)}, u32[]{:S(2)}) collective-permute-start(f32[144,128]{1,0:T(8,128)S(1)} %shard_map.65.refs_0_), channel_id=1, source_target_pairs={{0,16},{16,1},{1,17},{17,0},{2,18},{18,3},{3,19},{19,2},{4,20},{20... | collective-permute-start | bytes 221192 | tf_op jit(solution)/shard_map/ppermute | solution.py:315
  107.5 10.0 %collective-permute-start.27 = (f32[4,144,128]{2,1,0:T(8,128)S(1)}, f32[4,144,128]{2,1,0:T(8,128)S(1)}, u32[]{:S(2)}, u32[]{:S(2)}) collective-permute-start(f32[4,144,128]{2,1,0:T(8,128)S(1)} %get-tuple-element.49.refs_0_), channel_id=1, source_target_pairs={{0,6},{2,0},{4,2},{6,4},{1,7},{3,1},{5,3},{7,5},{8,14},{10,8},{12,... | collective-permute-start | bytes 884744 | tf_op jit(solution)/shard_map/ppermute | solution.py:302
  107.6 30.5 %collective-permute-start.26 = (f32[4,144,128]{2,1,0:T(8,128)S(1)}, f32[4,144,128]{2,1,0:T(8,128)S(1)}, u32[]{:S(2)}, u32[]{:S(2)}) collective-permute-start(f32[4,144,128]{2,1,0:T(8,128)S(1)} %get-tuple-element.49.refs_0_), channel_id=1, source_target_pairs={{0,4},{2,6},{4,0},{6,2},{1,5},{3,7},{5,1},{7,3},{8,12},{10,14},{12... | collective-permute-start | bytes 884744 | tf_op jit(solution)/shard_map/ppermute | solution.py:302
  109.2 29.0 %collective-permute-start.25 = (f32[4,144,128]{2,1,0:T(8,128)S(1)}, f32[4,144,128]{2,1,0:T(8,128)S(1)}, u32[]{:S(2)}, u32[]{:S(2)}) collective-permute-start(f32[4,144,128]{2,1,0:T(8,128)S(1)} %get-tuple-element.49.refs_0_), channel_id=1, source_target_pairs={{0,2},{2,4},{4,6},{6,0},{1,3},{3,5},{5,7},{7,1},{8,10},{10,12},{12... | collective-permute-start | bytes 884744 | tf_op jit(solution)/shard_map/ppermute | solution.py:302
  110.1 28.1 %copy-start.4 = (f32[2]{0:T(128)S(1)}, f32[2]{0:T(128)}, u32[]{:S(2)}) copy-start(f32[2]{0:T(128)} %damp_ref.1) | copy-start | bytes 28
  110.1 28.1 %collective-permute-start.30 = (f32[4,144,128]{2,1,0:T(8,128)S(1)}, f32[4,144,128]{2,1,0:T(8,128)S(1)}, u32[]{:S(2)}, u32[]{:S(2)}) collective-permute-start(f32[4,144,128]{2,1,0:T(8,128)S(1)} %get-tuple-element.50.refs_4_), channel_id=1, source_target_pairs={{0,17},{16,0},{1,16},{17,1},{2,19},{18,2},{3,18},{19,3},{4,21},{20... | collective-permute-start | bytes 884744 | tf_op jit(solution)/shard_map/ppermute | solution.py:302
  110.7 27.5 %collective-permute-start.29 = (f32[4,144,128]{2,1,0:T(8,128)S(1)}, f32[4,144,128]{2,1,0:T(8,128)}, u32[]{:S(2)}, u32[]{:S(2)}) collective-permute-start(f32[4,144,128]{2,1,0:T(8,128)S(1)} %get-tuple-element.50.refs_4_), channel_id=1, source_target_pairs={{0,1},{16,17},{1,0},{17,16},{2,3},{18,19},{3,2},{19,18},{4,5},{20,... | collective-permute-start | bytes 884744 | tf_op jit(solution)/shard_map/ppermute | solution.py:302
  117.5 20.7 %collective-permute-start.28 = (f32[4,144,128]{2,1,0:T(8,128)S(1)}, f32[4,144,128]{2,1,0:T(8,128)}, u32[]{:S(2)}, u32[]{:S(2)}) collective-permute-start(f32[4,144,128]{2,1,0:T(8,128)S(1)} %get-tuple-element.50.refs_4_), channel_id=1, source_target_pairs={{0,16},{16,1},{1,17},{17,0},{2,18},{18,3},{3,19},{19,2},{4,20},{20... | collective-permute-start | bytes 884744 | tf_op jit(solution)/shard_map/ppermute | solution.py:302
  129.0 28.6 %all-to-all-start.2 = ((f32[32,32,128]{2,1,0:T(8,128)}), f32[32,32,128]{2,1,0:T(8,128)S(1)}, u32[]{:S(2)}, u32[]{:S(2)}) async-start(f32[32,32,128]{2,1,0:T(8,128)} %shard_map.73), calls=%async_computation.2 | async-start | bytes 1048576 | tf_op jit(solution)/shard_map/all_to_all | solution.py:399
  155.6 2.0 %collective-permute-start.31 = (f32[128,1024]{1,0:T(8,128)S(1)}, f32[128,1024]{1,0:T(8,128)S(1)}, u32[]{:S(2)}, u32[]{:S(2)}) collective-permute-start(f32[128,1024]{1,0:T(8,128)S(1)} %shard_map.67.mine_ref), channel_id=1, source_target_pairs={{0,8},{8,0},{1,9},{9,1},{2,10},{10,2},{3,11},{11,3},{4,12},{12,4},... | collective-permute-start | bytes 1572872 | tf_op jit(solution)/shard_map/ppermute | solution.py:296
  158.5 5.9 %collective-permute-start.36 = (f32[4,32,128]{2,1,0:T(8,128)S(1)}, f32[4,32,128]{2,1,0:T(8,128)S(1)}, u32[]{:S(2)}, u32[]{:S(2)}) collective-permute-start(f32[4,32,128]{2,1,0:T(8,128)S(1)} %shard_map.74.refs_0_), channel_id=1, source_target_pairs={{0,48},{16,32},{32,16},{48,0},{1,49},{17,33},{33,17},{49,1},{2,50}... | collective-permute-start | bytes 196616 | tf_op jit(solution)/shard_map/ppermute | solution.py:296
  158.6 6.5 %collective-permute-start.35 = (f32[4,32,128]{2,1,0:T(8,128)S(1)}, f32[4,32,128]{2,1,0:T(8,128)S(1)}, u32[]{:S(2)}, u32[]{:S(2)}) collective-permute-start(f32[4,32,128]{2,1,0:T(8,128)S(1)} %shard_map.74.refs_0_), channel_id=1, source_target_pairs={{0,32},{32,0},{1,33},{33,1},{2,34},{34,2},{3,35},{35,3},{4,36},{36... | collective-permute-start | bytes 196616 | tf_op jit(solution)/shard_map/ppermute | solution.py:296
  161.6 4.3 %collective-permute-start.34 = (f32[4,32,128]{2,1,0:T(8,128)S(1)}, f32[4,32,128]{2,1,0:T(8,128)S(1)}, u32[]{:S(2)}, u32[]{:S(2)}) collective-permute-start(f32[4,32,128]{2,1,0:T(8,128)S(1)} %shard_map.74.refs_0_), channel_id=1, source_target_pairs={{0,16},{16,0},{1,17},{17,1},{2,18},{18,2},{3,19},{19,3},{4,20},{20... | collective-permute-start | bytes 196616 | tf_op jit(solution)/shard_map/ppermute | solution.py:296
  165.9 1.6 collective-permute-start.37
